TPU v7x, 128 devices: a whole 4x4x4 slice. The times are simulated.
128 devices in a mesh: strike: 32 (over y, x, z_lo), depth: 4 (over z_hi, core).
Axes of the slice: x: 4, y: 4, z: 4 (z_hi: 2, z_lo: 2; z = z_hi * 2 + z_lo), core: 2. Of those that a mesh axis runs over, the one named last changes fastest.
Arguments:
- fault_slip: float32 [16384, 2048], P('strike', 'depth'), may hold values from -6 to 6
- rate_prev: float32 [16384, 2048], P('strike', 'depth'), may hold values from -1 to 3
- log_state: float32 [16384, 2048], P('strike', 'depth'), may hold values from -2 to 2
- weakening: float32 [16384, 2048], P('strike', 'depth'), may hold values from 0.5 to 2
- strength: float32 [16384, 2048], P('strike', 'depth'), may hold values from 0.25 to 2.5
- pre_stress: float32 [16384, 2048], P('strike', 'depth'), may hold values from 1 to 3
- kernel: float32 [9, 1024, 16384], P(None, ('strike', 'depth')), may hold values from -2 to 2
- history: float32 [8, 2, 1024, 16384], P(None, None, ('strike', 'depth')), may hold values from -6 to 6
Outputs:
- velocity: float32 [16384, 2048], P('strike', 'depth')
- new_slip: float32 [16384, 2048], P('strike', 'depth')
- slip_modes: float32 [2, 1024, 16384], P(None, ('strike', 'depth'))
All inputs are finite; a program needn't handle non-finite values.
Results may differ from a plain program's by a relative error of at most 0.0003.
Values sent between devices are 32-bit elements; how exact they have to be, the bound alone decides.
No kernel may reach another device: no remote copies, remote signals or barrier semaphores. Data moves between devices by JAX's collectives and lax.ppermute only.
A program may use at most 128 MiB of HBM per device.

v0:
```python
import functools
import math

import jax
import jax.numpy as jnp
import ml_dtypes
import numpy as np
from jax import lax
from jax.experimental import pallas as pl
from jax.experimental.pallas import tpu as pltpu
from jax.sharding import PartitionSpec as P

NEWTON_ITERS = 4
DAMPING = 0.5
RELAXATION = 0.5
ADVANCE = 0.5
LAGS = 8
ALL = ("strike", "depth")
F32 = jnp.float32
BF16 = jnp.bfloat16
NN = (((1,), (0,)), ((), ()))
NT = (((1,), (1,)), ((), ()))
TN = (((0,), (0,)), ((), ()))
VMEM = pl.BlockSpec(memory_space=pltpu.VMEM)


def split_np(table):
    high = table.astype(ml_dtypes.bfloat16)
    low = (table - high.astype(np.float64)).astype(ml_dtypes.bfloat16)
    return high, low


def split(value):
    high = value.astype(BF16)
    return high, (value - high.astype(F32)).astype(BF16)


def dot3(left, right, dims):
    mul = functools.partial(lax.dot_general, dimension_numbers=dims, preferred_element_type=F32)
    return mul(left[0], right[0]) + (mul(left[0], right[1]) + mul(left[1], right[0]))


def depth_seeds(depth_len, blocks):
    cells = depth_len // 4
    cell = np.arange(cells)
    turn = 2.0 * np.pi / depth_len
    coarse = turn * ((8 * np.arange(blocks)[:, None] * cell[None]) % depth_len)
    fine = turn * ((np.arange(8)[:, None] * cell[None]) % depth_len)
    pack = lambda angle: np.stack([np.cos(angle), np.sin(angle)]).astype(np.float32)
    return pack(coarse), pack(fine)


def table_kernel(coarse_ref, fine_ref, high_ref, low_ref):
    blocks = coarse_ref.shape[1]
    cos_a, sin_a = coarse_ref[0], coarse_ref[1]
    for cls in range(4):
        for half in range(2):
            row = 4 * half + cls
            cos_b, sin_b = fine_ref[0, row : row + 1, :], fine_ref[1, row : row + 1, :]
            for part, value in enumerate(
                (cos_a * cos_b - sin_a * sin_b, sin_a * cos_b + cos_a * sin_b)
            ):
                high, low = split(value)
                rows = pl.ds((part * 2 + half) * blocks, blocks)
                high_ref[cls, rows, :] = high
                low_ref[cls, rows, :] = low


def depth_tables(depth_len, blocks):
    coarse, fine = depth_seeds(depth_len, blocks)
    shape = jax.ShapeDtypeStruct((4, 4 * blocks, depth_len // 4), BF16)
    return pl.pallas_call(
        table_kernel,
        out_shape=(shape, shape),
        in_specs=[VMEM, VMEM],
        out_specs=(VMEM, VMEM),
        name="depth_tables",
        cost_estimate=pl.CostEstimate(flops=10_000_000, bytes_accessed=5_000_000, transcendentals=0),
    )(coarse, fine)


def depth_forward_kernel(x_ref, high_ref, low_ref, out_ref):
    rows = x_ref.shape[1]
    blocks = high_ref.shape[1] // 4
    a, b, c, d = x_ref[0], x_ref[1], x_ref[2], x_ref[3]
    even, odd = a + c, b + d
    both = jnp.concatenate([a - c, b - d], axis=0)

    def put(cls, real, imag):
        for plane, value in enumerate((real, imag)):
            for half in range(2):
                start = plane * 8 + half * 4 + cls
                out_ref[pl.ds(start, blocks, stride=16), :] = value[half * blocks : (half + 1) * blocks]

    top = 2 * blocks
    for cls, value in ((0, even + odd), (2, even - odd)):
        res = dot3((high_ref[cls], low_ref[cls]), split(value), NT)
        put(cls, res[:top], -res[top:])
    parts = split(both)
    res = dot3((high_ref[1], low_ref[1]), parts, NT)
    put(1, res[:top, :rows] - res[top:, rows:], -(res[top:, :rows] + res[:top, rows:]))
    res = dot3((high_ref[3], low_ref[3]), parts, NT)
    put(3, res[:top, :rows] + res[top:, rows:], res[:top, rows:] - res[top:, :rows])


def depth_forward(lines, tables):
    blocks = tables[0].shape[1] // 4
    return pl.pallas_call(
        depth_forward_kernel,
        out_shape=jax.ShapeDtypeStruct((blocks * 16, lines.shape[1]), F32),
        in_specs=[VMEM] * 3,
        out_specs=VMEM,
        name="depth_forward",
        cost_estimate=pl.CostEstimate(flops=1_600_000_000, bytes_accessed=6_000_000, transcendentals=0),
    )(lines, *tables)


def depth_inverse_kernel(y_ref, high_ref, low_ref, out_ref):
    rows = y_ref.shape[1]
    blocks = high_ref.shape[1] // 4

    def get(cls, plane):
        return jnp.concatenate(
            [y_ref[pl.ds(plane * 8 + half * 4 + cls, blocks, stride=16), :] for half in range(2)],
            axis=0,
        )

    def turn(cls, value):
        return dot3(split(value), (high_ref[cls], low_ref[cls]), TN)

    real, imag = get(0, 0), get(0, 1)
    first = lax.broadcasted_iota(jnp.int32, real.shape, 0) == 0
    real = jnp.where(first, 0.5 * real, real)
    imag = jnp.where(first, 0.5 * imag, imag)
    zero = turn(0, jnp.concatenate([real, -imag], axis=0))
    two = turn(2, jnp.concatenate([get(2, 0), -get(2, 1)], axis=0))
    real, imag = get(1, 0), get(1, 1)
    one = turn(
        1,
        jnp.concatenate(
            [jnp.concatenate([real, -imag], axis=0), jnp.concatenate([-imag, -real], axis=0)], axis=1
        ),
    )
    real, imag = get(3, 0), get(3, 1)
    odd = one + turn(
        3,
        jnp.concatenate(
            [jnp.concatenate([real, -imag], axis=0), jnp.concatenate([imag, real], axis=0)], axis=1
        ),
    )
    plus, minus = zero + two, zero - two
    out_ref[0] = plus + odd[:rows]
    out_ref[1] = minus + odd[rows:]
    out_ref[2] = plus - odd[:rows]
    out_ref[3] = minus - odd[rows:]


def depth_inverse(waves, tables):
    return pl.pallas_call(
        depth_inverse_kernel,
        out_shape=jax.ShapeDtypeStruct((4, waves.shape[1], tables[0].shape[2]), F32),
        in_specs=[VMEM] * 3,
        out_specs=VMEM,
        name="depth_inverse",
        cost_estimate=pl.CostEstimate(flops=1_600_000_000, bytes_accessed=6_000_000, transcendentals=0),
    )(waves, *tables)


def strike_tables(edge, scale):
    turn = 2.0 * np.pi / edge
    angle = turn * (np.outer(np.arange(edge), np.arange(edge)) % edge)
    cosine, sine = np.cos(angle), np.sin(angle)
    forward = np.block([[cosine, sine], [-sine, cosine]])
    twist = 2.0 * np.pi / (edge * edge) * np.outer(np.arange(edge), np.arange(edge))
    twist = np.stack([np.cos(twist), np.sin(twist)]) * scale
    return (*split_np(forward), *split_np(forward.T), twist.astype(np.float32))


def strike_kernel(
    x_ref, gain_ref, past_ref, fh_ref, fl_ref, bh_ref, bl_ref, twist_ref, modes_ref, out_ref, held
):
    edge = twist_ref.shape[1]
    forward = (fh_ref[...], fl_ref[...])
    backward = (bh_ref[...], bl_ref[...])
    cosine, sine = twist_ref[0], twist_ref[1]
    lanes = lambda value, m: value[:, m * edge : (m + 1) * edge]

    def gather(ref, m):
        return jnp.concatenate(
            [ref[pl.ds(plane * 8 + m, edge, stride=16), :] for plane in range(2)], axis=0
        )

    value = jnp.concatenate([gather(x_ref, m) for m in range(8)], axis=1)
    first = dot3(forward, split(value), NN)
    turned = []
    for m in range(8):
        part = lanes(first, m)
        real, imag = part[:edge], part[edge:]
        turned.append(
            jnp.concatenate([real * cosine + imag * sine, imag * cosine - real * sine], axis=1)
        )
    modes = dot3(forward, split(jnp.concatenate(turned, axis=0)), NT)
    for plane in range(2):
        for m in range(8):
            held[plane, pl.ds(m, edge, stride=8), :] = lanes(modes, m)[plane * edge : (plane + 1) * edge]
    spectrum = []
    for m in range(8):
        part = lanes(modes, m)
        rows = pl.ds(m, edge, stride=8)
        gain = gain_ref[rows, :]
        spectrum.append(
            jnp.concatenate(
                [gain * part[:edge] + past_ref[0, rows, :], gain * part[edge:] + past_ref[1, rows, :]],
                axis=0,
            )
        )
    third = dot3(backward, split(jnp.concatenate(spectrum, axis=1)), NN)
    turned = []
    for m in range(8):
        part = lanes(third, m)
        real, imag = part[:edge], part[edge:]
        turned.append(
            jnp.concatenate(
                [2.0 * (real * cosine - imag * sine), 2.0 * (imag * cosine + real * sine)], axis=1
            )
        )
    last = dot3(backward, split(jnp.concatenate(turned, axis=0)), NT)
    for plane in range(2):
        for m in range(8):
            out_ref[pl.ds(plane * 8 + m, edge, stride=16), :] = lanes(last, m)[
                plane * edge : (plane + 1) * edge
            ]
        for k in range(edge):
            modes_ref[plane, :, k * edge : (k + 1) * edge] = held[plane, k * 8 : (k + 1) * 8, :]


def strike_both(pencil, gain, past, tables):
    edge = tables[-1].shape[1]
    return pl.pallas_call(
        strike_kernel,
        out_shape=(
            jax.ShapeDtypeStruct((2, 8, edge * edge), F32),
            jax.ShapeDtypeStruct((edge * 16, edge), F32),
        ),
        in_specs=[VMEM] * 8,
        out_specs=(VMEM, VMEM),
        scratch_shapes=[pltpu.VMEM((2, edge * 8, edge), F32)],
        name="strike_both",
        cost_estimate=pl.CostEstimate(flops=1_600_000_000, bytes_accessed=6_000_000, transcendentals=0),
    )(pencil, gain, past, *tables)


def past_kernel(kernel_ref, history_ref, gain_ref, past_ref):
    tiles = kernel_ref.shape[2] // 128
    for tile in range(tiles):
        cols = pl.ds(tile * 128, 128)
        rows = pl.ds(tile * 8, 8)
        gain_ref[rows, :] = kernel_ref[0, :, cols]
        for plane in range(2):
            total = kernel_ref[1, :, cols] * history_ref[0, plane, :, cols]
            for lag in range(1, LAGS):
                total = total + kernel_ref[lag + 1, :, cols] * history_ref[lag, plane, :, cols]
            past_ref[plane, rows, :] = total


def past_sum(kernel, history):
    length = kernel.shape[2]
    block = 2048
    return pl.pallas_call(
        past_kernel,
        grid=(length // block,),
        out_shape=(
            jax.ShapeDtypeStruct((length // 16, 128), F32),
            jax.ShapeDtypeStruct((2, length // 16, 128), F32),
        ),
        in_specs=[
            pl.BlockSpec((LAGS + 1, 8, block), lambda i: (0, 0, i)),
            pl.BlockSpec((LAGS, 2, 8, block), lambda i: (0, 0, 0, i)),
        ],
        out_specs=(
            pl.BlockSpec((block // 16, 128), lambda i: (i, 0)),
            pl.BlockSpec((2, block // 16, 128), lambda i: (0, i, 0)),
        ),
        name="past_sum",
        cost_estimate=pl.CostEstimate(flops=4_200_000, bytes_accessed=14_700_000, transcendentals=0),
    )(kernel, history)


def inverse_sinh(value):
    magnitude = jnp.abs(value)
    positive = jnp.log(magnitude + jnp.sqrt(1.0 + magnitude * magnitude))
    return jnp.where(value < 0, -positive, positive)


def friction_rate(total_stress, rate_prev, weakening, log_state, strength):
    scaling = 0.5 * jnp.exp(weakening * log_state)
    rate_now = rate_prev
    for sweep in range(NEWTON_ITERS):
        scaled = rate_now * scaling
        residual = total_stress - DAMPING * rate_now - strength * inverse_sinh(scaled)
        slope_now = -DAMPING - strength * scaling / jnp.sqrt(1.0 + scaled * scaled)
        rate_now = rate_now - RELAXATION * residual / slope_now
    return rate_now


def body(fault_slip, rate_prev, log_state, weakening, strength, pre_stress, kernel, history):
    rows, cells = fault_slip.shape
    depth_size = lax.axis_size("depth")
    devices = lax.axis_size("strike") * depth_size
    edge = rows // depth_size
    depth_len = cells * depth_size
    tables = depth_tables(depth_len, devices)
    lines = lax.all_to_all(fault_slip.reshape(depth_size, edge, cells), "depth", 0, 0)
    gain, past = past_sum(kernel, history)
    waves = depth_forward(lines, tables)
    pencil = lax.all_to_all(waves.reshape(devices, 16, edge), ALL, 0, 0)
    scale = 1.0 / math.sqrt(depth_len * edge * devices)
    slip_modes, waves = strike_both(
        pencil.reshape(devices * 16, edge), gain, past, strike_tables(edge, scale)
    )
    waves = lax.all_to_all(waves.reshape(devices, 16, edge), ALL, 0, 0)
    cell_rows = depth_inverse(waves.reshape(devices * 16, edge), tables)
    elastic = lax.all_to_all(cell_rows, "depth", 0, 0).reshape(rows, cells)
    velocity = friction_rate(pre_stress + elastic, rate_prev, weakening, log_state, strength)
    return (velocity, fault_slip + ADVANCE * velocity, slip_modes)


def solution(mesh):
    return jax.shard_map(
        body,
        mesh=mesh,
        in_specs=(
            P("strike", "depth"),
            P("strike", "depth"),
            P("strike", "depth"),
            P("strike", "depth"),
            P("strike", "depth"),
            P("strike", "depth"),
            P(None, ("strike", "depth"), None),
            P(None, None, ("strike", "depth"), None),
        ),
        out_specs=(P("strike", "depth"), P("strike", "depth"), P(None, ("strike", "depth"), None)),
        check_vma=False,
    )
```

profile of v0, /device:TPU:1, one launch (start us, length us, event | category | flops | bytes accessed | tf_op | source)
XLA Modules:
  0.0 118.9 jit_solution(9373780628226846073)
XLA Ops:
  0.6 6.7 %all-to-all-start = ((f32[4,128,512]{2,1,0:T(8,128)}), f32[4,128,512]{2,1,0:T(8,128)S(1)}, u32[]{:S(2)}, u32[]{:S(2)}) async-start(f32[4,128,512]{2,1,0:T(8,128)} %bitcast.10), calls=%async_computation | async-start | bytes 2097152 | tf_op jit(solution)/shard_map/all_to_all | solution.py:313
  7.3 4.0 %depth_tables.1 = (bf16[4,512,512]{2,1,0:T(8,128)(2,1)}, bf16[4,512,512]{2,1,0:T(8,128)(2,1)}) custom-call(f32[2,128,512]{2,1,0:T(8,128)} %constant.22.clone.coarse_ref, f32[2,8,512]{2,1,0:T(8,128)} %constant.23.clone.fine_ref), custom_call_target="tpu_custom_call" | custom-call | flops 10000000 | bytes 5000000 | tf_op jit(solution)/shard_map/depth_tables/pallas_call | solution.py:72
  11.3 11.1 %all-to-all-done.x_ref = f32[4,128,512]{2,1,0:T(8,128)S(1)} async-done(((f32[4,128,512]{2,1,0:T(8,128)}), f32[4,128,512]{2,1,0:T(8,128)S(1)}, u32[]{:S(2)}, u32[]{:S(2)}) %all-to-all-start) | async-done | bytes 1048608 | tf_op jit(solution)/shard_map/all_to_all | solution.py:313
  22.4 0.0 copy-start.1
  22.4 1.0 copy-done.1
  23.4 5.5 %depth_forward.1 = f32[2048,128]{1,0:T(8,128)} custom-call(f32[4,128,512]{2,1,0:T(8,128)} %copy-done.1, bf16[4,512,512]{2,1,0:T(8,128)(2,1)} %get-tuple-element.9.high_ref, bf16[4,512,512]{2,1,0:T(8,128)(2,1)} %get-tuple-element.10.low_ref), custom_call_target="tpu_custom_call" | custom-call | flops 1600000000 | bytes 6000000 | tf_op jit(solution)/shard_map/depth_forward/pallas_call | solution.py:108
  28.8 7.9 %all-to-all-start.1 = ((f32[128,16,128]{2,1,0:T(8,128)}), f32[128,16,128]{2,1,0:T(8,128)S(1)}, u32[]{:S(2)}, u32[]{:S(2)}) async-start(f32[128,16,128]{2,1,0:T(8,128)} %bitcast.11), calls=%async_computation.1 | async-start | bytes 2097152 | tf_op jit(solution)/shard_map/all_to_all | solution.py:316
  36.7 8.0 %past_sum.1 = (f32[1024,128]{1,0:T(8,128)}, f32[2,1024,128]{2,1,0:T(8,128)}) custom-call(f32[9,8,16384]{2,1,0:T(8,128)} %kernel_ref.1, f32[8,2,8,16384]{3,2,1,0:T(8,128)} %history_ref.1), custom_call_target="tpu_custom_call" | custom-call | flops 4200000 | bytes 14700000 | tf_op jit(solution)/shard_map/past_sum/pallas_call | solution.py:269
  44.6 11.2 %all-to-all-done.1 = f32[128,16,128]{2,1,0:T(8,128)S(1)} async-done(((f32[128,16,128]{2,1,0:T(8,128)}), f32[128,16,128]{2,1,0:T(8,128)S(1)}, u32[]{:S(2)}, u32[]{:S(2)}) %all-to-all-start.1) | async-done | bytes 1048608 | tf_op jit(solution)/shard_map/all_to_all | solution.py:316
  55.9 0.0 copy-start.4
  55.9 1.0 copy-done.4
  56.8 5.8 %strike_both.1 = (f32[2,8,16384]{2,1,0:T(8,128)}, f32[2048,128]{1,0:T(8,128)}) custom-call(f32[2048,128]{1,0:T(8,128)} %bitcast.13, f32[1024,128]{1,0:T(8,128)} %get-tuple-element.11.gain_ref, f32[2,1024,128]{2,1,0:T(8,128)} %get-tuple-element.12.past_ref, bf16[256,256]{1,0:T(8,128)(2,1)} %constant.24.clone.fh_ref, bf16[256,256]{1,0:T(8,128)(2,1)} %constant.25.clone.fl_ref, ...), custom_call_target="tpu_custom_call" | custom-call | flops 1600000000 | bytes 6000000 | tf_op jit(solution)/shard_map/strike_both/pallas_call | solution.py:239
  62.7 24.8 %all_to_all.20 = f32[128,16,128]{2,1,0:T(8,128)} all-to-all(f32[128,16,128]{2,1,0:T(8,128)} %bitcast.14), channel_id=1, replica_groups=mesh['strike'=32,'depth'=4] {'strike','depth'}, dimensions={0} | all-to-all | bytes 2097152 | tf_op jit(solution)/shard_map/all_to_all | solution.py:321
  87.5 0.0 copy-start
  87.5 0.0 copy-start.2
  87.5 0.0 copy-start.3
  87.5 5.2 %depth_inverse.1 = f32[4,128,512]{2,1,0:T(8,128)} custom-call(f32[2048,128]{1,0:T(8,128)} %bitcast.12, bf16[4,512,512]{2,1,0:T(8,128)(2,1)} %get-tuple-element.9.high_ref, bf16[4,512,512]{2,1,0:T(8,128)(2,1)} %get-tuple-element.10.low_ref), custom_call_target="tpu_custom_call" | custom-call | flops 1600000000 | bytes 6000000 | tf_op jit(solution)/shard_map/depth_inverse/pallas_call | solution.py:159
  92.7 19.6 %all_to_all.21 = f32[4,128,512]{2,1,0:T(8,128)S(1)} all-to-all(f32[4,128,512]{2,1,0:T(8,128)} %depth_inverse.1), channel_id=1, replica_groups=mesh['strike'=32,'depth'=4] {'depth'}, dimensions={0} | all-to-all | bytes 2097152 | tf_op jit(solution)/shard_map/all_to_all | solution.py:323
  112.3 0.0 copy-done
  112.3 0.0 copy-done.2
  112.3 0.0 copy-done.3
  112.3 6.6 %multiply_add_fusion = (f32[512,512]{1,0:T(8,128)}, f32[512,512]{1,0:T(8,128)}) fusion(f32[512,512]{1,0:T(8,128)S(1)} %copy-done, f32[512,512]{1,0:T(8,128)S(1)} %copy-done.2, f32[512,512]{1,0:T(8,128)S(1)} %copy-done.3, f32[512,512]{1,0:T(8,128)} %param.18, f32[512,512]{1,0:T(8,128)} %param.17, f32[512,512]{1,0:T(8,128)} %param.20, ...), kind=kLoop, calls=%fused_computation.25 | loop fusion | flops 19398656 | bytes 9437184 | tf_op jit(solution)/shard_map/add | solution.py:325
Async XLA Ops:
  0.6 21.8 %all-to-all-start = ((f32[4,128,512]{2,1,0:T(8,128)}), f32[4,128,512]{2,1,0:T(8,128)S(1)}, u32[]{:S(2)}, u32[]{:S(2)}) async-start(f32[4,128,512]{2,1,0:T(8,128)} %bitcast.10), calls=%async_computation | async-start | bytes 2097152 | tf_op jit(solution)/shard_map/all_to_all | solution.py:313
  22.4 1.0 copy-start.1
  28.8 27.0 %all-to-all-start.1 = ((f32[128,16,128]{2,1,0:T(8,128)}), f32[128,16,128]{2,1,0:T(8,128)S(1)}, u32[]{:S(2)}, u32[]{:S(2)}) async-start(f32[128,16,128]{2,1,0:T(8,128)} %bitcast.11), calls=%async_computation.1 | async-start | bytes 2097152 | tf_op jit(solution)/shard_map/all_to_all | solution.py:316
  55.9 1.0 copy-start.4
  87.5 24.8 %copy-start = (f32[512,512]{1,0:T(8,128)S(1)}, f32[512,512]{1,0:T(8,128)}, u32[]{:S(2)}) copy-start(f32[512,512]{1,0:T(8,128)} %param.15) | copy-start | bytes 3145732
  87.5 24.8 %copy-start.2 = (f32[512,512]{1,0:T(8,128)S(1)}, f32[512,512]{1,0:T(8,128)}, u32[]{:S(2)}) copy-start(f32[512,512]{1,0:T(8,128)} %param.19) | copy-start | bytes 3145732
  87.5 24.8 %copy-start.3 = (f32[512,512]{1,0:T(8,128)S(1)}, f32[512,512]{1,0:T(8,128)}, u32[]{:S(2)}) copy-start(f32[512,512]{1,0:T(8,128)} %param.16) | copy-start | bytes 3145732
where the time goes:
time: 119 us
  blocking collectives  44.4 us (37%)
  Pallas kernels  28.4 us (24%)
  waiting for transfers between devices  22.3 us (19%)
  starting transfers between devices  14.5 us (12%)
  other arithmetic  6.57 us (6%)
  local copies, waits for them, and re-layouts  1.95 us (2%)
    all_to_all x1, blocking collectives, body(): waves = lax.all_to_all(waves.reshape(devices, 16, edge), ALL, 0, 0)  24.8 us
    all_to_all x1, blocking collectives, body(): elastic = lax.all_to_all(cell_rows, 'depth', 0, 0).reshape(rows, cells)  19.6 us
    all_to_all x1, waiting for transfers between devices, body(): pencil = lax.all_to_all(waves.reshape(devices, 16, edge), ALL, 0, 0)  11.2 us
    all_to_all x1, waiting for transfers between devices, body(): lax.all_to_all(fault_slip.reshape(depth_size, edge, cells), 'depth', 0, 0)  11.1 us
    pallas_call x1, Pallas kernels, past_sum(): pl.pallas_call(past_kernel, grid=(length // block,), out_shape=(jax.Shape...  7.95 us
    all_to_all x1, starting transfers between devices, body(): pencil = lax.all_to_all(waves.reshape(devices, 16, edge), ALL, 0, 0)  7.85 us
    all_to_all x1, starting transfers between devices, body(): lax.all_to_all(fault_slip.reshape(depth_size, edge, cells), 'depth', 0, 0)  6.66 us
    add x1, other arithmetic, body(): return (velocity, fault_slip + ADVANCE * velocity, slip_modes)  6.57 us
  transfers between devices with their start and end apart: 2, of which 2 were waited for; matrix products, arithmetic and copies ran while one was open for 0% of the time, Pallas kernels for 10%

commit v1 on v0

v1 whole, which is shorter than its diff:
```python
import functools
import math

import jax
import jax.numpy as jnp
import ml_dtypes
import numpy as np
from jax import lax
from jax.experimental import pallas as pl
from jax.experimental.pallas import tpu as pltpu
from jax.sharding import PartitionSpec as P

NEWTON_ITERS = 4
DAMPING = 0.5
RELAXATION = 0.5
ADVANCE = 0.5
LAGS = 8
FORWARD = ((0, 384), (384, 128))
INVERSE = ((0, 128), (128, 256), (384, 128))
GRANT = 16 << 20
WIDE = 24 << 20
ALL = ("strike", "depth")
F32 = jnp.float32
BF16 = jnp.bfloat16
NN = (((1,), (0,)), ((), ()))
NT = (((1,), (1,)), ((), ()))
TN = (((0,), (0,)), ((), ()))
VMEM = pl.BlockSpec(memory_space=pltpu.VMEM)
SMEM = pl.BlockSpec(memory_space=pltpu.SMEM)
HBM = pl.BlockSpec(memory_space=pltpu.HBM)


def split_np(table):
    high = table.astype(ml_dtypes.bfloat16)
    low = (table - high.astype(np.float64)).astype(ml_dtypes.bfloat16)
    return high, low


def split(value):
    high = value.astype(BF16)
    return high, (value - high.astype(F32)).astype(BF16)


def in_hbm(*values):
    return [pltpu.with_memory_space_constraint(jnp.asarray(v), pltpu.HBM) for v in values]


def dot3(left, right, dims):
    mul = functools.partial(lax.dot_general, dimension_numbers=dims, preferred_element_type=F32)
    return mul(left[0], right[0]) + (mul(left[0], right[1]) + mul(left[1], right[0]))


def depth_seeds(depth_len, blocks):
    cells = depth_len // 4
    cell = np.arange(cells)
    turn = 2.0 * np.pi / depth_len
    coarse = turn * ((8 * np.arange(blocks)[:, None] * cell[None]) % depth_len)
    fine = turn * ((np.arange(8)[:, None] * cell[None]) % depth_len)
    pack = lambda angle: np.stack([np.cos(angle), np.sin(angle)]).astype(np.float32)
    return pack(coarse), pack(fine)


def table_kernel(coarse_ref, fine_ref, high_ref, low_ref):
    blocks = coarse_ref.shape[1]
    cos_a, sin_a = coarse_ref[0], coarse_ref[1]
    for cls in range(4):
        for half in range(2):
            row = 4 * half + cls
            cos_b, sin_b = fine_ref[0, row : row + 1, :], fine_ref[1, row : row + 1, :]
            for part, value in enumerate(
                (cos_a * cos_b - sin_a * sin_b, sin_a * cos_b + cos_a * sin_b)
            ):
                high, low = split(value)
                rows = pl.ds((part * 2 + half) * blocks, blocks)
                high_ref[cls, rows, :] = high
                low_ref[cls, rows, :] = low


def depth_tables(depth_len, blocks):
    coarse, fine = depth_seeds(depth_len, blocks)
    shape = jax.ShapeDtypeStruct((4, 4 * blocks, depth_len // 4), BF16)
    return pl.pallas_call(
        table_kernel,
        out_shape=(shape, shape),
        in_specs=[VMEM, VMEM],
        out_specs=(VMEM, VMEM),
        compiler_params=pltpu.CompilerParams(vmem_limit_bytes=GRANT),
        name="depth_tables",
        cost_estimate=pl.CostEstimate(flops=10_000_000, bytes_accessed=5_000_000, transcendentals=0),
    )(coarse, fine)


def depth_forward_kernel(first, column, me_ref, own_ref, one_ref, two_ref, three_ref, high_ref, low_ref, *refs):
    rows, cells = own_ref.shape
    blocks = high_ref.shape[1] // 4
    cols = pl.ds(column, cells)
    me = me_ref[0]
    swap = (me & 1) == 1
    tau = (1 - 2 * (me & 1)).astype(F32)
    sigma = (1 - (me & 2)).astype(F32)
    even, odd = own_ref[...] + two_ref[...], one_ref[...] + three_ref[...]
    left, right = sigma * (own_ref[...] - two_ref[...]), sigma * (one_ref[...] - three_ref[...])
    both = jnp.concatenate(
        [jnp.where(swap, right, left), jnp.where(swap, left, right)], axis=0
    )

    def put(cls, real, imag):
        for plane, value in enumerate((real, imag)):
            for half in range(2):
                part = value[half * blocks : (half + 1) * blocks]
                slot = cls * 4 + plane * 2 + half
                if first:
                    refs[0][slot] = part
                else:
                    start = plane * 8 + half * 4 + cls
                    refs[1][pl.ds(start, blocks, stride=16), :] = part + refs[0][slot]

    def turn(cls, parts):
        return dot3((high_ref[cls, :, cols], low_ref[cls, :, cols]), parts, NT)

    top = 2 * blocks
    for cls, value in ((0, even + odd), (2, tau * (even - odd))):
        res = turn(cls, split(value))
        put(cls, res[:top], -res[top:])
    parts = split(both)
    res = turn(1, parts)
    put(1, res[:top, :rows] - res[top:, rows:], -(res[top:, :rows] + res[:top, rows:]))
    res = turn(3, parts)
    put(3, res[:top, :rows] + res[top:, rows:], res[:top, rows:] - res[top:, :rows])


def depth_forward(column, me, parts, tables, held=None):
    blocks = tables[0].shape[1] // 4
    rows = parts[0].shape[0]
    first = held is None
    shape = (16, blocks, rows) if first else (blocks * 16, rows)
    return pl.pallas_call(
        functools.partial(depth_forward_kernel, first, column),
        out_shape=jax.ShapeDtypeStruct(shape, F32),
        in_specs=[SMEM] + [VMEM] * (6 if first else 7),
        out_specs=VMEM,
        compiler_params=pltpu.CompilerParams(vmem_limit_bytes=GRANT),
        name="depth_forward",
        cost_estimate=pl.CostEstimate(flops=1_200_000_000, bytes_accessed=4_000_000, transcendentals=0),
    )(me, *parts, *tables, *(() if first else (held,)))


def depth_inverse_kernel(column, me_ref, y_ref, high_ref, low_ref, own_ref, one_ref, two_ref, three_ref):
    rows, cells = own_ref.shape
    blocks = high_ref.shape[1] // 4
    cols = pl.ds(column, cells)
    me = me_ref[0]
    swap = (me & 1) == 1
    tau = (1 - 2 * (me & 1)).astype(F32)
    sigma = (1 - (me & 2)).astype(F32)

    def get(cls, plane):
        return jnp.concatenate(
            [y_ref[pl.ds(plane * 8 + half * 4 + cls, blocks, stride=16), :] for half in range(2)],
            axis=0,
        )

    def turn(cls, value):
        return dot3(split(value), (high_ref[cls, :, cols], low_ref[cls, :, cols]), TN)

    real, imag = get(0, 0), get(0, 1)
    first = lax.broadcasted_iota(jnp.int32, real.shape, 0) == 0
    real = jnp.where(first, 0.5 * real, real)
    imag = jnp.where(first, 0.5 * imag, imag)
    zero = turn(0, jnp.concatenate([real, -imag], axis=0))
    two = tau * turn(2, jnp.concatenate([get(2, 0), -get(2, 1)], axis=0))
    real, imag = get(1, 0), get(1, 1)
    odd = turn(
        1,
        jnp.concatenate(
            [jnp.concatenate([real, -imag], axis=0), jnp.concatenate([-imag, -real], axis=0)], axis=1
        ),
    )
    real, imag = get(3, 0), get(3, 1)
    odd = sigma * (
        odd
        + turn(
            3,
            jnp.concatenate(
                [jnp.concatenate([real, -imag], axis=0), jnp.concatenate([imag, real], axis=0)], axis=1
            ),
        )
    )
    low, high = odd[:rows], odd[rows:]
    base, turned = zero + two, jnp.where(swap, high, low)
    own_ref[...] = base + turned
    two_ref[...] = base - turned
    base, turned = zero - two, jnp.where(swap, low, high)
    one_ref[...] = base + turned
    three_ref[...] = base - turned


def depth_inverse(column, width, me, waves, tables):
    rows = waves.shape[1]
    shape = jax.ShapeDtypeStruct((rows, width), F32)
    return pl.pallas_call(
        functools.partial(depth_inverse_kernel, column),
        out_shape=(shape,) * 4,
        in_specs=[SMEM] + [VMEM] * 3,
        out_specs=(VMEM,) * 4,
        compiler_params=pltpu.CompilerParams(vmem_limit_bytes=GRANT),
        name="depth_inverse",
        cost_estimate=pl.CostEstimate(flops=1_200_000_000, bytes_accessed=4_000_000, transcendentals=0),
    )(me, waves, *tables)


def strike_tables(edge, scale):
    turn = 2.0 * np.pi / edge
    angle = turn * (np.outer(np.arange(edge), np.arange(edge)) % edge)
    waves = np.stack([*split_np(np.cos(angle)), *split_np(np.sin(angle))])
    twist = 2.0 * np.pi / (edge * edge) * np.outer(np.arange(edge), np.arange(edge))
    twist = np.stack([np.cos(twist), np.sin(twist)]) * scale
    return waves, twist.astype(np.float32)


def strike_kernel(
    x_ref, gain_hbm, past_hbm, wave_hbm, twist_hbm, modes_hbm, out_ref,
    gain_ref, past_ref, wave_ref, twist_ref, held, modes_ref, sems,
):
    edge = twist_ref.shape[1]
    pairs = ((wave_hbm, wave_ref), (twist_hbm, twist_ref), (gain_hbm, gain_ref), (past_hbm, past_ref))
    loads = [pltpu.make_async_copy(a, b, sems.at[n]) for n, (a, b) in enumerate(pairs)]
    for load in loads:
        load.start()
    lanes = lambda value, m: value[:, m * edge : (m + 1) * edge]

    def gather(ref, m):
        return jnp.concatenate(
            [ref[pl.ds(plane * 8 + m, edge, stride=16), :] for plane in range(2)], axis=0
        )

    parts = split(jnp.concatenate([gather(x_ref, m) for m in range(8)], axis=1))
    loads[0].wait()

    def block(sign, part):
        cosine, sine = wave_ref[part], wave_ref[2 + part]
        left, right = (sine, -sine) if sign > 0 else (-sine, sine)
        return jnp.concatenate(
            [jnp.concatenate([cosine, left], axis=1), jnp.concatenate([right, cosine], axis=1)], axis=0
        )

    forward = (block(1, 0), block(1, 1))
    backward = (block(-1, 0), block(-1, 1))
    first = dot3(forward, parts, NN)
    loads[1].wait()
    cosine, sine = twist_ref[0], twist_ref[1]
    turned = []
    for m in range(8):
        part = lanes(first, m)
        real, imag = part[:edge], part[edge:]
        turned.append(
            jnp.concatenate([real * cosine + imag * sine, imag * cosine - real * sine], axis=1)
        )
    modes = dot3(forward, split(jnp.concatenate(turned, axis=0)), NT)
    for plane in range(2):
        for m in range(8):
            held[plane, pl.ds(m, edge, stride=8), :] = lanes(modes, m)[plane * edge : (plane + 1) * edge]
        for k in range(edge):
            modes_ref[plane, :, k * edge : (k + 1) * edge] = held[plane, k * 8 : (k + 1) * 8, :]
    save = pltpu.make_async_copy(modes_ref, modes_hbm, sems.at[4])
    save.start()
    loads[2].wait()
    loads[3].wait()
    spectrum = []
    for m in range(8):
        part = lanes(modes, m)
        rows = pl.ds(m, edge, stride=8)
        gain = gain_ref[rows, :]
        spectrum.append(
            jnp.concatenate(
                [gain * part[:edge] + past_ref[0, rows, :], gain * part[edge:] + past_ref[1, rows, :]],
                axis=0,
            )
        )
    third = dot3(backward, split(jnp.concatenate(spectrum, axis=1)), NN)
    turned = []
    for m in range(8):
        part = lanes(third, m)
        real, imag = part[:edge], part[edge:]
        turned.append(
            jnp.concatenate(
                [2.0 * (real * cosine - imag * sine), 2.0 * (imag * cosine + real * sine)], axis=1
            )
        )
    last = dot3(backward, split(jnp.concatenate(turned, axis=0)), NT)
    for plane in range(2):
        for m in range(8):
            out_ref[pl.ds(plane * 8 + m, edge, stride=16), :] = lanes(last, m)[
                plane * edge : (plane + 1) * edge
            ]
    save.wait()


def strike_both(pencil, gain, past, tables):
    waves, twist = tables
    edge = twist.shape[1]
    modes = (2, 8, edge * edge)
    return pl.pallas_call(
        strike_kernel,
        out_shape=(
            jax.ShapeDtypeStruct(modes, F32),
            jax.ShapeDtypeStruct((edge * 16, edge), F32),
        ),
        in_specs=[VMEM] + [HBM] * 4,
        out_specs=(HBM, VMEM),
        scratch_shapes=[
            pltpu.VMEM(gain.shape, F32),
            pltpu.VMEM(past.shape, F32),
            pltpu.VMEM(waves.shape, BF16),
            pltpu.VMEM(twist.shape, F32),
            pltpu.VMEM((2, edge * 8, edge), F32),
            pltpu.VMEM(modes, F32),
            pltpu.SemaphoreType.DMA((5,)),
        ],
        compiler_params=pltpu.CompilerParams(vmem_limit_bytes=WIDE),
        name="strike_both",
        cost_estimate=pl.CostEstimate(flops=1_600_000_000, bytes_accessed=6_000_000, transcendentals=0),
    )(pencil, *in_hbm(gain, past, waves, twist))


def past_kernel(kernel_ref, history_ref, gain_ref, past_ref):
    tiles = kernel_ref.shape[2] // 128
    for tile in range(tiles):
        cols = pl.ds(tile * 128, 128)
        rows = pl.ds(tile * 8, 8)
        gain_ref[rows, :] = kernel_ref[0, :, cols]
        for plane in range(2):
            total = kernel_ref[1, :, cols] * history_ref[0, plane, :, cols]
            for lag in range(1, LAGS):
                total = total + kernel_ref[lag + 1, :, cols] * history_ref[lag, plane, :, cols]
            past_ref[plane, rows, :] = total


def past_sum(kernel, history):
    length = kernel.shape[2]
    block = 2048
    return pl.pallas_call(
        past_kernel,
        grid=(length // block,),
        out_shape=(
            jax.ShapeDtypeStruct((length // 16, 128), F32),
            jax.ShapeDtypeStruct((2, length // 16, 128), F32),
        ),
        in_specs=[
            pl.BlockSpec((LAGS + 1, 8, block), lambda i: (0, 0, i)),
            pl.BlockSpec((LAGS, 2, 8, block), lambda i: (0, 0, 0, i)),
        ],
        out_specs=(
            pl.BlockSpec((block // 16, 128), lambda i: (i, 0)),
            pl.BlockSpec((2, block // 16, 128), lambda i: (0, i, 0)),
        ),
        compiler_params=pltpu.CompilerParams(vmem_limit_bytes=WIDE),
        name="past_sum",
        cost_estimate=pl.CostEstimate(flops=4_200_000, bytes_accessed=14_700_000, transcendentals=0),
    )(*in_hbm(kernel, history))


def newton_parts(rate, scaling, strength):
    scaled = rate * scaling
    magnitude = jnp.abs(scaled)
    square = 1.0 + scaled * scaled
    inverse = lax.rsqrt(square)
    positive = jnp.log(magnitude + square * inverse)
    friction = strength * jnp.where(scaled < 0, -positive, positive)
    return friction, 1.0 + (strength * scaling) * (inverse * (1.0 / DAMPING))


STEP = RELAXATION / DAMPING


def start_kernel(rate_ref, state_ref, weak_ref, strength_ref, stress_ref, scale_ref, rest_ref, gain_ref):
    scaling = 0.5 * jnp.exp(weak_ref[...] * state_ref[...])
    rate = rate_ref[...]
    friction, divisor = newton_parts(rate, scaling, strength_ref[...])
    gain = STEP / divisor
    scale_ref[...] = scaling
    gain_ref[...] = gain
    rest_ref[...] = rate + gain * (stress_ref[...] - DAMPING * rate - friction)


def friction_start(rate_prev, log_state, weakening, strength, pre_stress):
    rows, cells = rate_prev.shape
    spec = pl.BlockSpec((64, cells), lambda i: (i, 0))
    shape = jax.ShapeDtypeStruct((rows, cells), F32)
    return pl.pallas_call(
        start_kernel,
        grid=(rows // 64,),
        out_shape=(shape,) * 3,
        in_specs=[spec] * 5,
        out_specs=(spec,) * 3,
        compiler_params=pltpu.CompilerParams(vmem_limit_bytes=GRANT),
        name="friction_start",
        cost_estimate=pl.CostEstimate(flops=20_000_000, bytes_accessed=8_000_000, transcendentals=1_000_000),
    )(rate_prev, log_state, weakening, strength, pre_stress)


def friction_kernel(
    column, me_ref, own_ref, one_ref, two_ref, three_ref, scale_ref, rest_ref, gain_ref, strength_ref,
    stress_ref, slip_ref, *refs
):
    velocity_hbm, new_hbm, velocity_ref, new_ref, sems = refs[-5:]
    edge, width = own_ref.shape
    cols = pl.ds(column, width)
    saves = []
    for slot, ref in enumerate((own_ref, one_ref, two_ref, three_ref)):
        rows = pl.ds(pl.multiple_of((me_ref[0] ^ slot) * edge, edge), edge)
        elastic = ref[...]
        scaling, strength = scale_ref[rows, cols], strength_ref[rows, cols]
        total = stress_ref[rows, cols] + elastic
        rate = rest_ref[rows, cols] + gain_ref[rows, cols] * elastic
        for sweep in range(NEWTON_ITERS - 1):
            friction, divisor = newton_parts(rate, scaling, strength)
            rate = rate + STEP * (total - DAMPING * rate - friction) / divisor
        velocity_ref[slot] = rate
        new_ref[slot] = slip_ref[rows, cols] + ADVANCE * rate
        for n, (source, target) in enumerate(((velocity_ref, velocity_hbm), (new_ref, new_hbm))):
            save = pltpu.make_async_copy(source.at[slot], target.at[rows, cols], sems.at[slot, n])
            save.start()
            saves.append(save)
    for save in saves:
        save.wait()


def friction_finish(column, me, elastic, start, strength, pre_stress, fault_slip, held=()):
    edge, width = elastic[0].shape
    shape = jax.ShapeDtypeStruct(fault_slip.shape, F32)
    count = 1 + 4 + 6
    return pl.pallas_call(
        functools.partial(friction_kernel, column),
        in_specs=[SMEM] + [VMEM] * 10 + [HBM] * len(held),
        out_specs=(HBM, HBM),
        out_shape=(shape, shape),
        scratch_shapes=[
            pltpu.VMEM((4, edge, width), F32),
            pltpu.VMEM((4, edge, width), F32),
            pltpu.SemaphoreType.DMA((4, 2)),
        ],
        input_output_aliases={count + n: n for n in range(len(held))},
        compiler_params=pltpu.CompilerParams(vmem_limit_bytes=GRANT),
        name="friction_finish",
        cost_estimate=pl.CostEstimate(flops=20_000_000, bytes_accessed=5_000_000, transcendentals=1_000_000),
    )(me, *elastic, *start, strength, pre_stress, fault_slip, *in_hbm(*held))


def exchange(parts, size):
    swap = lambda part, k: lax.ppermute(part, "depth", [(place, place ^ k) for place in range(size)])
    moved = {k: swap(parts[k], k) for k in (2, 3, 1)}
    return [parts[0]] + [moved[k] for k in (1, 2, 3)]


def body(fault_slip, rate_prev, log_state, weakening, strength, pre_stress, kernel, history):
    rows, cells = fault_slip.shape
    depth_size = lax.axis_size("depth")
    devices = lax.axis_size("strike") * depth_size
    edge = rows // depth_size
    depth_len = cells * depth_size
    place = lax.axis_index("depth")
    me = place.reshape(1)
    lines, source = [], fault_slip
    for column, width in FORWARD:
        blocks = [
            lax.dynamic_slice(source, ((place ^ k) * edge, column), (edge, width))
            for k in range(depth_size)
        ]
        source, *blocks = lax.optimization_barrier((source, *blocks))
        lines.append(exchange(blocks, depth_size))
    tables = depth_tables(depth_len, devices)
    gain, past = past_sum(kernel, history)
    start = friction_start(rate_prev, log_state, weakening, strength, pre_stress)
    waves = None
    for (column, _), parts in zip(FORWARD, lines):
        waves = depth_forward(column, me, parts, tables, waves)
    pencil = lax.all_to_all(waves.reshape(devices, 16, edge), ALL, 0, 0)
    scale = 1.0 / math.sqrt(depth_len * edge * devices)
    slip_modes, waves = strike_both(
        pencil.reshape(devices * 16, edge), gain, past, strike_tables(edge, scale)
    )
    waves = lax.all_to_all(waves.reshape(devices, 16, edge), ALL, 0, 0).reshape(devices * 16, edge)
    elastic = [
        exchange(depth_inverse(column, width, me, waves, tables), depth_size)
        for column, width in INVERSE
    ]
    out = ()
    for (column, _), parts in zip(INVERSE, elastic):
        out = friction_finish(column, me, parts, start, strength, pre_stress, fault_slip, out)
    return (*out, slip_modes)


def solution(mesh):
    return jax.shard_map(
        body,
        mesh=mesh,
        in_specs=(
            P("strike", "depth"),
            P("strike", "depth"),
            P("strike", "depth"),
            P("strike", "depth"),
            P("strike", "depth"),
            P("strike", "depth"),
            P(None, ("strike", "depth"), None),
            P(None, None, ("strike", "depth"), None),
        ),
        out_specs=(P("strike", "depth"), P("strike", "depth"), P(None, ("strike", "depth"), None)),
        check_vma=False,
    )
```

time: 119 us -> 103 us (0.87)
  blocking collectives: 44.4 us -> 23.3 us
  starting transfers between devices: 14.5 us -> 30.9 us
  other arithmetic: 6.57 us -> 0 us
  waiting for transfers between devices: 22.3 us -> 17.2 us
  local copies, waits for them, and re-layouts: 1.95 us -> 5.84 us
  Pallas kernels: 28.4 us -> 24.7 us
    ppermute x0 -> x15, starting transfers between devices: none -> 22.6 us  [exchange(): lax.ppermute(part, 'depth', [(place, place ^ k) for place in range(size)])]
    all_to_all x2 -> x1, blocking collectives: 44.4 us -> 23.3 us  [body(): lax.all_to_all(waves.reshape(devices, 16, edge), ALL, 0, 0)]
    all_to_all x1 -> x0, waiting for transfers between devices: 11.1 us -> none  [body(): lax.all_to_all(fault_slip.reshape(depth_size, edge, cells), 'depth', 0, 0)]
    ppermute x0 -> x15, waiting for transfers between devices: none -> 6.68 us  [exchange(): lax.ppermute(part, 'depth', [(place, place ^ k) for place in range(size)])]
    all_to_all x1 -> x0, starting transfers between devices: 6.66 us -> none  [body(): lax.all_to_all(fault_slip.reshape(depth_size, edge, cells), 'depth', 0, 0)]
    add x1 -> x0, other arithmetic: 6.57 us -> none  [body(): return (velocity, fault_slip + ADVANCE * velocity, slip_modes)]
    pallas_call x1, Pallas kernels: 3.97 us -> 1.02 us  [depth_tables(): pl.pallas_call(table_kernel, out_shape=(shape, shape), in_specs=[VMEM, VM...]
    dynamic_slice x0 -> x2, local copies, waits for them, and re-layouts: none -> 2.24 us  [body(): lax.dynamic_slice(source, ((place ^ k) * edge, column), (edge, width))]
  transfers between devices with their start and end apart: 2 -> 16, of which waited for: 2 -> 4; matrix products, arithmetic and copies ran while one was open for 0% -> 1% of each run, Pallas kernels for 10% -> 16%
where the time goes in v1:
time: 103 us
  starting transfers between devices  30.9 us (30%)
  Pallas kernels  24.7 us (24%)
  blocking collectives  23.3 us (23%)
  waiting for transfers between devices  17.2 us (17%)
  local copies, waits for them, and re-layouts  5.84 us (6%)
  between operations  1.06 us (1%)
    all_to_all x1, blocking collectives, body(): lax.all_to_all(waves.reshape(devices, 16, edge), ALL, 0, 0)  23.3 us
    ppermute x15, starting transfers between devices, exchange(): lax.ppermute(part, 'depth', [(place, place ^ k) for place in range(size)])  22.6 us
    all_to_all x1, waiting for transfers between devices, body(): pencil = lax.all_to_all(waves.reshape(devices, 16, edge), ALL, 0, 0)  10.6 us
    all_to_all x1, starting transfers between devices, body(): pencil = lax.all_to_all(waves.reshape(devices, 16, edge), ALL, 0, 0)  8.34 us
    pallas_call x1, Pallas kernels, past_sum(): pl.pallas_call(past_kernel, grid=(length // block,), out_shape=(jax.Shape...  6.81 us
    ppermute x15, waiting for transfers between devices, exchange(): lax.ppermute(part, 'depth', [(place, place ^ k) for place in range(size)])  6.68 us
    pallas_call x3, Pallas kernels, friction_finish(): pl.pallas_call(functools.partial(friction_kernel, column), in_specs=[SMEM...  4.83 us
    pallas_call x1, Pallas kernels, strike_both(): pl.pallas_call(strike_kernel, out_shape=(jax.ShapeDtypeStruct(modes, F32)...  4.1 us
  transfers between devices with their start and end apart: 16, of which 4 were waited for; matrix products, arithmetic and copies ran while one was open for 1% of the time, Pallas kernels for 16%

profile of v1, /device:TPU:1, one launch (start us, length us, event | category | flops | bytes accessed | tf_op | source)
XLA Modules:
  0.0 103.0 jit_solution(1769805190478896065)
XLA Ops:
  0.7 1.3 %constant_dynamic-slice_fusion.4 = (f32[128,384]{1,0:T(8,128)S(1)}, f32[128,384]{1,0:T(8,128)S(1)}, f32[128,384]{1,0:T(8,128)S(1)}, f32[128,384]{1,0:T(8,128)S(1)}) fusion(f32[512,512]{1,0:T(8,128)} %slip_ref.5, s32[]{:T(128)S(6)} %select_n.19, s32[]{:T(128)S(6)} %select_n.18, s32[]{:T(128)S(6)} %select_n.17, s32[]{:T(128)S(6)} %select_n.16), kind=kLoop, calls=%fused_computation.4 | loop fusion | bytes 1572880 | tf_op jit(solution)/shard_map/dynamic_slice | solution.py:467
  1.9 1.5 %collective-permute-start.3 = (f32[128,384]{1,0:T(8,128)S(1)}, f32[128,384]{1,0:T(8,128)S(1)}, u32[]{:S(2)}, u32[]{:S(2)}) collective-permute-start(f32[128,384]{1,0:T(8,128)S(1)} %get-tuple-element.47), channel_id=1, source_target_pairs={{0,1},{1,0},{2,3},{3,2},{4,5},{5,4},{6,7},{7,6},{8,9},{9,8},{10,11... | collective-permute-start | bytes 589832 | tf_op jit(solution)/shard_map/ppermute | solution.py:451
  3.4 3.7 %collective-permute-start.4 = (f32[128,384]{1,0:T(8,128)S(1)}, f32[128,384]{1,0:T(8,128)S(1)}, u32[]{:S(2)}, u32[]{:S(2)}) collective-permute-start(f32[128,384]{1,0:T(8,128)S(1)} %get-tuple-element.48), channel_id=1, source_target_pairs={{0,2},{1,3},{2,0},{3,1},{4,6},{5,7},{6,4},{7,5},{8,10},{9,11},{10,... | collective-permute-start | bytes 589832 | tf_op jit(solution)/shard_map/ppermute | solution.py:451
  7.1 0.1 collective-permute-start.5
  7.2 1.0 constant_dynamic-slice_fusion
  8.1 0.4 collective-permute-start
  8.6 3.0 %collective-permute-start.1 = (f32[128,128]{1,0:T(8,128)S(1)}, f32[128,128]{1,0:T(8,128)S(1)}, u32[]{:S(2)}, u32[]{:S(2)}) collective-permute-start(f32[128,128]{1,0:T(8,128)S(1)} %get-tuple-element.42), channel_id=1, source_target_pairs={{0,2},{1,3},{2,0},{3,1},{4,6},{5,7},{6,4},{7,5},{8,10},{9,11},{10,... | collective-permute-start | bytes 196616 | tf_op jit(solution)/shard_map/ppermute | solution.py:451
  11.5 1.0 %copy-done.8 = f32[2,128,512]{2,1,0:T(8,128)S(1)} copy-done((f32[2,128,512]{2,1,0:T(8,128)S(1)}, f32[2,128,512]{2,1,0:T(8,128)}, u32[]{:S(2)}) %copy-start.8) | copy-done | bytes 524312
  12.6 0.8 copy-done.9
  13.3 1.0 depth_tables.1
  14.4 0.0 copy-start
  14.4 0.0 collective-permute-done.3.one_ref
  14.4 0.4 collective-permute-start.2
  14.8 0.0 collective-permute-done.4.two_ref
  14.8 2.0 %collective-permute-done.5.three_ref = f32[128,384]{1,0:T(8,128)S(1)} collective-permute-done((f32[128,384]{1,0:T(8,128)S(1)}, f32[128,384]{1,0:T(8,128)S(1)}, u32[]{:S(2)}, u32[]{:S(2)}) %collective-permute-start.5) | collective-permute-done | bytes 196640 | tf_op jit(solution)/shard_map/ppermute | solution.py:451
  16.8 1.7 %depth_forward.2.refs_0_ = f32[16,128,128]{2,1,0:T(8,128)S(1)} custom-call(s32[1]{0:T(128)} %bitcast.me_ref, f32[128,384]{1,0:T(8,128)S(1)} %get-tuple-element.46.own_ref, f32[128,384]{1,0:T(8,128)S(1)} %collective-permute-done.3.one_ref, f32[128,384]{1,0:T(8,128)S(1)} %collective-permute-done.4.two_ref, f32[128,384]{1,0:T(8,128)S(1)} %collective-permute-done.5.three_ref, ...), custom_call_target="tpu_custom_call" | custom-call | flops 1200000000 | bytes 4000000 | tf_op jit(solution)/shard_map/depth_forward/pallas_call | solution.py:137
  18.5 0.0 collective-permute-done.one_ref
  18.5 0.0 collective-permute-done.1.two_ref
  18.5 2.1 %collective-permute-done.2.three_ref = f32[128,128]{1,0:T(8,128)S(1)} collective-permute-done((f32[128,128]{1,0:T(8,128)S(1)}, f32[128,128]{1,0:T(8,128)S(1)}, u32[]{:S(2)}, u32[]{:S(2)}) %collective-permute-start.2) | collective-permute-done | bytes 65568 | tf_op jit(solution)/shard_map/ppermute | solution.py:451
  20.6 2.0 %depth_forward.3 = f32[2048,128]{1,0:T(8,128)} custom-call(s32[1]{0:T(128)} %bitcast.me_ref, f32[128,128]{1,0:T(8,128)S(1)} %get-tuple-element.40.own_ref, f32[128,128]{1,0:T(8,128)S(1)} %collective-permute-done.one_ref, f32[128,128]{1,0:T(8,128)S(1)} %collective-permute-done.1.two_ref, f32[128,128]{1,0:T(8,128)S(1)} %collective-permute-done.2.three_ref, ...), custom_call_target="tpu_custom_call" | custom-call | flops 1200000000 | bytes 4000000 | tf_op jit(solution)/shard_map/depth_forward/pallas_call | solution.py:137
  22.6 0.0 copy-done
  22.6 8.3 %all-to-all-start = ((f32[128,16,128]{2,1,0:T(8,128)}), f32[128,16,128]{2,1,0:T(8,128)S(1)}, u32[]{:S(2)}, u32[]{:S(2)}) async-start(f32[128,16,128]{2,1,0:T(8,128)} %bitcast.1), calls=%async_computation | async-start | bytes 2097152 | tf_op jit(solution)/shard_map/all_to_all | solution.py:478
  30.9 6.8 %past_sum.1 = (f32[1024,128]{1,0:T(8,128)S(1)}, f32[2,1024,128]{2,1,0:T(8,128)S(1)}) custom-call(f32[9,8,16384]{2,1,0:T(8,128)} %kernel_ref.1, f32[8,2,8,16384]{3,2,1,0:T(8,128)} %history_ref.1), custom_call_target="tpu_custom_call" | custom-call | flops 4200000 | bytes 14700000 | tf_op jit(solution)/shard_map/past_sum/pallas_call | solution.py:342
  37.7 0.0 copy-start.10
  37.8 1.0 copy-done.10
  38.7 0.8 copy-done.11
  39.5 10.6 %all-to-all-done = f32[128,16,128]{2,1,0:T(8,128)S(1)} async-done(((f32[128,16,128]{2,1,0:T(8,128)}), f32[128,16,128]{2,1,0:T(8,128)S(1)}, u32[]{:S(2)}, u32[]{:S(2)}) %all-to-all-start) | async-done | bytes 1048608 | tf_op jit(solution)/shard_map/all_to_all | solution.py:478
  50.1 4.1 %strike_both.1 = (f32[2,8,16384]{2,1,0:T(8,128)}, f32[2048,128]{1,0:T(8,128)S(1)}) custom-call(f32[2048,128]{1,0:T(8,128)S(1)} %bitcast.8, f32[1024,128]{1,0:T(8,128)} %copy-done.11, f32[2,1024,128]{2,1,0:T(8,128)} %copy-done.10, bf16[4,128,128]{2,1,0:T(8,128)(2,1)} %constant.28.clone.wave_hbm, f32[2,128,128]{2,1,0:T(8,128)} %constant.29.clone.twist_hbm), custom_call_target="tpu_custom_call" | custom-call | flops 1600000000 | bytes 6000000 | tf_op jit(solution)/shard_map/strike_both/pallas_call | solution.py:303
  54.2 23.3 %all_to_all.10 = f32[128,16,128]{2,1,0:T(8,128)S(1)} all-to-all(f32[128,16,128]{2,1,0:T(8,128)S(1)} %bitcast.9), channel_id=1, replica_groups=mesh['strike'=32,'depth'=4] {'strike','depth'}, dimensions={0} | all-to-all | bytes 2097152 | tf_op jit(solution)/shard_map/all_to_all | solution.py:483
  77.5 0.0 copy-done.1
  77.5 1.0 depth_inverse.5
  78.5 0.0 copy-start.3
  78.5 0.0 copy-start.4
  78.5 0.0 copy-start.5
  78.5 0.0 copy-start.6
  78.5 0.0 copy-start.7
  78.5 1.3 %collective-permute-start.12 = (f32[128,128]{1,0:T(8,128)S(1)}, f32[128,128]{1,0:T(8,128)S(1)}, u32[]{:S(2)}, u32[]{:S(2)}) collective-permute-start(f32[128,128]{1,0:T(8,128)S(1)} %get-tuple-element.65), channel_id=1, source_target_pairs={{0,1},{1,0},{2,3},{3,2},{4,5},{5,4},{6,7},{7,6},{8,9},{9,8},{10,11... | collective-permute-start | bytes 196616 | tf_op jit(solution)/shard_map/ppermute | solution.py:451
  79.8 1.1 %depth_inverse.4 = (f32[128,256]{1,0:T(8,128)S(1)}, f32[128,256]{1,0:T(8,128)S(1)}, f32[128,256]{1,0:T(8,128)S(1)}, f32[128,256]{1,0:T(8,128)S(1)}) custom-call(s32[1]{0:T(128)} %bitcast.me_ref, f32[2048,128]{1,0:T(8,128)S(1)} %bitcast.6, bf16[4,512,512]{2,1,0:T(8,128)(2,1)S(1)} %get-tuple-element.44.high_ref, bf16[4,512,512]{2,1,0:T(8,128)(2,1)S(1)} %copy-done.1), custom_call_target="tpu_custom_call" | custom-call | flops 1200000000 | bytes 4000000 | tf_op jit(solution)/shard_map/depth_inverse/pallas_call | solution.py:201
  80.9 0.3 collective-permute-start.9
  81.2 0.7 collective-permute-start.10
  81.9 3.0 %collective-permute-start.11 = (f32[128,256]{1,0:T(8,128)S(1)}, f32[128,256]{1,0:T(8,128)S(1)}, u32[]{:S(2)}, u32[]{:S(2)}) collective-permute-start(f32[128,256]{1,0:T(8,128)S(1)} %get-tuple-element.63), channel_id=1, source_target_pairs={{0,3},{1,2},{2,1},{3,0},{4,7},{5,6},{6,5},{7,4},{8,11},{9,10},{10,... | collective-permute-start | bytes 393224 | tf_op jit(solution)/shard_map/ppermute | solution.py:451
  84.8 0.6 collective-permute-start.13
  85.4 0.0 collective-permute-done.12.one_ref
  85.4 2.4 %collective-permute-start.14 = (f32[128,128]{1,0:T(8,128)S(1)}, f32[128,128]{1,0:T(8,128)S(1)}, u32[]{:S(2)}, u32[]{:S(2)}) collective-permute-start(f32[128,128]{1,0:T(8,128)S(1)} %get-tuple-element.67), channel_id=1, source_target_pairs={{0,3},{1,2},{2,1},{3,0},{4,7},{5,6},{6,5},{7,4},{8,11},{9,10},{10,... | collective-permute-start | bytes 196616 | tf_op jit(solution)/shard_map/ppermute | solution.py:451
  87.8 1.0 depth_inverse.3
  88.8 2.6 %collective-permute-done.13.two_ref = f32[128,128]{1,0:T(8,128)S(1)} collective-permute-done((f32[128,128]{1,0:T(8,128)S(1)}, f32[128,128]{1,0:T(8,128)S(1)}, u32[]{:S(2)}, u32[]{:S(2)}) %collective-permute-start.13) | collective-permute-done | bytes 65568 | tf_op jit(solution)/shard_map/ppermute | solution.py:451
  91.4 2.2 %collective-permute-start.6 = (f32[128,128]{1,0:T(8,128)S(1)}, f32[128,128]{1,0:T(8,128)S(1)}, u32[]{:S(2)}, u32[]{:S(2)}) collective-permute-start(f32[128,128]{1,0:T(8,128)S(1)} %get-tuple-element.54), channel_id=1, source_target_pairs={{0,1},{1,0},{2,3},{3,2},{4,5},{5,4},{6,7},{7,6},{8,9},{9,8},{10,11... | collective-permute-start | bytes 196616 | tf_op jit(solution)/shard_map/ppermute | solution.py:451
  93.6 0.0 collective-permute-done.14.three_ref
  93.6 1.0 collective-permute-start.7
  94.7 0.0 collective-permute-done.9.one_ref
  94.7 2.1 %collective-permute-start.8 = (f32[128,128]{1,0:T(8,128)S(1)}, f32[128,128]{1,0:T(8,128)S(1)}, u32[]{:S(2)}, u32[]{:S(2)}) collective-permute-start(f32[128,128]{1,0:T(8,128)S(1)} %get-tuple-element.56), channel_id=1, source_target_pairs={{0,3},{1,2},{2,1},{3,0},{4,7},{5,6},{6,5},{7,4},{8,11},{9,10},{10,... | collective-permute-start | bytes 196616 | tf_op jit(solution)/shard_map/ppermute | solution.py:451
  96.8 0.0 copy-done.3
  96.8 0.0 copy-done.4
  96.8 0.0 copy-done.5
  96.8 1.2 %friction_start.1 = (f32[512,512]{1,0:T(8,128)S(1)}, f32[512,512]{1,0:T(8,128)S(1)}, f32[512,512]{1,0:T(8,128)S(1)}) custom-call(f32[512,512]{1,0:T(8,128)S(1)} %copy-done.5, f32[512,512]{1,0:T(8,128)S(1)} %copy-done.6, f32[512,512]{1,0:T(8,128)S(1)} %copy-done.7, f32[512,512]{1,0:T(8,128)S(1)} %copy-done.3, f32[512,512]{1,0:T(8,128)S(1)} %copy-done.4), custom_call_target="tpu_custom_call" | custom-call | flops 20000000 | bytes 8000000 | tf_op jit(solution)/shard_map/friction_start/pallas_call | solution.py:390
  98.0 0.0 copy-done.2
  98.0 1.4 %friction_finish.3 = (f32[512,512]{1,0:T(8,128)}, f32[512,512]{1,0:T(8,128)}) custom-call(s32[1]{0:T(128)} %bitcast.me_ref, f32[128,128]{1,0:T(8,128)S(1)} %get-tuple-element.64.own_ref, f32[128,128]{1,0:T(8,128)S(1)} %collective-permute-done.12.one_ref, f32[128,128]{1,0:T(8,128)S(1)} %collective-permute-done.13.two_ref, ...), custom_call_target="tpu_custom_call" | custom-call | flops 20000000 | bytes 5000000 | tf_op jit(solution)/shard_map/friction_finish/pallas_call | solution.py:433
  99.4 0.0 collective-permute-done.10.two_ref
  99.4 0.0 collective-permute-done.11.three_ref
  99.4 2.1 %friction_finish.4 = (f32[512,512]{1,0:T(8,128)}, f32[512,512]{1,0:T(8,128)}) custom-call(s32[1]{0:T(128)} %bitcast.me_ref, f32[128,256]{1,0:T(8,128)S(1)} %get-tuple-element.60.own_ref, f32[128,256]{1,0:T(8,128)S(1)} %collective-permute-done.9.one_ref, ...), custom_call_target="tpu_custom_call", output_to_operand_aliasing={{0}: (11, {}), {1}: (12, {})} | custom-call | flops 20000000 | bytes 5000000 | tf_op jit(solution)/shard_map/friction_finish/pallas_call | solution.py:433
  101.5 0.0 collective-permute-done.6.one_ref
  101.5 0.0 collective-permute-done.7.two_ref
  101.5 0.0 collective-permute-done.8.three_ref
  101.5 1.4 %friction_finish.5 = (f32[512,512]{1,0:T(8,128)}, f32[512,512]{1,0:T(8,128)}) custom-call(s32[1]{0:T(128)} %bitcast.me_ref, f32[128,128]{1,0:T(8,128)S(1)} %get-tuple-element.53.own_ref, f32[128,128]{1,0:T(8,128)S(1)} %collective-permute-done.6.one_ref, ...), custom_call_target="tpu_custom_call", output_to_operand_aliasing={{0}: (11, {}), {1}: (12, {})} | custom-call | flops 20000000 | bytes 5000000 | tf_op jit(solution)/shard_map/friction_finish/pallas_call | solution.py:433
  (7 shorter events, 0.0 us)
Async XLA Ops:
  1.9 12.4 %collective-permute-start.3 = (f32[128,384]{1,0:T(8,128)S(1)}, f32[128,384]{1,0:T(8,128)S(1)}, u32[]{:S(2)}, u32[]{:S(2)}) collective-permute-start(f32[128,384]{1,0:T(8,128)S(1)} %get-tuple-element.47), channel_id=1, source_target_pairs={{0,1},{1,0},{2,3},{3,2},{4,5},{5,4},{6,7},{7,6},{8,9},{9,8},{10,11... | collective-permute-start | bytes 589832 | tf_op jit(solution)/shard_map/ppermute | solution.py:451
  3.4 11.4 %collective-permute-start.4 = (f32[128,384]{1,0:T(8,128)S(1)}, f32[128,384]{1,0:T(8,128)S(1)}, u32[]{:S(2)}, u32[]{:S(2)}) collective-permute-start(f32[128,384]{1,0:T(8,128)S(1)} %get-tuple-element.48), channel_id=1, source_target_pairs={{0,2},{1,3},{2,0},{3,1},{4,6},{5,7},{6,4},{7,5},{8,10},{9,11},{10,... | collective-permute-start | bytes 589832 | tf_op jit(solution)/shard_map/ppermute | solution.py:451
  7.1 9.6 %collective-permute-start.5 = (f32[128,384]{1,0:T(8,128)S(1)}, f32[128,384]{1,0:T(8,128)S(1)}, u32[]{:S(2)}, u32[]{:S(2)}) collective-permute-start(f32[128,384]{1,0:T(8,128)S(1)} %get-tuple-element.49), channel_id=1, source_target_pairs={{0,3},{1,2},{2,1},{3,0},{4,7},{5,6},{6,5},{7,4},{8,11},{9,10},{10,... | collective-permute-start | bytes 589832 | tf_op jit(solution)/shard_map/ppermute | solution.py:451
  8.1 10.3 %collective-permute-start = (f32[128,128]{1,0:T(8,128)S(1)}, f32[128,128]{1,0:T(8,128)S(1)}, u32[]{:S(2)}, u32[]{:S(2)}) collective-permute-start(f32[128,128]{1,0:T(8,128)S(1)} %get-tuple-element.41), channel_id=1, source_target_pairs={{0,1},{1,0},{2,3},{3,2},{4,5},{5,4},{6,7},{7,6},{8,9},{9,8},{10,11... | collective-permute-start | bytes 196616 | tf_op jit(solution)/shard_map/ppermute | solution.py:451
  8.6 9.9 %collective-permute-start.1 = (f32[128,128]{1,0:T(8,128)S(1)}, f32[128,128]{1,0:T(8,128)S(1)}, u32[]{:S(2)}, u32[]{:S(2)}) collective-permute-start(f32[128,128]{1,0:T(8,128)S(1)} %get-tuple-element.42), channel_id=1, source_target_pairs={{0,2},{1,3},{2,0},{3,1},{4,6},{5,7},{6,4},{7,5},{8,10},{9,11},{10,... | collective-permute-start | bytes 196616 | tf_op jit(solution)/shard_map/ppermute | solution.py:451
  11.5 1.0 %copy-start.8 = (f32[2,128,512]{2,1,0:T(8,128)S(1)}, f32[2,128,512]{2,1,0:T(8,128)}, u32[]{:S(2)}) copy-start(f32[2,128,512]{2,1,0:T(8,128)} %constant.26.clone.coarse_ref) | copy-start | bytes 1572868
  12.6 0.8 copy-start.9
  14.4 8.2 %copy-start = (bf16[4,512,512]{2,1,0:T(8,128)(2,1)}, bf16[4,512,512]{2,1,0:T(8,128)(2,1)S(1)}, u32[]{:S(2)}) copy-start(bf16[4,512,512]{2,1,0:T(8,128)(2,1)S(1)} %get-tuple-element.45.low_ref) | copy-start | bytes 6291460
  14.4 6.2 %collective-permute-start.2 = (f32[128,128]{1,0:T(8,128)S(1)}, f32[128,128]{1,0:T(8,128)S(1)}, u32[]{:S(2)}, u32[]{:S(2)}) collective-permute-start(f32[128,128]{1,0:T(8,128)S(1)} %get-tuple-element.43), channel_id=1, source_target_pairs={{0,3},{1,2},{2,1},{3,0},{4,7},{5,6},{6,5},{7,4},{8,11},{9,10},{10,... | collective-permute-start | bytes 196616 | tf_op jit(solution)/shard_map/ppermute | solution.py:451
  22.6 27.5 %all-to-all-start = ((f32[128,16,128]{2,1,0:T(8,128)}), f32[128,16,128]{2,1,0:T(8,128)S(1)}, u32[]{:S(2)}, u32[]{:S(2)}) async-start(f32[128,16,128]{2,1,0:T(8,128)} %bitcast.1), calls=%async_computation | async-start | bytes 2097152 | tf_op jit(solution)/shard_map/all_to_all | solution.py:478
  37.7 1.0 copy-start.10
  38.7 0.8 copy-start.11
  50.1 27.4 %copy-start.1 = (bf16[4,512,512]{2,1,0:T(8,128)(2,1)S(1)}, bf16[4,512,512]{2,1,0:T(8,128)(2,1)}, u32[]{:S(2)}) copy-start(bf16[4,512,512]{2,1,0:T(8,128)(2,1)} %copy-done) | copy-start | bytes 6291460
  78.5 18.3 %copy-start.3 = (f32[512,512]{1,0:T(8,128)S(1)}, f32[512,512]{1,0:T(8,128)}, u32[]{:S(2)}) copy-start(f32[512,512]{1,0:T(8,128)} %strength_ref.7) | copy-start | bytes 3145732
  78.5 18.3 %copy-start.4 = (f32[512,512]{1,0:T(8,128)S(1)}, f32[512,512]{1,0:T(8,128)}, u32[]{:S(2)}) copy-start(f32[512,512]{1,0:T(8,128)} %stress_ref.7) | copy-start | bytes 3145732
  78.5 18.3 %copy-start.5 = (f32[512,512]{1,0:T(8,128)S(1)}, f32[512,512]{1,0:T(8,128)}, u32[]{:S(2)}) copy-start(f32[512,512]{1,0:T(8,128)} %rate_ref.1) | copy-start | bytes 3145732
  78.5 18.3 %copy-start.6 = (f32[512,512]{1,0:T(8,128)S(1)}, f32[512,512]{1,0:T(8,128)}, u32[]{:S(2)}) copy-start(f32[512,512]{1,0:T(8,128)} %state_ref.1) | copy-start | bytes 3145732
  78.5 18.3 %copy-start.7 = (f32[512,512]{1,0:T(8,128)S(1)}, f32[512,512]{1,0:T(8,128)}, u32[]{:S(2)}) copy-start(f32[512,512]{1,0:T(8,128)} %weak_ref.1) | copy-start | bytes 3145732
  78.5 6.9 %collective-permute-start.12 = (f32[128,128]{1,0:T(8,128)S(1)}, f32[128,128]{1,0:T(8,128)S(1)}, u32[]{:S(2)}, u32[]{:S(2)}) collective-permute-start(f32[128,128]{1,0:T(8,128)S(1)} %get-tuple-element.65), channel_id=1, source_target_pairs={{0,1},{1,0},{2,3},{3,2},{4,5},{5,4},{6,7},{7,6},{8,9},{9,8},{10,11... | collective-permute-start | bytes 196616 | tf_op jit(solution)/shard_map/ppermute | solution.py:451
  80.9 13.7 %collective-permute-start.9 = (f32[128,256]{1,0:T(8,128)S(1)}, f32[128,256]{1,0:T(8,128)S(1)}, u32[]{:S(2)}, u32[]{:S(2)}) collective-permute-start(f32[128,256]{1,0:T(8,128)S(1)} %get-tuple-element.61), channel_id=1, source_target_pairs={{0,1},{1,0},{2,3},{3,2},{4,5},{5,4},{6,7},{7,6},{8,9},{9,8},{10,11... | collective-permute-start | bytes 393224 | tf_op jit(solution)/shard_map/ppermute | solution.py:451
  81.2 18.2 %collective-permute-start.10 = (f32[128,256]{1,0:T(8,128)S(1)}, f32[128,256]{1,0:T(8,128)S(1)}, u32[]{:S(2)}, u32[]{:S(2)}) collective-permute-start(f32[128,256]{1,0:T(8,128)S(1)} %get-tuple-element.62), channel_id=1, source_target_pairs={{0,2},{1,3},{2,0},{3,1},{4,6},{5,7},{6,4},{7,5},{8,10},{9,11},{10,... | collective-permute-start | bytes 393224 | tf_op jit(solution)/shard_map/ppermute | solution.py:451
  81.9 17.5 %collective-permute-start.11 = (f32[128,256]{1,0:T(8,128)S(1)}, f32[128,256]{1,0:T(8,128)S(1)}, u32[]{:S(2)}, u32[]{:S(2)}) collective-permute-start(f32[128,256]{1,0:T(8,128)S(1)} %get-tuple-element.63), channel_id=1, source_target_pairs={{0,3},{1,2},{2,1},{3,0},{4,7},{5,6},{6,5},{7,4},{8,11},{9,10},{10,... | collective-permute-start | bytes 393224 | tf_op jit(solution)/shard_map/ppermute | solution.py:451
  84.8 6.5 %collective-permute-start.13 = (f32[128,128]{1,0:T(8,128)S(1)}, f32[128,128]{1,0:T(8,128)S(1)}, u32[]{:S(2)}, u32[]{:S(2)}) collective-permute-start(f32[128,128]{1,0:T(8,128)S(1)} %get-tuple-element.66), channel_id=1, source_target_pairs={{0,2},{1,3},{2,0},{3,1},{4,6},{5,7},{6,4},{7,5},{8,10},{9,11},{10,... | collective-permute-start | bytes 196616 | tf_op jit(solution)/shard_map/ppermute | solution.py:451
  85.4 12.5 %copy-start.2 = (f32[512,512]{1,0:T(8,128)S(1)}, f32[512,512]{1,0:T(8,128)}, u32[]{:S(2)}) copy-start(f32[512,512]{1,0:T(8,128)} %slip_ref.5) | copy-start | bytes 3145732
  85.4 8.2 %collective-permute-start.14 = (f32[128,128]{1,0:T(8,128)S(1)}, f32[128,128]{1,0:T(8,128)S(1)}, u32[]{:S(2)}, u32[]{:S(2)}) collective-permute-start(f32[128,128]{1,0:T(8,128)S(1)} %get-tuple-element.67), channel_id=1, source_target_pairs={{0,3},{1,2},{2,1},{3,0},{4,7},{5,6},{6,5},{7,4},{8,11},{9,10},{10,... | collective-permute-start | bytes 196616 | tf_op jit(solution)/shard_map/ppermute | solution.py:451
  91.4 10.1 %collective-permute-start.6 = (f32[128,128]{1,0:T(8,128)S(1)}, f32[128,128]{1,0:T(8,128)S(1)}, u32[]{:S(2)}, u32[]{:S(2)}) collective-permute-start(f32[128,128]{1,0:T(8,128)S(1)} %get-tuple-element.54), channel_id=1, source_target_pairs={{0,1},{1,0},{2,3},{3,2},{4,5},{5,4},{6,7},{7,6},{8,9},{9,8},{10,11... | collective-permute-start | bytes 196616 | tf_op jit(solution)/shard_map/ppermute | solution.py:451
  93.6 7.8 %collective-permute-start.7 = (f32[128,128]{1,0:T(8,128)S(1)}, f32[128,128]{1,0:T(8,128)S(1)}, u32[]{:S(2)}, u32[]{:S(2)}) collective-permute-start(f32[128,128]{1,0:T(8,128)S(1)} %get-tuple-element.55), channel_id=1, source_target_pairs={{0,2},{1,3},{2,0},{3,1},{4,6},{5,7},{6,4},{7,5},{8,10},{9,11},{10,... | collective-permute-start | bytes 196616 | tf_op jit(solution)/shard_map/ppermute | solution.py:451
  94.7 6.8 %collective-permute-start.8 = (f32[128,128]{1,0:T(8,128)S(1)}, f32[128,128]{1,0:T(8,128)S(1)}, u32[]{:S(2)}, u32[]{:S(2)}) collective-permute-start(f32[128,128]{1,0:T(8,128)S(1)} %get-tuple-element.56), channel_id=1, source_target_pairs={{0,3},{1,2},{2,1},{3,0},{4,7},{5,6},{6,5},{7,4},{8,11},{9,10},{10,... | collective-permute-start | bytes 196616 | tf_op jit(solution)/shard_map/ppermute | solution.py:451

commit v2 on v1

--- a/solution.py
+++ b/solution.py
@@ -15,8 +15,8 @@
 RELAXATION = 0.5
 ADVANCE = 0.5
 LAGS = 8
-FORWARD = ((0, 384), (384, 128))
-INVERSE = ((0, 128), (128, 256), (384, 128))
+FORWARD = ((0, 256), (256, 256))
+INVERSE = ((0, 256), (256, 256))
 GRANT = 16 << 20
 WIDE = 24 << 20
 ALL = ("strike", "depth")
@@ -219,11 +219,11 @@
 
 
 def strike_kernel(
-    x_ref, gain_hbm, past_hbm, wave_hbm, twist_hbm, modes_hbm, out_ref,
-    gain_ref, past_ref, wave_ref, twist_ref, held, modes_ref, sems,
+    x_ref, gain_hbm, past_hbm, wave_ref, twist_ref, modes_hbm, out_ref,
+    gain_ref, past_ref, held, modes_ref, sems,
 ):
     edge = twist_ref.shape[1]
-    pairs = ((wave_hbm, wave_ref), (twist_hbm, twist_ref), (gain_hbm, gain_ref), (past_hbm, past_ref))
+    pairs = ((gain_hbm, gain_ref), (past_hbm, past_ref))
     loads = [pltpu.make_async_copy(a, b, sems.at[n]) for n, (a, b) in enumerate(pairs)]
     for load in loads:
         load.start()
@@ -235,7 +235,6 @@
         )
 
     parts = split(jnp.concatenate([gather(x_ref, m) for m in range(8)], axis=1))
-    loads[0].wait()
 
     def block(sign, part):
         cosine, sine = wave_ref[part], wave_ref[2 + part]
@@ -247,7 +246,6 @@
     forward = (block(1, 0), block(1, 1))
     backward = (block(-1, 0), block(-1, 1))
     first = dot3(forward, parts, NN)
-    loads[1].wait()
     cosine, sine = twist_ref[0], twist_ref[1]
     turned = []
     for m in range(8):
@@ -262,10 +260,10 @@
             held[plane, pl.ds(m, edge, stride=8), :] = lanes(modes, m)[plane * edge : (plane + 1) * edge]
         for k in range(edge):
             modes_ref[plane, :, k * edge : (k + 1) * edge] = held[plane, k * 8 : (k + 1) * 8, :]
-    save = pltpu.make_async_copy(modes_ref, modes_hbm, sems.at[4])
+    save = pltpu.make_async_copy(modes_ref, modes_hbm, sems.at[2])
     save.start()
-    loads[2].wait()
-    loads[3].wait()
+    for load in loads:
+        load.wait()
     spectrum = []
     for m in range(8):
         part = lanes(modes, m)
@@ -306,21 +304,19 @@
             jax.ShapeDtypeStruct(modes, F32),
             jax.ShapeDtypeStruct((edge * 16, edge), F32),
         ),
-        in_specs=[VMEM] + [HBM] * 4,
+        in_specs=[VMEM, HBM, HBM, VMEM, VMEM],
         out_specs=(HBM, VMEM),
         scratch_shapes=[
             pltpu.VMEM(gain.shape, F32),
             pltpu.VMEM(past.shape, F32),
-            pltpu.VMEM(waves.shape, BF16),
-            pltpu.VMEM(twist.shape, F32),
             pltpu.VMEM((2, edge * 8, edge), F32),
             pltpu.VMEM(modes, F32),
-            pltpu.SemaphoreType.DMA((5,)),
+            pltpu.SemaphoreType.DMA((3,)),
         ],
         compiler_params=pltpu.CompilerParams(vmem_limit_bytes=WIDE),
         name="strike_both",
         cost_estimate=pl.CostEstimate(flops=1_600_000_000, bytes_accessed=6_000_000, transcendentals=0),
-    )(pencil, *in_hbm(gain, past, waves, twist))
+    )(pencil, *in_hbm(gain, past), waves, twist)
 
 
 def past_kernel(kernel_ref, history_ref, gain_ref, past_ref):

time: 103 us -> 98.2 us (0.953)
  starting transfers between devices: 30.9 us -> 26.6 us
  Pallas kernels: 24.7 us -> 23.1 us
    ppermute x15 -> x12, starting transfers between devices: 22.6 us -> 17.4 us  [exchange(): lax.ppermute(part, 'depth', [(place, place ^ k) for place in range(size)])]
    pallas_call x3 -> x2, Pallas kernels: 3.07 us -> 2.23 us  [depth_inverse(): pl.pallas_call(functools.partial(depth_inverse_kernel, column), out_shape...]
    ppermute x15 -> x12, waiting for transfers between devices: 6.68 us -> 7.43 us  [exchange(): lax.ppermute(part, 'depth', [(place, place ^ k) for place in range(size)])]
    pallas_call x3 -> x2, Pallas kernels: 4.83 us -> 4.08 us  [friction_finish(): pl.pallas_call(functools.partial(friction_kernel, column), in_specs=[SMEM...]
    unnamed x24 -> x28, local copies, waits for them, and re-layouts: 3.61 us -> 3.61 us
  transfers between devices with their start and end apart: 16 -> 13, of which waited for: 4 -> 6; matrix products, arithmetic and copies ran while one was open for 1% -> 1% of each run, Pallas kernels for 16% -> 13%
where the time goes in v2:
time: 98.2 us; the launch traced here: 97.8 us
  starting transfers between devices  26.6 us (27%)
  blocking collectives  23.3 us (24%)
  Pallas kernels  23.1 us (24%)
  waiting for transfers between devices  17.9 us (18%)
  local copies, waits for them, and re-layouts  5.88 us (6%)
  between operations  1.01 us (1%)
    all_to_all x1, blocking collectives, body(): lax.all_to_all(waves.reshape(devices, 16, edge), ALL, 0, 0)  23.3 us
    ppermute x12, starting transfers between devices, exchange(): lax.ppermute(part, 'depth', [(place, place ^ k) for place in range(size)])  17.4 us
    all_to_all x1, waiting for transfers between devices, body(): pencil = lax.all_to_all(waves.reshape(devices, 16, edge), ALL, 0, 0)  10.5 us
    all_to_all x1, starting transfers between devices, body(): pencil = lax.all_to_all(waves.reshape(devices, 16, edge), ALL, 0, 0)  9.17 us
    ppermute x12, waiting for transfers between devices, exchange(): lax.ppermute(part, 'depth', [(place, place ^ k) for place in range(size)])  7.43 us
    pallas_call x1, Pallas kernels, past_sum(): pl.pallas_call(past_kernel, grid=(length // block,), out_shape=(jax.Shape...  6.84 us
    pallas_call x1, Pallas kernels, strike_both(): pl.pallas_call(strike_kernel, out_shape=(jax.ShapeDtypeStruct(modes, F32)...  4.59 us
    pallas_call x2, Pallas kernels, friction_finish(): pl.pallas_call(functools.partial(friction_kernel, column), in_specs=[SMEM...  4.08 us
  transfers between devices with their start and end apart: 13, of which 6 were waited for; matrix products, arithmetic and copies ran while one was open for 1% of the time, Pallas kernels for 13%

profile of v2, /device:TPU:1, one launch (start us, length us, event | category | flops | bytes accessed | tf_op | source)
XLA Modules:
  0.0 97.8 jit_solution(1233509129960258284)
XLA Ops:
  0.7 1.1 %constant_dynamic-slice_fusion.4 = (f32[128,256]{1,0:T(8,128)S(1)}, f32[128,256]{1,0:T(8,128)S(1)}, f32[128,256]{1,0:T(8,128)S(1)}, f32[128,256]{1,0:T(8,128)S(1)}) fusion(f32[512,512]{1,0:T(8,128)} %slip_ref.3, s32[]{:T(128)S(6)} %select_n.19, s32[]{:T(128)S(6)} %select_n.18, s32[]{:T(128)S(6)} %select_n.17, s32[]{:T(128)S(6)} %select_n.16), kind=kLoop, calls=%fused_computation.4 | loop fusion | bytes 1048592 | tf_op jit(solution)/shard_map/dynamic_slice | solution.py:463
  1.8 1.5 %collective-permute-start.3 = (f32[128,256]{1,0:T(8,128)S(1)}, f32[128,256]{1,0:T(8,128)S(1)}, u32[]{:S(2)}, u32[]{:S(2)}) collective-permute-start(f32[128,256]{1,0:T(8,128)S(1)} %get-tuple-element.41), channel_id=1, source_target_pairs={{0,1},{1,0},{2,3},{3,2},{4,5},{5,4},{6,7},{7,6},{8,9},{9,8},{10,11... | collective-permute-start | bytes 393224 | tf_op jit(solution)/shard_map/ppermute | solution.py:447
  3.3 3.7 %collective-permute-start.4 = (f32[128,256]{1,0:T(8,128)S(1)}, f32[128,256]{1,0:T(8,128)S(1)}, u32[]{:S(2)}, u32[]{:S(2)}) collective-permute-start(f32[128,256]{1,0:T(8,128)S(1)} %get-tuple-element.42), channel_id=1, source_target_pairs={{0,2},{1,3},{2,0},{3,1},{4,6},{5,7},{6,4},{7,5},{8,10},{9,11},{10,... | collective-permute-start | bytes 393224 | tf_op jit(solution)/shard_map/ppermute | solution.py:447
  7.0 0.1 collective-permute-start.5
  7.0 1.1 %constant_dynamic-slice_fusion = (f32[128,256]{1,0:T(8,128)S(1)}, f32[128,256]{1,0:T(8,128)S(1)}, f32[128,256]{1,0:T(8,128)S(1)}, f32[128,256]{1,0:T(8,128)S(1)}) fusion(f32[512,512]{1,0:T(8,128)} %slip_ref.3, s32[]{:T(128)S(6)} %select_n.19, s32[]{:T(128)S(6)} %select_n.18, s32[]{:T(128)S(6)} %select_n.17, s32[]{:T(128)S(6)} %select_n.16), kind=kLoop, calls=%fused_computation | loop fusion | bytes 1048592 | tf_op jit(solution)/shard_map/dynamic_slice | solution.py:463
  8.2 0.4 collective-permute-start
  8.6 3.0 %collective-permute-start.1 = (f32[128,256]{1,0:T(8,128)S(1)}, f32[128,256]{1,0:T(8,128)S(1)}, u32[]{:S(2)}, u32[]{:S(2)}) collective-permute-start(f32[128,256]{1,0:T(8,128)S(1)} %get-tuple-element.36), channel_id=1, source_target_pairs={{0,2},{1,3},{2,0},{3,1},{4,6},{5,7},{6,4},{7,5},{8,10},{9,11},{10,... | collective-permute-start | bytes 393224 | tf_op jit(solution)/shard_map/ppermute | solution.py:447
  11.6 0.0 collective-permute-done.3.one_ref
  11.6 0.4 collective-permute-start.2
  11.9 0.0 copy-start.8
  11.9 1.0 %copy-done.8 = f32[2,128,512]{2,1,0:T(8,128)S(1)} copy-done((f32[2,128,512]{2,1,0:T(8,128)S(1)}, f32[2,128,512]{2,1,0:T(8,128)}, u32[]{:S(2)}) %copy-start.8) | copy-done | bytes 524312
  13.0 0.0 copy-start.9
  13.0 0.8 copy-done.9
  13.7 1.0 %depth_tables.1 = (bf16[4,512,512]{2,1,0:T(8,128)(2,1)S(1)}, bf16[4,512,512]{2,1,0:T(8,128)(2,1)S(1)}) custom-call(f32[2,128,512]{2,1,0:T(8,128)S(1)} %copy-done.8, f32[2,8,512]{2,1,0:T(8,128)S(1)} %copy-done.9), custom_call_target="tpu_custom_call" | custom-call | flops 10000000 | bytes 5000000 | tf_op jit(solution)/shard_map/depth_tables/pallas_call | solution.py:82
  14.7 0.0 copy-start
  14.8 0.0 collective-permute-done.4.two_ref
  14.8 0.0 collective-permute-done.5.three_ref
  14.8 1.0 %depth_forward.2.refs_0_ = f32[16,128,128]{2,1,0:T(8,128)S(1)} custom-call(s32[1]{0:T(128)} %bitcast.me_ref, f32[128,256]{1,0:T(8,128)S(1)} %get-tuple-element.40.own_ref, f32[128,256]{1,0:T(8,128)S(1)} %collective-permute-done.3.one_ref, f32[128,256]{1,0:T(8,128)S(1)} %collective-permute-done.4.two_ref, f32[128,256]{1,0:T(8,128)S(1)} %collective-permute-done.5.three_ref, ...), custom_call_target="tpu_custom_call" | custom-call | flops 1200000000 | bytes 4000000 | tf_op jit(solution)/shard_map/depth_forward/pallas_call | solution.py:137
  15.8 0.0 collective-permute-done.one_ref
  15.8 0.9 collective-permute-done.1.two_ref
  16.7 2.8 %collective-permute-done.2.three_ref = f32[128,256]{1,0:T(8,128)S(1)} collective-permute-done((f32[128,256]{1,0:T(8,128)S(1)}, f32[128,256]{1,0:T(8,128)S(1)}, u32[]{:S(2)}, u32[]{:S(2)}) %collective-permute-start.2) | collective-permute-done | bytes 131104 | tf_op jit(solution)/shard_map/ppermute | solution.py:447
  19.6 2.2 %depth_forward.3 = f32[2048,128]{1,0:T(8,128)} custom-call(s32[1]{0:T(128)} %bitcast.me_ref, f32[128,256]{1,0:T(8,128)S(1)} %get-tuple-element.34.own_ref, f32[128,256]{1,0:T(8,128)S(1)} %collective-permute-done.one_ref, f32[128,256]{1,0:T(8,128)S(1)} %collective-permute-done.1.two_ref, f32[128,256]{1,0:T(8,128)S(1)} %collective-permute-done.2.three_ref, ...), custom_call_target="tpu_custom_call" | custom-call | flops 1200000000 | bytes 4000000 | tf_op jit(solution)/shard_map/depth_forward/pallas_call | solution.py:137
  21.8 0.0 copy-done
  21.8 9.2 %all-to-all-start = ((f32[128,16,128]{2,1,0:T(8,128)}), f32[128,16,128]{2,1,0:T(8,128)S(1)}, u32[]{:S(2)}, u32[]{:S(2)}) async-start(f32[128,16,128]{2,1,0:T(8,128)} %bitcast.1), calls=%async_computation | async-start | bytes 2097152 | tf_op jit(solution)/shard_map/all_to_all | solution.py:474
  30.9 0.0 copy-start.12
  31.0 0.0 copy-start.13
  31.0 6.8 %past_sum.1 = (f32[1024,128]{1,0:T(8,128)S(1)}, f32[2,1024,128]{2,1,0:T(8,128)S(1)}) custom-call(f32[9,8,16384]{2,1,0:T(8,128)} %kernel_ref.1, f32[8,2,8,16384]{3,2,1,0:T(8,128)} %history_ref.1), custom_call_target="tpu_custom_call" | custom-call | flops 4200000 | bytes 14700000 | tf_op jit(solution)/shard_map/past_sum/pallas_call | solution.py:338
  37.8 0.0 copy-start.10
  37.8 1.0 copy-done.10
  38.8 0.0 copy-start.11
  38.8 0.8 copy-done.11
  39.6 10.5 %all-to-all-done = f32[128,16,128]{2,1,0:T(8,128)S(1)} async-done(((f32[128,16,128]{2,1,0:T(8,128)}), f32[128,16,128]{2,1,0:T(8,128)S(1)}, u32[]{:S(2)}, u32[]{:S(2)}) %all-to-all-start) | async-done | bytes 1048608 | tf_op jit(solution)/shard_map/all_to_all | solution.py:474
  50.1 0.0 copy-start.1
  50.1 0.0 copy-done.12
  50.1 0.0 copy-done.13
  50.1 4.6 %strike_both.1 = (f32[2,8,16384]{2,1,0:T(8,128)}, f32[2048,128]{1,0:T(8,128)S(1)}) custom-call(f32[2048,128]{1,0:T(8,128)S(1)} %bitcast.7, f32[1024,128]{1,0:T(8,128)} %copy-done.11, f32[2,1024,128]{2,1,0:T(8,128)} %copy-done.10, bf16[4,128,128]{2,1,0:T(8,128)(2,1)S(1)} %copy-done.12, f32[2,128,128]{2,1,0:T(8,128)S(1)} %copy-done.13), custom_call_target="tpu_custom_call" | custom-call | flops 1600000000 | bytes 6000000 | tf_op jit(solution)/shard_map/strike_both/pallas_call | solution.py:301
  54.7 23.3 %all_to_all.10 = f32[128,16,128]{2,1,0:T(8,128)S(1)} all-to-all(f32[128,16,128]{2,1,0:T(8,128)S(1)} %bitcast.8), channel_id=1, replica_groups=mesh['strike'=32,'depth'=4] {'strike','depth'}, dimensions={0} | all-to-all | bytes 2097152 | tf_op jit(solution)/shard_map/all_to_all | solution.py:479
  78.0 0.0 copy-done.1
  78.0 0.0 copy-start.3
  78.0 0.0 copy-start.6
  78.0 0.0 copy-start.7
  78.0 1.1 %depth_inverse.3 = (f32[128,256]{1,0:T(8,128)S(1)}, f32[128,256]{1,0:T(8,128)S(1)}, f32[128,256]{1,0:T(8,128)S(1)}, f32[128,256]{1,0:T(8,128)S(1)}) custom-call(s32[1]{0:T(128)} %bitcast.me_ref, f32[2048,128]{1,0:T(8,128)S(1)} %bitcast.5, bf16[4,512,512]{2,1,0:T(8,128)(2,1)S(1)} %get-tuple-element.38.high_ref, bf16[4,512,512]{2,1,0:T(8,128)(2,1)S(1)} %copy-done.1), custom_call_target="tpu_custom_call" | custom-call | flops 1200000000 | bytes 4000000 | tf_op jit(solution)/shard_map/depth_inverse/pallas_call | solution.py:201
  79.2 1.3 %collective-permute-start.9 = (f32[128,256]{1,0:T(8,128)S(1)}, f32[128,256]{1,0:T(8,128)S(1)}, u32[]{:S(2)}, u32[]{:S(2)}) collective-permute-start(f32[128,256]{1,0:T(8,128)S(1)} %get-tuple-element.55), channel_id=1, source_target_pairs={{0,1},{1,0},{2,3},{3,2},{4,5},{5,4},{6,7},{7,6},{8,9},{9,8},{10,11... | collective-permute-start | bytes 393224 | tf_op jit(solution)/shard_map/ppermute | solution.py:447
  80.4 0.6 collective-permute-start.10
  81.0 2.6 %collective-permute-start.11 = (f32[128,256]{1,0:T(8,128)S(1)}, f32[128,256]{1,0:T(8,128)S(1)}, u32[]{:S(2)}, u32[]{:S(2)}) collective-permute-start(f32[128,256]{1,0:T(8,128)S(1)} %get-tuple-element.57), channel_id=1, source_target_pairs={{0,3},{1,2},{2,1},{3,0},{4,7},{5,6},{6,5},{7,4},{8,11},{9,10},{10,... | collective-permute-start | bytes 393224 | tf_op jit(solution)/shard_map/ppermute | solution.py:447
  83.7 1.1 %depth_inverse.2 = (f32[128,256]{1,0:T(8,128)S(1)}, f32[128,256]{1,0:T(8,128)S(1)}, f32[128,256]{1,0:T(8,128)S(1)}, f32[128,256]{1,0:T(8,128)S(1)}) custom-call(s32[1]{0:T(128)} %bitcast.me_ref, f32[2048,128]{1,0:T(8,128)S(1)} %bitcast.6, bf16[4,512,512]{2,1,0:T(8,128)(2,1)S(1)} %get-tuple-element.38.high_ref, bf16[4,512,512]{2,1,0:T(8,128)(2,1)S(1)} %copy-done.1), custom_call_target="tpu_custom_call" | custom-call | flops 1200000000 | bytes 4000000 | tf_op jit(solution)/shard_map/depth_inverse/pallas_call | solution.py:201
  84.8 0.4 collective-permute-start.6
  85.2 0.6 collective-permute-start.7
  85.8 0.0 collective-permute-done.9.one_ref
  85.8 2.9 %collective-permute-start.8 = (f32[128,256]{1,0:T(8,128)S(1)}, f32[128,256]{1,0:T(8,128)S(1)}, u32[]{:S(2)}, u32[]{:S(2)}) collective-permute-start(f32[128,256]{1,0:T(8,128)S(1)} %get-tuple-element.50), channel_id=1, source_target_pairs={{0,3},{1,2},{2,1},{3,0},{4,7},{5,6},{6,5},{7,4},{8,11},{9,10},{10,... | collective-permute-start | bytes 393224 | tf_op jit(solution)/shard_map/ppermute | solution.py:447
  88.7 0.0 copy-done.3
  88.7 0.0 copy-done.4
  88.7 0.0 copy-done.5
  88.7 0.0 copy-done.6
  88.7 0.0 copy-done.7
  88.7 1.2 %friction_start.1 = (f32[512,512]{1,0:T(8,128)S(1)}, f32[512,512]{1,0:T(8,128)S(1)}, f32[512,512]{1,0:T(8,128)S(1)}) custom-call(f32[512,512]{1,0:T(8,128)S(1)} %copy-done.5, f32[512,512]{1,0:T(8,128)S(1)} %copy-done.6, f32[512,512]{1,0:T(8,128)S(1)} %copy-done.7, f32[512,512]{1,0:T(8,128)S(1)} %copy-done.3, f32[512,512]{1,0:T(8,128)S(1)} %copy-done.4), custom_call_target="tpu_custom_call" | custom-call | flops 20000000 | bytes 8000000 | tf_op jit(solution)/shard_map/friction_start/pallas_call | solution.py:386
  89.9 0.0 collective-permute-done.10.two_ref
  89.9 0.6 collective-permute-done.11.three_ref
  90.5 0.0 copy-done.2
  90.5 2.0 %friction_finish.2 = (f32[512,512]{1,0:T(8,128)}, f32[512,512]{1,0:T(8,128)}) custom-call(s32[1]{0:T(128)} %bitcast.me_ref, f32[128,256]{1,0:T(8,128)S(1)} %get-tuple-element.54.own_ref, f32[128,256]{1,0:T(8,128)S(1)} %collective-permute-done.9.one_ref, f32[128,256]{1,0:T(8,128)S(1)} %collective-permute-done.10.two_ref, ...), custom_call_target="tpu_custom_call" | custom-call | flops 20000000 | bytes 5000000 | tf_op jit(solution)/shard_map/friction_finish/pallas_call | solution.py:429
  92.5 0.0 collective-permute-done.6.one_ref
  92.5 0.1 collective-permute-done.7.two_ref
  92.6 3.0 %collective-permute-done.8.three_ref = f32[128,256]{1,0:T(8,128)S(1)} collective-permute-done((f32[128,256]{1,0:T(8,128)S(1)}, f32[128,256]{1,0:T(8,128)S(1)}, u32[]{:S(2)}, u32[]{:S(2)}) %collective-permute-start.8) | collective-permute-done | bytes 131104 | tf_op jit(solution)/shard_map/ppermute | solution.py:447
  95.6 2.0 %friction_finish.3 = (f32[512,512]{1,0:T(8,128)}, f32[512,512]{1,0:T(8,128)}) custom-call(s32[1]{0:T(128)} %bitcast.me_ref, f32[128,256]{1,0:T(8,128)S(1)} %get-tuple-element.47.own_ref, f32[128,256]{1,0:T(8,128)S(1)} %collective-permute-done.6.one_ref, ...), custom_call_target="tpu_custom_call", output_to_operand_aliasing={{0}: (11, {}), {1}: (12, {})} | custom-call | flops 20000000 | bytes 5000000 | tf_op jit(solution)/shard_map/friction_finish/pallas_call | solution.py:429
  (3 shorter events, 0.0 us)
Async XLA Ops:
  1.8 9.8 %collective-permute-start.3 = (f32[128,256]{1,0:T(8,128)S(1)}, f32[128,256]{1,0:T(8,128)S(1)}, u32[]{:S(2)}, u32[]{:S(2)}) collective-permute-start(f32[128,256]{1,0:T(8,128)S(1)} %get-tuple-element.41), channel_id=1, source_target_pairs={{0,1},{1,0},{2,3},{3,2},{4,5},{5,4},{6,7},{7,6},{8,9},{9,8},{10,11... | collective-permute-start | bytes 393224 | tf_op jit(solution)/shard_map/ppermute | solution.py:447
  3.3 11.5 %collective-permute-start.4 = (f32[128,256]{1,0:T(8,128)S(1)}, f32[128,256]{1,0:T(8,128)S(1)}, u32[]{:S(2)}, u32[]{:S(2)}) collective-permute-start(f32[128,256]{1,0:T(8,128)S(1)} %get-tuple-element.42), channel_id=1, source_target_pairs={{0,2},{1,3},{2,0},{3,1},{4,6},{5,7},{6,4},{7,5},{8,10},{9,11},{10,... | collective-permute-start | bytes 393224 | tf_op jit(solution)/shard_map/ppermute | solution.py:447
  7.0 7.8 %collective-permute-start.5 = (f32[128,256]{1,0:T(8,128)S(1)}, f32[128,256]{1,0:T(8,128)S(1)}, u32[]{:S(2)}, u32[]{:S(2)}) collective-permute-start(f32[128,256]{1,0:T(8,128)S(1)} %get-tuple-element.43), channel_id=1, source_target_pairs={{0,3},{1,2},{2,1},{3,0},{4,7},{5,6},{6,5},{7,4},{8,11},{9,10},{10,... | collective-permute-start | bytes 393224 | tf_op jit(solution)/shard_map/ppermute | solution.py:447
  8.2 7.6 %collective-permute-start = (f32[128,256]{1,0:T(8,128)S(1)}, f32[128,256]{1,0:T(8,128)S(1)}, u32[]{:S(2)}, u32[]{:S(2)}) collective-permute-start(f32[128,256]{1,0:T(8,128)S(1)} %get-tuple-element.35), channel_id=1, source_target_pairs={{0,1},{1,0},{2,3},{3,2},{4,5},{5,4},{6,7},{7,6},{8,9},{9,8},{10,11... | collective-permute-start | bytes 393224 | tf_op jit(solution)/shard_map/ppermute | solution.py:447
  8.6 8.1 %collective-permute-start.1 = (f32[128,256]{1,0:T(8,128)S(1)}, f32[128,256]{1,0:T(8,128)S(1)}, u32[]{:S(2)}, u32[]{:S(2)}) collective-permute-start(f32[128,256]{1,0:T(8,128)S(1)} %get-tuple-element.36), channel_id=1, source_target_pairs={{0,2},{1,3},{2,0},{3,1},{4,6},{5,7},{6,4},{7,5},{8,10},{9,11},{10,... | collective-permute-start | bytes 393224 | tf_op jit(solution)/shard_map/ppermute | solution.py:447
  11.6 8.0 %collective-permute-start.2 = (f32[128,256]{1,0:T(8,128)S(1)}, f32[128,256]{1,0:T(8,128)S(1)}, u32[]{:S(2)}, u32[]{:S(2)}) collective-permute-start(f32[128,256]{1,0:T(8,128)S(1)} %get-tuple-element.37), channel_id=1, source_target_pairs={{0,3},{1,2},{2,1},{3,0},{4,7},{5,6},{6,5},{7,4},{8,11},{9,10},{10,... | collective-permute-start | bytes 393224 | tf_op jit(solution)/shard_map/ppermute | solution.py:447
  11.9 1.0 %copy-start.8 = (f32[2,128,512]{2,1,0:T(8,128)S(1)}, f32[2,128,512]{2,1,0:T(8,128)}, u32[]{:S(2)}) copy-start(f32[2,128,512]{2,1,0:T(8,128)} %constant.26.clone.coarse_ref) | copy-start | bytes 1572868
  13.0 0.8 copy-start.9
  14.7 7.0 %copy-start = (bf16[4,512,512]{2,1,0:T(8,128)(2,1)}, bf16[4,512,512]{2,1,0:T(8,128)(2,1)S(1)}, u32[]{:S(2)}) copy-start(bf16[4,512,512]{2,1,0:T(8,128)(2,1)S(1)} %get-tuple-element.39.low_ref) | copy-start | bytes 6291460
  21.8 28.3 %all-to-all-start = ((f32[128,16,128]{2,1,0:T(8,128)}), f32[128,16,128]{2,1,0:T(8,128)S(1)}, u32[]{:S(2)}, u32[]{:S(2)}) async-start(f32[128,16,128]{2,1,0:T(8,128)} %bitcast.1), calls=%async_computation | async-start | bytes 2097152 | tf_op jit(solution)/shard_map/all_to_all | solution.py:474
  30.9 19.2 %copy-start.12 = (bf16[4,128,128]{2,1,0:T(8,128)(2,1)S(1)}, bf16[4,128,128]{2,1,0:T(8,128)(2,1)}, u32[]{:S(2)}) copy-start(bf16[4,128,128]{2,1,0:T(8,128)(2,1)} %constant.28.clone.wave_ref) | copy-start | bytes 393220
  31.0 19.2 %copy-start.13 = (f32[2,128,128]{2,1,0:T(8,128)S(1)}, f32[2,128,128]{2,1,0:T(8,128)}, u32[]{:S(2)}) copy-start(f32[2,128,128]{2,1,0:T(8,128)} %constant.29.clone.twist_ref) | copy-start | bytes 393220
  37.8 1.0 copy-start.10
  38.8 0.8 copy-start.11
  50.1 27.9 %copy-start.1 = (bf16[4,512,512]{2,1,0:T(8,128)(2,1)S(1)}, bf16[4,512,512]{2,1,0:T(8,128)(2,1)}, u32[]{:S(2)}) copy-start(bf16[4,512,512]{2,1,0:T(8,128)(2,1)} %copy-done) | copy-start | bytes 6291460
  78.0 10.7 %copy-start.3 = (f32[512,512]{1,0:T(8,128)S(1)}, f32[512,512]{1,0:T(8,128)}, u32[]{:S(2)}) copy-start(f32[512,512]{1,0:T(8,128)} %strength_ref.5) | copy-start | bytes 3145732
  78.0 10.7 %copy-start.4 = (f32[512,512]{1,0:T(8,128)S(1)}, f32[512,512]{1,0:T(8,128)}, u32[]{:S(2)}) copy-start(f32[512,512]{1,0:T(8,128)} %stress_ref.5) | copy-start | bytes 3145732
  78.0 10.7 %copy-start.5 = (f32[512,512]{1,0:T(8,128)S(1)}, f32[512,512]{1,0:T(8,128)}, u32[]{:S(2)}) copy-start(f32[512,512]{1,0:T(8,128)} %rate_ref.1) | copy-start | bytes 3145732
  78.0 10.7 %copy-start.6 = (f32[512,512]{1,0:T(8,128)S(1)}, f32[512,512]{1,0:T(8,128)}, u32[]{:S(2)}) copy-start(f32[512,512]{1,0:T(8,128)} %state_ref.1) | copy-start | bytes 3145732
  78.0 10.7 %copy-start.7 = (f32[512,512]{1,0:T(8,128)S(1)}, f32[512,512]{1,0:T(8,128)}, u32[]{:S(2)}) copy-start(f32[512,512]{1,0:T(8,128)} %weak_ref.1) | copy-start | bytes 3145732
  79.2 6.6 %collective-permute-start.9 = (f32[128,256]{1,0:T(8,128)S(1)}, f32[128,256]{1,0:T(8,128)S(1)}, u32[]{:S(2)}, u32[]{:S(2)}) collective-permute-start(f32[128,256]{1,0:T(8,128)S(1)} %get-tuple-element.55), channel_id=1, source_target_pairs={{0,1},{1,0},{2,3},{3,2},{4,5},{5,4},{6,7},{7,6},{8,9},{9,8},{10,11... | collective-permute-start | bytes 393224 | tf_op jit(solution)/shard_map/ppermute | solution.py:447
  80.4 9.5 %collective-permute-start.10 = (f32[128,256]{1,0:T(8,128)S(1)}, f32[128,256]{1,0:T(8,128)S(1)}, u32[]{:S(2)}, u32[]{:S(2)}) collective-permute-start(f32[128,256]{1,0:T(8,128)S(1)} %get-tuple-element.56), channel_id=1, source_target_pairs={{0,2},{1,3},{2,0},{3,1},{4,6},{5,7},{6,4},{7,5},{8,10},{9,11},{10,... | collective-permute-start | bytes 393224 | tf_op jit(solution)/shard_map/ppermute | solution.py:447
  81.0 9.4 %copy-start.2 = (f32[512,512]{1,0:T(8,128)S(1)}, f32[512,512]{1,0:T(8,128)}, u32[]{:S(2)}) copy-start(f32[512,512]{1,0:T(8,128)} %slip_ref.3) | copy-start | bytes 3145732
  81.0 9.4 %collective-permute-start.11 = (f32[128,256]{1,0:T(8,128)S(1)}, f32[128,256]{1,0:T(8,128)S(1)}, u32[]{:S(2)}, u32[]{:S(2)}) collective-permute-start(f32[128,256]{1,0:T(8,128)S(1)} %get-tuple-element.57), channel_id=1, source_target_pairs={{0,3},{1,2},{2,1},{3,0},{4,7},{5,6},{6,5},{7,4},{8,11},{9,10},{10,... | collective-permute-start | bytes 393224 | tf_op jit(solution)/shard_map/ppermute | solution.py:447
  84.8 7.7 %collective-permute-start.6 = (f32[128,256]{1,0:T(8,128)S(1)}, f32[128,256]{1,0:T(8,128)S(1)}, u32[]{:S(2)}, u32[]{:S(2)}) collective-permute-start(f32[128,256]{1,0:T(8,128)S(1)} %get-tuple-element.48), channel_id=1, source_target_pairs={{0,1},{1,0},{2,3},{3,2},{4,5},{5,4},{6,7},{7,6},{8,9},{9,8},{10,11... | collective-permute-start | bytes 393224 | tf_op jit(solution)/shard_map/ppermute | solution.py:447
  85.2 7.4 %collective-permute-start.7 = (f32[128,256]{1,0:T(8,128)S(1)}, f32[128,256]{1,0:T(8,128)S(1)}, u32[]{:S(2)}, u32[]{:S(2)}) collective-permute-start(f32[128,256]{1,0:T(8,128)S(1)} %get-tuple-element.49), channel_id=1, source_target_pairs={{0,2},{1,3},{2,0},{3,1},{4,6},{5,7},{6,4},{7,5},{8,10},{9,11},{10,... | collective-permute-start | bytes 393224 | tf_op jit(solution)/shard_map/ppermute | solution.py:447
  85.8 9.8 %collective-permute-start.8 = (f32[128,256]{1,0:T(8,128)S(1)}, f32[128,256]{1,0:T(8,128)S(1)}, u32[]{:S(2)}, u32[]{:S(2)}) collective-permute-start(f32[128,256]{1,0:T(8,128)S(1)} %get-tuple-element.50), channel_id=1, source_target_pairs={{0,3},{1,2},{2,1},{3,0},{4,7},{5,6},{6,5},{7,4},{8,11},{9,10},{10,... | collective-permute-start | bytes 393224 | tf_op jit(solution)/shard_map/ppermute | solution.py:447

commit v3 on v2

--- a/solution.py
+++ b/solution.py
@@ -17,6 +17,7 @@
 LAGS = 8
 FORWARD = ((0, 256), (256, 256))
 INVERSE = ((0, 256), (256, 256))
+SLOTS = (((0, 1, 2, 3),), ((0, 1), (2,), (3,)))
 GRANT = 16 << 20
 WIDE = 24 << 20
 ALL = ("strike", "depth")
@@ -46,8 +47,13 @@
 
 
 def dot3(left, right, dims):
-    mul = functools.partial(lax.dot_general, dimension_numbers=dims, preferred_element_type=F32)
-    return mul(left[0], right[0]) + (mul(left[0], right[1]) + mul(left[1], right[0]))
+    (left_axis,), (right_axis,) = dims[0]
+    return lax.dot_general(
+        jnp.concatenate([left[0], left[0], left[1]], axis=left_axis),
+        jnp.concatenate([right[0], right[1], right[0]], axis=right_axis),
+        dims,
+        preferred_element_type=F32,
+    )
 
 
 def depth_seeds(depth_len, blocks):
@@ -220,7 +226,7 @@
 
 def strike_kernel(
     x_ref, gain_hbm, past_hbm, wave_ref, twist_ref, modes_hbm, out_ref,
-    gain_ref, past_ref, held, modes_ref, sems,
+    gain_ref, past_ref, modes_ref, sems,
 ):
     edge = twist_ref.shape[1]
     pairs = ((gain_hbm, gain_ref), (past_hbm, past_ref))
@@ -257,22 +263,19 @@
     modes = dot3(forward, split(jnp.concatenate(turned, axis=0)), NT)
     for plane in range(2):
         for m in range(8):
-            held[plane, pl.ds(m, edge, stride=8), :] = lanes(modes, m)[plane * edge : (plane + 1) * edge]
-        for k in range(edge):
-            modes_ref[plane, :, k * edge : (k + 1) * edge] = held[plane, k * 8 : (k + 1) * 8, :]
+            modes_ref[plane, pl.ds(m, edge, stride=8), :] = lanes(modes, m)[
+                plane * edge : (plane + 1) * edge
+            ]
     save = pltpu.make_async_copy(modes_ref, modes_hbm, sems.at[2])
     save.start()
     for load in loads:
         load.wait()
     spectrum = []
     for m in range(8):
-        part = lanes(modes, m)
-        rows = pl.ds(m, edge, stride=8)
-        gain = gain_ref[rows, :]
+        part, gain = lanes(modes, m), gain_ref[m]
         spectrum.append(
             jnp.concatenate(
-                [gain * part[:edge] + past_ref[0, rows, :], gain * part[edge:] + past_ref[1, rows, :]],
-                axis=0,
+                [gain * part[:edge] + past_ref[0, m], gain * part[edge:] + past_ref[1, m]], axis=0
             )
         )
     third = dot3(backward, split(jnp.concatenate(spectrum, axis=1)), NN)
@@ -297,11 +300,11 @@
 def strike_both(pencil, gain, past, tables):
     waves, twist = tables
     edge = twist.shape[1]
-    modes = (2, 8, edge * edge)
+    modes = (2, edge * 8, edge)
     return pl.pallas_call(
         strike_kernel,
         out_shape=(
-            jax.ShapeDtypeStruct(modes, F32),
+            pltpu.HBM(modes, F32),
             jax.ShapeDtypeStruct((edge * 16, edge), F32),
         ),
         in_specs=[VMEM, HBM, HBM, VMEM, VMEM],
@@ -309,7 +312,6 @@
         scratch_shapes=[
             pltpu.VMEM(gain.shape, F32),
             pltpu.VMEM(past.shape, F32),
-            pltpu.VMEM((2, edge * 8, edge), F32),
             pltpu.VMEM(modes, F32),
             pltpu.SemaphoreType.DMA((3,)),
         ],
@@ -320,16 +322,14 @@
 
 
 def past_kernel(kernel_ref, history_ref, gain_ref, past_ref):
-    tiles = kernel_ref.shape[2] // 128
-    for tile in range(tiles):
+    for tile in range(kernel_ref.shape[2] // 128):
         cols = pl.ds(tile * 128, 128)
-        rows = pl.ds(tile * 8, 8)
-        gain_ref[rows, :] = kernel_ref[0, :, cols]
+        gain_ref[:, tile, :] = kernel_ref[0, :, cols]
         for plane in range(2):
             total = kernel_ref[1, :, cols] * history_ref[0, plane, :, cols]
             for lag in range(1, LAGS):
                 total = total + kernel_ref[lag + 1, :, cols] * history_ref[lag, plane, :, cols]
-            past_ref[plane, rows, :] = total
+            past_ref[plane, :, tile, :] = total
 
 
 def past_sum(kernel, history):
@@ -339,16 +339,16 @@
         past_kernel,
         grid=(length // block,),
         out_shape=(
-            jax.ShapeDtypeStruct((length // 16, 128), F32),
-            jax.ShapeDtypeStruct((2, length // 16, 128), F32),
+            pltpu.HBM((8, length // 128, 128), F32),
+            pltpu.HBM((2, 8, length // 128, 128), F32),
         ),
         in_specs=[
             pl.BlockSpec((LAGS + 1, 8, block), lambda i: (0, 0, i)),
             pl.BlockSpec((LAGS, 2, 8, block), lambda i: (0, 0, 0, i)),
         ],
         out_specs=(
-            pl.BlockSpec((block // 16, 128), lambda i: (i, 0)),
-            pl.BlockSpec((2, block // 16, 128), lambda i: (0, i, 0)),
+            pl.BlockSpec((8, block // 128, 128), lambda i: (0, i, 0)),
+            pl.BlockSpec((2, 8, block // 128, 128), lambda i: (0, 0, i, 0)),
         ),
         compiler_params=pltpu.CompilerParams(vmem_limit_bytes=WIDE),
         name="past_sum",
@@ -396,14 +396,14 @@
 
 
 def friction_kernel(
-    column, me_ref, own_ref, one_ref, two_ref, three_ref, scale_ref, rest_ref, gain_ref, strength_ref,
-    stress_ref, slip_ref, *refs
+    slots, column, me_ref, scale_ref, rest_ref, gain_ref, strength_ref, stress_ref, slip_ref, *refs
 ):
     velocity_hbm, new_hbm, velocity_ref, new_ref, sems = refs[-5:]
-    edge, width = own_ref.shape
+    parts = refs[: len(slots)]
+    edge, width = parts[0].shape
     cols = pl.ds(column, width)
     saves = []
-    for slot, ref in enumerate((own_ref, one_ref, two_ref, three_ref)):
+    for place, (slot, ref) in enumerate(zip(slots, parts)):
         rows = pl.ds(pl.multiple_of((me_ref[0] ^ slot) * edge, edge), edge)
         elastic = ref[...]
         scaling, strength = scale_ref[rows, cols], strength_ref[rows, cols]
@@ -412,35 +412,35 @@
         for sweep in range(NEWTON_ITERS - 1):
             friction, divisor = newton_parts(rate, scaling, strength)
             rate = rate + STEP * (total - DAMPING * rate - friction) / divisor
-        velocity_ref[slot] = rate
-        new_ref[slot] = slip_ref[rows, cols] + ADVANCE * rate
+        velocity_ref[place] = rate
+        new_ref[place] = slip_ref[rows, cols] + ADVANCE * rate
         for n, (source, target) in enumerate(((velocity_ref, velocity_hbm), (new_ref, new_hbm))):
-            save = pltpu.make_async_copy(source.at[slot], target.at[rows, cols], sems.at[slot, n])
+            save = pltpu.make_async_copy(source.at[place], target.at[rows, cols], sems.at[place, n])
             save.start()
             saves.append(save)
     for save in saves:
         save.wait()
 
 
-def friction_finish(column, me, elastic, start, strength, pre_stress, fault_slip, held=()):
+def friction_finish(slots, column, me, elastic, start, strength, pre_stress, fault_slip, held=()):
     edge, width = elastic[0].shape
     shape = jax.ShapeDtypeStruct(fault_slip.shape, F32)
-    count = 1 + 4 + 6
-    return pl.pallas_call(
-        functools.partial(friction_kernel, column),
-        in_specs=[SMEM] + [VMEM] * 10 + [HBM] * len(held),
+    count = 7 + len(slots)
+    return pl.pallas_call(
+        functools.partial(friction_kernel, slots, column),
+        in_specs=[SMEM] + [VMEM] * (6 + len(slots)) + [HBM] * len(held),
         out_specs=(HBM, HBM),
         out_shape=(shape, shape),
         scratch_shapes=[
-            pltpu.VMEM((4, edge, width), F32),
-            pltpu.VMEM((4, edge, width), F32),
-            pltpu.SemaphoreType.DMA((4, 2)),
+            pltpu.VMEM((len(slots), edge, width), F32),
+            pltpu.VMEM((len(slots), edge, width), F32),
+            pltpu.SemaphoreType.DMA((len(slots), 2)),
         ],
         input_output_aliases={count + n: n for n in range(len(held))},
         compiler_params=pltpu.CompilerParams(vmem_limit_bytes=GRANT),
         name="friction_finish",
         cost_estimate=pl.CostEstimate(flops=20_000_000, bytes_accessed=5_000_000, transcendentals=1_000_000),
-    )(me, *elastic, *start, strength, pre_stress, fault_slip, *in_hbm(*held))
+    )(me, *start, strength, pre_stress, fault_slip, *elastic, *in_hbm(*held))
 
 
 def exchange(parts, size):
@@ -467,23 +467,28 @@
         lines.append(exchange(blocks, depth_size))
     tables = depth_tables(depth_len, devices)
     gain, past = past_sum(kernel, history)
-    start = friction_start(rate_prev, log_state, weakening, strength, pre_stress)
     waves = None
     for (column, _), parts in zip(FORWARD, lines):
         waves = depth_forward(column, me, parts, tables, waves)
     pencil = lax.all_to_all(waves.reshape(devices, 16, edge), ALL, 0, 0)
     scale = 1.0 / math.sqrt(depth_len * edge * devices)
-    slip_modes, waves = strike_both(
+    modes, waves = strike_both(
         pencil.reshape(devices * 16, edge), gain, past, strike_tables(edge, scale)
     )
+    start = friction_start(rate_prev, log_state, weakening, strength, pre_stress)
     waves = lax.all_to_all(waves.reshape(devices, 16, edge), ALL, 0, 0).reshape(devices * 16, edge)
     elastic = [
         exchange(depth_inverse(column, width, me, waves, tables), depth_size)
         for column, width in INVERSE
     ]
     out = ()
-    for (column, _), parts in zip(INVERSE, elastic):
-        out = friction_finish(column, me, parts, start, strength, pre_stress, fault_slip, out)
+    for (column, _), parts, groups in zip(INVERSE, elastic, SLOTS):
+        for slots in groups:
+            parts_now = [parts[slot] for slot in slots]
+            out = friction_finish(
+                slots, column, me, parts_now, start, strength, pre_stress, fault_slip, out
+            )
+    slip_modes = modes.reshape(2, devices, 8, edge).transpose(0, 2, 1, 3).reshape(2, 8, devices * edge)
     return (*out, slip_modes)
 
 

time: 98.2 us -> 96.8 us (0.986)
  Pallas kernels: 23.1 us -> 25.6 us
  waiting for transfers between devices: 17.9 us -> 16 us
  local copies, waits for them, and re-layouts: 5.88 us -> 4.12 us
    pallas_call x4 -> x6, Pallas kernels: 15.5 us -> 17.9 us  [the longest x1 8.28 us: past_sum(): pl.pallas_call(past_kernel, grid=(length // block,), out_shape=(pltpu.HBM...]
    ppermute x12, waiting for transfers between devices: 7.43 us -> 5.09 us  [exchange(): lax.ppermute(part, 'depth', [(place, place ^ k) for place in range(size)])]
    unnamed x28 -> x24, local copies, waits for them, and re-layouts: 3.61 us -> 1.85 us
  transfers between devices with their start and end apart: 13 -> 13, of which waited for: 6 -> 5; matrix products, arithmetic and copies ran while one was open for 1% -> 1% of each run, Pallas kernels for 13% -> 18%
where the time goes in v3:
time: 96.8 us; the launch traced here: 96.3 us
  starting transfers between devices  26.4 us (27%)
  Pallas kernels  25.6 us (26%)
  blocking collectives  23.3 us (24%)
  waiting for transfers between devices  16 us (17%)
  local copies, waits for them, and re-layouts  4.12 us (4%)
  between operations  1.02 us (1%)
    all_to_all x1, blocking collectives, body(): lax.all_to_all(waves.reshape(devices, 16, edge), ALL, 0, 0)  23.3 us
    ppermute x12, starting transfers between devices, exchange(): lax.ppermute(part, 'depth', [(place, place ^ k) for place in range(size)])  17.2 us
    all_to_all x1, waiting for transfers between devices, body(): pencil = lax.all_to_all(waves.reshape(devices, 16, edge), ALL, 0, 0)  10.9 us
    all_to_all x1, starting transfers between devices, body(): pencil = lax.all_to_all(waves.reshape(devices, 16, edge), ALL, 0, 0)  9.18 us
    pallas_call x1, Pallas kernels, past_sum(): pl.pallas_call(past_kernel, grid=(length // block,), out_shape=(pltpu.HBM...  8.28 us
    pallas_call x4, Pallas kernels, friction_finish(): pl.pallas_call(functools.partial(friction_kernel, slots, column), in_spec...  5.57 us
    ppermute x12, waiting for transfers between devices, exchange(): lax.ppermute(part, 'depth', [(place, place ^ k) for place in range(size)])  5.09 us
    pallas_call x1, Pallas kernels, strike_both(): pl.pallas_call(strike_kernel, out_shape=(pltpu.HBM(modes, F32), jax.Shape...  4.1 us
  transfers between devices with their start and end apart: 13, of which 5 were waited for; matrix products, arithmetic and copies ran while one was open for 1% of the time, Pallas kernels for 18%

profile of v3, /device:TPU:1, one launch (start us, length us, event | category | flops | bytes accessed | tf_op | source)
XLA Modules:
  0.0 96.3 jit_solution(14467341304827842399)
XLA Ops:
  0.7 1.1 %constant_dynamic-slice_fusion.4 = (f32[128,256]{1,0:T(8,128)S(1)}, f32[128,256]{1,0:T(8,128)S(1)}, f32[128,256]{1,0:T(8,128)S(1)}, f32[128,256]{1,0:T(8,128)S(1)}) fusion(f32[512,512]{1,0:T(8,128)} %slip_ref.7, s32[]{:T(128)S(6)} %select_n.19, s32[]{:T(128)S(6)} %select_n.18, s32[]{:T(128)S(6)} %select_n.17, s32[]{:T(128)S(6)} %select_n.16), kind=kLoop, calls=%fused_computation.4 | loop fusion | bytes 1048592 | tf_op jit(solution)/shard_map/dynamic_slice | solution.py:463
  1.8 1.5 %collective-permute-start.3 = (f32[128,256]{1,0:T(8,128)S(1)}, f32[128,256]{1,0:T(8,128)S(1)}, u32[]{:S(2)}, u32[]{:S(2)}) collective-permute-start(f32[128,256]{1,0:T(8,128)S(1)} %get-tuple-element.48), channel_id=1, source_target_pairs={{0,1},{1,0},{2,3},{3,2},{4,5},{5,4},{6,7},{7,6},{8,9},{9,8},{10,11... | collective-permute-start | bytes 393224 | tf_op jit(solution)/shard_map/ppermute | solution.py:447
  3.3 3.7 %collective-permute-start.4 = (f32[128,256]{1,0:T(8,128)S(1)}, f32[128,256]{1,0:T(8,128)S(1)}, u32[]{:S(2)}, u32[]{:S(2)}) collective-permute-start(f32[128,256]{1,0:T(8,128)S(1)} %get-tuple-element.49), channel_id=1, source_target_pairs={{0,2},{1,3},{2,0},{3,1},{4,6},{5,7},{6,4},{7,5},{8,10},{9,11},{10,... | collective-permute-start | bytes 393224 | tf_op jit(solution)/shard_map/ppermute | solution.py:447
  7.0 0.1 collective-permute-start.5
  7.0 1.1 %constant_dynamic-slice_fusion = (f32[128,256]{1,0:T(8,128)S(1)}, f32[128,256]{1,0:T(8,128)S(1)}, f32[128,256]{1,0:T(8,128)S(1)}, f32[128,256]{1,0:T(8,128)S(1)}) fusion(f32[512,512]{1,0:T(8,128)} %slip_ref.7, s32[]{:T(128)S(6)} %select_n.19, s32[]{:T(128)S(6)} %select_n.18, s32[]{:T(128)S(6)} %select_n.17, s32[]{:T(128)S(6)} %select_n.16), kind=kLoop, calls=%fused_computation | loop fusion | bytes 1048592 | tf_op jit(solution)/shard_map/dynamic_slice | solution.py:463
  8.2 0.4 collective-permute-start
  8.6 3.0 %collective-permute-start.1 = (f32[128,256]{1,0:T(8,128)S(1)}, f32[128,256]{1,0:T(8,128)S(1)}, u32[]{:S(2)}, u32[]{:S(2)}) collective-permute-start(f32[128,256]{1,0:T(8,128)S(1)} %get-tuple-element.43), channel_id=1, source_target_pairs={{0,2},{1,3},{2,0},{3,1},{4,6},{5,7},{6,4},{7,5},{8,10},{9,11},{10,... | collective-permute-start | bytes 393224 | tf_op jit(solution)/shard_map/ppermute | solution.py:447
  11.6 0.0 collective-permute-done.3.one_ref
  11.6 0.4 collective-permute-start.2
  11.9 0.0 copy-start.8
  11.9 1.0 %copy-done.8 = f32[2,128,512]{2,1,0:T(8,128)S(1)} copy-done((f32[2,128,512]{2,1,0:T(8,128)S(1)}, f32[2,128,512]{2,1,0:T(8,128)}, u32[]{:S(2)}) %copy-start.8) | copy-done | bytes 524312
  13.0 0.0 copy-start.9
  13.0 0.8 copy-done.9
  13.7 1.0 %depth_tables.1 = (bf16[4,512,512]{2,1,0:T(8,128)(2,1)S(1)}, bf16[4,512,512]{2,1,0:T(8,128)(2,1)S(1)}) custom-call(f32[2,128,512]{2,1,0:T(8,128)S(1)} %copy-done.8, f32[2,8,512]{2,1,0:T(8,128)S(1)} %copy-done.9), custom_call_target="tpu_custom_call" | custom-call | flops 10000000 | bytes 5000000 | tf_op jit(solution)/shard_map/depth_tables/pallas_call | solution.py:88
  14.7 0.0 copy-start
  14.8 0.0 collective-permute-done.4.two_ref
  14.8 0.0 collective-permute-done.5.three_ref
  14.8 1.0 %depth_forward.2.refs_0_ = f32[16,128,128]{2,1,0:T(8,128)S(1)} custom-call(s32[1]{0:T(128)} %bitcast.me_ref, f32[128,256]{1,0:T(8,128)S(1)} %get-tuple-element.47.own_ref, f32[128,256]{1,0:T(8,128)S(1)} %collective-permute-done.3.one_ref, f32[128,256]{1,0:T(8,128)S(1)} %collective-permute-done.4.two_ref, f32[128,256]{1,0:T(8,128)S(1)} %collective-permute-done.5.three_ref, ...), custom_call_target="tpu_custom_call" | custom-call | flops 1200000000 | bytes 4000000 | tf_op jit(solution)/shard_map/depth_forward/pallas_call | solution.py:143
  15.8 0.0 collective-permute-done.one_ref
  15.8 0.9 collective-permute-done.1.two_ref
  16.7 2.8 %collective-permute-done.2.three_ref = f32[128,256]{1,0:T(8,128)S(1)} collective-permute-done((f32[128,256]{1,0:T(8,128)S(1)}, f32[128,256]{1,0:T(8,128)S(1)}, u32[]{:S(2)}, u32[]{:S(2)}) %collective-permute-start.2) | collective-permute-done | bytes 131104 | tf_op jit(solution)/shard_map/ppermute | solution.py:447
  19.6 2.2 %depth_forward.3 = f32[2048,128]{1,0:T(8,128)} custom-call(s32[1]{0:T(128)} %bitcast.me_ref, f32[128,256]{1,0:T(8,128)S(1)} %get-tuple-element.41.own_ref, f32[128,256]{1,0:T(8,128)S(1)} %collective-permute-done.one_ref, f32[128,256]{1,0:T(8,128)S(1)} %collective-permute-done.1.two_ref, f32[128,256]{1,0:T(8,128)S(1)} %collective-permute-done.2.three_ref, ...), custom_call_target="tpu_custom_call" | custom-call | flops 1200000000 | bytes 4000000 | tf_op jit(solution)/shard_map/depth_forward/pallas_call | solution.py:143
  21.8 0.0 copy-done
  21.8 9.2 %all-to-all-start = ((f32[128,16,128]{2,1,0:T(8,128)}), f32[128,16,128]{2,1,0:T(8,128)S(1)}, u32[]{:S(2)}, u32[]{:S(2)}) async-start(f32[128,16,128]{2,1,0:T(8,128)} %bitcast.1), calls=%async_computation | async-start | bytes 2097152 | tf_op jit(solution)/shard_map/all_to_all | solution.py:473
  30.9 0.0 copy-start.10
  30.9 0.0 copy-start.11
  31.0 8.3 %past_sum.1 = (f32[8,128,128]{2,1,0:T(8,128)}, f32[2,8,128,128]{3,2,1,0:T(8,128)}) custom-call(f32[9,8,16384]{2,1,0:T(8,128)} %kernel_ref.1, f32[8,2,8,16384]{3,2,1,0:T(8,128)} %history_ref.1), custom_call_target="tpu_custom_call" | custom-call | flops 4200000 | bytes 14700000 | tf_op jit(solution)/shard_map/past_sum/pallas_call | solution.py:338
  39.2 10.9 %all-to-all-done = f32[128,16,128]{2,1,0:T(8,128)S(1)} async-done(((f32[128,16,128]{2,1,0:T(8,128)}), f32[128,16,128]{2,1,0:T(8,128)S(1)}, u32[]{:S(2)}, u32[]{:S(2)}) %all-to-all-start) | async-done | bytes 1048608 | tf_op jit(solution)/shard_map/all_to_all | solution.py:473
  50.1 0.0 copy-start.1
  50.1 0.0 copy-done.10
  50.1 0.0 copy-done.11
  50.1 4.1 %strike_both.1 = (f32[2,1024,128]{2,1,0:T(8,128)}, f32[2048,128]{1,0:T(8,128)S(1)}) custom-call(f32[2048,128]{1,0:T(8,128)S(1)} %bitcast.12, f32[8,128,128]{2,1,0:T(8,128)} %get-tuple-element.51.gain_hbm, f32[2,8,128,128]{3,2,1,0:T(8,128)} %get-tuple-element.52.past_hbm, bf16[4,128,128]{2,1,0:T(8,128)(2,1)S(1)} %copy-done.11, f32[2,128,128]{2,1,0:T(8,128)S(1)} %copy-done.10), custom_call_target="tpu_custom_call" | custom-call | flops 1600000000 | bytes 6000000 | tf_op jit(solution)/shard_map/strike_both/pallas_call | solution.py:304
  54.2 23.3 %all_to_all.10 = f32[128,16,128]{2,1,0:T(8,128)S(1)} all-to-all(f32[128,16,128]{2,1,0:T(8,128)S(1)} %bitcast.13), channel_id=1, replica_groups=mesh['strike'=32,'depth'=4] {'strike','depth'}, dimensions={0} | all-to-all | bytes 2097152 | tf_op jit(solution)/shard_map/all_to_all | solution.py:479
  77.5 0.0 copy-done.1
  77.5 0.0 copy-start.2
  77.5 0.0 copy-start.3
  77.5 0.0 copy-start.5
  77.5 0.0 copy-start.6
  77.5 0.0 copy-start.7
  77.5 1.2 %depth_inverse.3 = (f32[128,256]{1,0:T(8,128)S(1)}, f32[128,256]{1,0:T(8,128)S(1)}, f32[128,256]{1,0:T(8,128)S(1)}, f32[128,256]{1,0:T(8,128)S(1)}) custom-call(s32[1]{0:T(128)} %bitcast.me_ref, f32[2048,128]{1,0:T(8,128)S(1)} %bitcast.10, bf16[4,512,512]{2,1,0:T(8,128)(2,1)S(1)} %get-tuple-element.45.high_ref, bf16[4,512,512]{2,1,0:T(8,128)(2,1)S(1)} %copy-done.1), custom_call_target="tpu_custom_call" | custom-call | flops 1200000000 | bytes 4000000 | tf_op jit(solution)/shard_map/depth_inverse/pallas_call | solution.py:207
  78.7 1.3 %collective-permute-start.9 = (f32[128,256]{1,0:T(8,128)S(1)}, f32[128,256]{1,0:T(8,128)S(1)}, u32[]{:S(2)}, u32[]{:S(2)}) collective-permute-start(f32[128,256]{1,0:T(8,128)S(1)} %get-tuple-element.59), channel_id=1, source_target_pairs={{0,1},{1,0},{2,3},{3,2},{4,5},{5,4},{6,7},{7,6},{8,9},{9,8},{10,11... | collective-permute-start | bytes 393224 | tf_op jit(solution)/shard_map/ppermute | solution.py:447
  80.0 0.6 collective-permute-start.10
  80.6 2.6 %collective-permute-start.11 = (f32[128,256]{1,0:T(8,128)S(1)}, f32[128,256]{1,0:T(8,128)S(1)}, u32[]{:S(2)}, u32[]{:S(2)}) collective-permute-start(f32[128,256]{1,0:T(8,128)S(1)} %get-tuple-element.61), channel_id=1, source_target_pairs={{0,3},{1,2},{2,1},{3,0},{4,7},{5,6},{6,5},{7,4},{8,11},{9,10},{10,... | collective-permute-start | bytes 393224 | tf_op jit(solution)/shard_map/ppermute | solution.py:447
  83.2 1.1 %depth_inverse.2 = (f32[128,256]{1,0:T(8,128)S(1)}, f32[128,256]{1,0:T(8,128)S(1)}, f32[128,256]{1,0:T(8,128)S(1)}, f32[128,256]{1,0:T(8,128)S(1)}) custom-call(s32[1]{0:T(128)} %bitcast.me_ref, f32[2048,128]{1,0:T(8,128)S(1)} %bitcast.11, bf16[4,512,512]{2,1,0:T(8,128)(2,1)S(1)} %get-tuple-element.45.high_ref, bf16[4,512,512]{2,1,0:T(8,128)(2,1)S(1)} %copy-done.1), custom_call_target="tpu_custom_call" | custom-call | flops 1200000000 | bytes 4000000 | tf_op jit(solution)/shard_map/depth_inverse/pallas_call | solution.py:207
  84.3 0.2 collective-permute-start.8
  84.6 0.7 collective-permute-start.7
  85.3 0.0 collective-permute-done.9.refs_1_
  85.3 2.8 %collective-permute-start.6 = (f32[128,256]{1,0:T(8,128)S(1)}, f32[128,256]{1,0:T(8,128)S(1)}, u32[]{:S(2)}, u32[]{:S(2)}) collective-permute-start(f32[128,256]{1,0:T(8,128)S(1)} %get-tuple-element.54), channel_id=1, source_target_pairs={{0,3},{1,2},{2,1},{3,0},{4,7},{5,6},{6,5},{7,4},{8,11},{9,10},{10,... | collective-permute-start | bytes 393224 | tf_op jit(solution)/shard_map/ppermute | solution.py:447
  88.1 0.0 copy-done.2
  88.1 0.0 copy-done.3
  88.1 0.0 copy-done.5
  88.1 0.0 copy-done.6
  88.1 0.0 copy-done.7
  88.1 1.2 %friction_start.1 = (f32[512,512]{1,0:T(8,128)S(1)}, f32[512,512]{1,0:T(8,128)S(1)}, f32[512,512]{1,0:T(8,128)S(1)}) custom-call(f32[512,512]{1,0:T(8,128)S(1)} %copy-done.5, f32[512,512]{1,0:T(8,128)S(1)} %copy-done.6, f32[512,512]{1,0:T(8,128)S(1)} %copy-done.7, f32[512,512]{1,0:T(8,128)S(1)} %copy-done.2, f32[512,512]{1,0:T(8,128)S(1)} %copy-done.3), custom_call_target="tpu_custom_call" | custom-call | flops 20000000 | bytes 8000000 | tf_op jit(solution)/shard_map/friction_start/pallas_call | solution.py:386
  89.3 0.0 collective-permute-done.10.refs_2_
  89.3 0.7 collective-permute-done.11.refs_3_
  90.0 0.0 copy-done.4
  90.0 2.0 %friction_finish.4 = (f32[512,512]{1,0:T(8,128)}, f32[512,512]{1,0:T(8,128)}) custom-call(s32[1]{0:T(128)} %bitcast.me_ref, f32[512,512]{1,0:T(8,128)S(1)} %get-tuple-element.37.scale_ref, f32[512,512]{1,0:T(8,128)S(1)} %get-tuple-element.38.rest_ref, f32[512,512]{1,0:T(8,128)S(1)} %get-tuple-element.39.gain_ref, f32[512,512]{1,0:T(8,128)S(1)} %copy-done.2, ...), custom_call_target="tpu_custom_call" | custom-call | flops 20000000 | bytes 5000000 | tf_op jit(solution)/shard_map/friction_finish/pallas_call | solution.py:429
  92.0 0.0 collective-permute-done.8.refs_1_
  92.0 1.4 %friction_finish.5 = (f32[512,512]{1,0:T(8,128)}, f32[512,512]{1,0:T(8,128)}) custom-call(s32[1]{0:T(128)} %bitcast.me_ref, f32[512,512]{1,0:T(8,128)S(1)} %get-tuple-element.37.scale_ref, f32[512,512]{1,0:T(8,128)S(1)} %get-tuple-element.38.rest_ref, f32[512,512]{1,0:T(8,128)S(1)} %get-tuple-element.39.gain_ref, ...), custom_call_target="tpu_custom_call", output_to_operand_aliasing={{0}: (9, {}), {1}: (10, {})} | custom-call | flops 20000000 | bytes 5000000 | tf_op jit(solution)/shard_map/friction_finish/pallas_call | solution.py:429
  93.4 0.0 collective-permute-done.7.refs_0_
  93.5 1.1 %friction_finish.6 = (f32[512,512]{1,0:T(8,128)}, f32[512,512]{1,0:T(8,128)}) custom-call(s32[1]{0:T(128)} %bitcast.me_ref, f32[512,512]{1,0:T(8,128)S(1)} %get-tuple-element.37.scale_ref, f32[512,512]{1,0:T(8,128)S(1)} %get-tuple-element.38.rest_ref, f32[512,512]{1,0:T(8,128)S(1)} %get-tuple-element.39.gain_ref, ...), custom_call_target="tpu_custom_call", output_to_operand_aliasing={{0}: (8, {}), {1}: (9, {})} | custom-call | flops 20000000 | bytes 5000000 | tf_op jit(solution)/shard_map/friction_finish/pallas_call | solution.py:429
  94.5 0.6 collective-permute-done.6.refs_0_
  95.1 1.1 %friction_finish.7 = (f32[512,512]{1,0:T(8,128)}, f32[512,512]{1,0:T(8,128)}) custom-call(s32[1]{0:T(128)} %bitcast.me_ref, f32[512,512]{1,0:T(8,128)S(1)} %get-tuple-element.37.scale_ref, f32[512,512]{1,0:T(8,128)S(1)} %get-tuple-element.38.rest_ref, f32[512,512]{1,0:T(8,128)S(1)} %get-tuple-element.39.gain_ref, ...), custom_call_target="tpu_custom_call", output_to_operand_aliasing={{0}: (8, {}), {1}: (9, {})} | custom-call | flops 20000000 | bytes 5000000 | tf_op jit(solution)/shard_map/friction_finish/pallas_call | solution.py:429
  (1 shorter events, 0.0 us)
Async XLA Ops:
  1.8 9.8 %collective-permute-start.3 = (f32[128,256]{1,0:T(8,128)S(1)}, f32[128,256]{1,0:T(8,128)S(1)}, u32[]{:S(2)}, u32[]{:S(2)}) collective-permute-start(f32[128,256]{1,0:T(8,128)S(1)} %get-tuple-element.48), channel_id=1, source_target_pairs={{0,1},{1,0},{2,3},{3,2},{4,5},{5,4},{6,7},{7,6},{8,9},{9,8},{10,11... | collective-permute-start | bytes 393224 | tf_op jit(solution)/shard_map/ppermute | solution.py:447
  3.3 11.5 %collective-permute-start.4 = (f32[128,256]{1,0:T(8,128)S(1)}, f32[128,256]{1,0:T(8,128)S(1)}, u32[]{:S(2)}, u32[]{:S(2)}) collective-permute-start(f32[128,256]{1,0:T(8,128)S(1)} %get-tuple-element.49), channel_id=1, source_target_pairs={{0,2},{1,3},{2,0},{3,1},{4,6},{5,7},{6,4},{7,5},{8,10},{9,11},{10,... | collective-permute-start | bytes 393224 | tf_op jit(solution)/shard_map/ppermute | solution.py:447
  7.0 7.8 %collective-permute-start.5 = (f32[128,256]{1,0:T(8,128)S(1)}, f32[128,256]{1,0:T(8,128)S(1)}, u32[]{:S(2)}, u32[]{:S(2)}) collective-permute-start(f32[128,256]{1,0:T(8,128)S(1)} %get-tuple-element.50), channel_id=1, source_target_pairs={{0,3},{1,2},{2,1},{3,0},{4,7},{5,6},{6,5},{7,4},{8,11},{9,10},{10,... | collective-permute-start | bytes 393224 | tf_op jit(solution)/shard_map/ppermute | solution.py:447
  8.2 7.6 %collective-permute-start = (f32[128,256]{1,0:T(8,128)S(1)}, f32[128,256]{1,0:T(8,128)S(1)}, u32[]{:S(2)}, u32[]{:S(2)}) collective-permute-start(f32[128,256]{1,0:T(8,128)S(1)} %get-tuple-element.42), channel_id=1, source_target_pairs={{0,1},{1,0},{2,3},{3,2},{4,5},{5,4},{6,7},{7,6},{8,9},{9,8},{10,11... | collective-permute-start | bytes 393224 | tf_op jit(solution)/shard_map/ppermute | solution.py:447
  8.6 8.1 %collective-permute-start.1 = (f32[128,256]{1,0:T(8,128)S(1)}, f32[128,256]{1,0:T(8,128)S(1)}, u32[]{:S(2)}, u32[]{:S(2)}) collective-permute-start(f32[128,256]{1,0:T(8,128)S(1)} %get-tuple-element.43), channel_id=1, source_target_pairs={{0,2},{1,3},{2,0},{3,1},{4,6},{5,7},{6,4},{7,5},{8,10},{9,11},{10,... | collective-permute-start | bytes 393224 | tf_op jit(solution)/shard_map/ppermute | solution.py:447
  11.6 8.0 %collective-permute-start.2 = (f32[128,256]{1,0:T(8,128)S(1)}, f32[128,256]{1,0:T(8,128)S(1)}, u32[]{:S(2)}, u32[]{:S(2)}) collective-permute-start(f32[128,256]{1,0:T(8,128)S(1)} %get-tuple-element.44), channel_id=1, source_target_pairs={{0,3},{1,2},{2,1},{3,0},{4,7},{5,6},{6,5},{7,4},{8,11},{9,10},{10,... | collective-permute-start | bytes 393224 | tf_op jit(solution)/shard_map/ppermute | solution.py:447
  11.9 1.0 %copy-start.8 = (f32[2,128,512]{2,1,0:T(8,128)S(1)}, f32[2,128,512]{2,1,0:T(8,128)}, u32[]{:S(2)}) copy-start(f32[2,128,512]{2,1,0:T(8,128)} %constant.26.clone.coarse_ref) | copy-start | bytes 1572868
  13.0 0.8 copy-start.9
  14.7 7.0 %copy-start = (bf16[4,512,512]{2,1,0:T(8,128)(2,1)}, bf16[4,512,512]{2,1,0:T(8,128)(2,1)S(1)}, u32[]{:S(2)}) copy-start(bf16[4,512,512]{2,1,0:T(8,128)(2,1)S(1)} %get-tuple-element.46.low_ref) | copy-start | bytes 6291460
  21.8 28.3 %all-to-all-start = ((f32[128,16,128]{2,1,0:T(8,128)}), f32[128,16,128]{2,1,0:T(8,128)S(1)}, u32[]{:S(2)}, u32[]{:S(2)}) async-start(f32[128,16,128]{2,1,0:T(8,128)} %bitcast.1), calls=%async_computation | async-start | bytes 2097152 | tf_op jit(solution)/shard_map/all_to_all | solution.py:473
  30.9 19.2 %copy-start.10 = (f32[2,128,128]{2,1,0:T(8,128)S(1)}, f32[2,128,128]{2,1,0:T(8,128)}, u32[]{:S(2)}) copy-start(f32[2,128,128]{2,1,0:T(8,128)} %constant.29.clone.twist_ref) | copy-start | bytes 393220
  30.9 19.2 %copy-start.11 = (bf16[4,128,128]{2,1,0:T(8,128)(2,1)S(1)}, bf16[4,128,128]{2,1,0:T(8,128)(2,1)}, u32[]{:S(2)}) copy-start(bf16[4,128,128]{2,1,0:T(8,128)(2,1)} %constant.28.clone.wave_ref) | copy-start | bytes 393220
  50.1 27.4 %copy-start.1 = (bf16[4,512,512]{2,1,0:T(8,128)(2,1)S(1)}, bf16[4,512,512]{2,1,0:T(8,128)(2,1)}, u32[]{:S(2)}) copy-start(bf16[4,512,512]{2,1,0:T(8,128)(2,1)} %copy-done) | copy-start | bytes 6291460
  77.5 10.6 %copy-start.2 = (f32[512,512]{1,0:T(8,128)S(1)}, f32[512,512]{1,0:T(8,128)}, u32[]{:S(2)}) copy-start(f32[512,512]{1,0:T(8,128)} %strength_ref.9) | copy-start | bytes 3145732
  77.5 10.6 %copy-start.3 = (f32[512,512]{1,0:T(8,128)S(1)}, f32[512,512]{1,0:T(8,128)}, u32[]{:S(2)}) copy-start(f32[512,512]{1,0:T(8,128)} %stress_ref.9) | copy-start | bytes 3145732
  77.5 10.6 %copy-start.5 = (f32[512,512]{1,0:T(8,128)S(1)}, f32[512,512]{1,0:T(8,128)}, u32[]{:S(2)}) copy-start(f32[512,512]{1,0:T(8,128)} %rate_ref.1) | copy-start | bytes 3145732
  77.5 10.6 %copy-start.6 = (f32[512,512]{1,0:T(8,128)S(1)}, f32[512,512]{1,0:T(8,128)}, u32[]{:S(2)}) copy-start(f32[512,512]{1,0:T(8,128)} %state_ref.1) | copy-start | bytes 3145732
  77.5 10.6 %copy-start.7 = (f32[512,512]{1,0:T(8,128)S(1)}, f32[512,512]{1,0:T(8,128)}, u32[]{:S(2)}) copy-start(f32[512,512]{1,0:T(8,128)} %weak_ref.1) | copy-start | bytes 3145732
  78.7 6.6 %collective-permute-start.9 = (f32[128,256]{1,0:T(8,128)S(1)}, f32[128,256]{1,0:T(8,128)S(1)}, u32[]{:S(2)}, u32[]{:S(2)}) collective-permute-start(f32[128,256]{1,0:T(8,128)S(1)} %get-tuple-element.59), channel_id=1, source_target_pairs={{0,1},{1,0},{2,3},{3,2},{4,5},{5,4},{6,7},{7,6},{8,9},{9,8},{10,11... | collective-permute-start | bytes 393224 | tf_op jit(solution)/shard_map/ppermute | solution.py:447
  80.0 9.3 %collective-permute-start.10 = (f32[128,256]{1,0:T(8,128)S(1)}, f32[128,256]{1,0:T(8,128)S(1)}, u32[]{:S(2)}, u32[]{:S(2)}) collective-permute-start(f32[128,256]{1,0:T(8,128)S(1)} %get-tuple-element.60), channel_id=1, source_target_pairs={{0,2},{1,3},{2,0},{3,1},{4,6},{5,7},{6,4},{7,5},{8,10},{9,11},{10,... | collective-permute-start | bytes 393224 | tf_op jit(solution)/shard_map/ppermute | solution.py:447
  80.6 9.4 %copy-start.4 = (f32[512,512]{1,0:T(8,128)S(1)}, f32[512,512]{1,0:T(8,128)}, u32[]{:S(2)}) copy-start(f32[512,512]{1,0:T(8,128)} %slip_ref.7) | copy-start | bytes 3145732
  80.6 9.4 %collective-permute-start.11 = (f32[128,256]{1,0:T(8,128)S(1)}, f32[128,256]{1,0:T(8,128)S(1)}, u32[]{:S(2)}, u32[]{:S(2)}) collective-permute-start(f32[128,256]{1,0:T(8,128)S(1)} %get-tuple-element.61), channel_id=1, source_target_pairs={{0,3},{1,2},{2,1},{3,0},{4,7},{5,6},{6,5},{7,4},{8,11},{9,10},{10,... | collective-permute-start | bytes 393224 | tf_op jit(solution)/shard_map/ppermute | solution.py:447
  84.3 7.7 %collective-permute-start.8 = (f32[128,256]{1,0:T(8,128)S(1)}, f32[128,256]{1,0:T(8,128)S(1)}, u32[]{:S(2)}, u32[]{:S(2)}) collective-permute-start(f32[128,256]{1,0:T(8,128)S(1)} %get-tuple-element.57), channel_id=1, source_target_pairs={{0,1},{1,0},{2,3},{3,2},{4,5},{5,4},{6,7},{7,6},{8,9},{9,8},{10,11... | collective-permute-start | bytes 393224 | tf_op jit(solution)/shard_map/ppermute | solution.py:447
  84.6 8.9 %collective-permute-start.7 = (f32[128,256]{1,0:T(8,128)S(1)}, f32[128,256]{1,0:T(8,128)S(1)}, u32[]{:S(2)}, u32[]{:S(2)}) collective-permute-start(f32[128,256]{1,0:T(8,128)S(1)} %get-tuple-element.55), channel_id=1, source_target_pairs={{0,2},{1,3},{2,0},{3,1},{4,6},{5,7},{6,4},{7,5},{8,10},{9,11},{10,... | collective-permute-start | bytes 393224 | tf_op jit(solution)/shard_map/ppermute | solution.py:447
  85.3 9.8 %collective-permute-start.6 = (f32[128,256]{1,0:T(8,128)S(1)}, f32[128,256]{1,0:T(8,128)S(1)}, u32[]{:S(2)}, u32[]{:S(2)}) collective-permute-start(f32[128,256]{1,0:T(8,128)S(1)} %get-tuple-element.54), channel_id=1, source_target_pairs={{0,3},{1,2},{2,1},{3,0},{4,7},{5,6},{6,5},{7,4},{8,11},{9,10},{10,... | collective-permute-start | bytes 393224 | tf_op jit(solution)/shard_map/ppermute | solution.py:447

commit v4 on v3

--- a/solution.py
+++ b/solution.py
@@ -18,6 +18,7 @@
 FORWARD = ((0, 256), (256, 256))
 INVERSE = ((0, 256), (256, 256))
 SLOTS = (((0, 1, 2, 3),), ((0, 1), (2,), (3,)))
+PAIR = 2
 GRANT = 16 << 20
 WIDE = 24 << 20
 ALL = ("strike", "depth")
@@ -221,26 +222,30 @@
     waves = np.stack([*split_np(np.cos(angle)), *split_np(np.sin(angle))])
     twist = 2.0 * np.pi / (edge * edge) * np.outer(np.arange(edge), np.arange(edge))
     twist = np.stack([np.cos(twist), np.sin(twist)]) * scale
-    return waves, twist.astype(np.float32)
+    return waves, np.concatenate([twist, 2.0 * twist]).astype(np.float32)
 
 
 def strike_kernel(
     x_ref, gain_hbm, past_hbm, wave_ref, twist_ref, modes_hbm, out_ref,
-    gain_ref, past_ref, modes_ref, sems,
+    gain_ref, past_ref, held_ref, modes_ref, sems,
 ):
     edge = twist_ref.shape[1]
     pairs = ((gain_hbm, gain_ref), (past_hbm, past_ref))
     loads = [pltpu.make_async_copy(a, b, sems.at[n]) for n, (a, b) in enumerate(pairs)]
     for load in loads:
         load.start()
-    lanes = lambda value, m: value[:, m * edge : (m + 1) * edge]
-
-    def gather(ref, m):
+
+    def lines(group):
+        return range(group * PAIR, (group + 1) * PAIR)
+
+    def lanes(value, place):
+        part = value[:, place * edge : (place + 1) * edge]
+        return part[:edge], part[edge:]
+
+    def gather(m):
         return jnp.concatenate(
-            [ref[pl.ds(plane * 8 + m, edge, stride=16), :] for plane in range(2)], axis=0
+            [x_ref[pl.ds(plane * 8 + m, edge, stride=16), :] for plane in range(2)], axis=0
         )
-
-    parts = split(jnp.concatenate([gather(x_ref, m) for m in range(8)], axis=1))
 
     def block(sign, part):
         cosine, sine = wave_ref[part], wave_ref[2 + part]
@@ -249,51 +254,45 @@
             [jnp.concatenate([cosine, left], axis=1), jnp.concatenate([right, cosine], axis=1)], axis=0
         )
 
+    def rotate(value, sign, cosine, sine):
+        rows = []
+        for place in range(PAIR):
+            real, imag = lanes(value, place)
+            if sign > 0:
+                rows.append([real * cosine + imag * sine, imag * cosine - real * sine])
+            else:
+                rows.append([real * cosine - imag * sine, imag * cosine + real * sine])
+        return jnp.concatenate([jnp.concatenate(row, axis=1) for row in rows], axis=0)
+
     forward = (block(1, 0), block(1, 1))
-    backward = (block(-1, 0), block(-1, 1))
-    first = dot3(forward, parts, NN)
-    cosine, sine = twist_ref[0], twist_ref[1]
-    turned = []
-    for m in range(8):
-        part = lanes(first, m)
-        real, imag = part[:edge], part[edge:]
-        turned.append(
-            jnp.concatenate([real * cosine + imag * sine, imag * cosine - real * sine], axis=1)
-        )
-    modes = dot3(forward, split(jnp.concatenate(turned, axis=0)), NT)
-    for plane in range(2):
-        for m in range(8):
-            modes_ref[plane, pl.ds(m, edge, stride=8), :] = lanes(modes, m)[
-                plane * edge : (plane + 1) * edge
-            ]
+    for group in range(8 // PAIR):
+        value = jnp.concatenate([gather(m) for m in lines(group)], axis=1)
+        value = dot3(forward, split(value), NN)
+        value = dot3(forward, split(rotate(value, 1, twist_ref[0], twist_ref[1])), NT)
+        for place, m in enumerate(lines(group)):
+            for plane, part in enumerate(lanes(value, place)):
+                held_ref[plane, m] = part
+                modes_ref[plane, pl.ds(m, edge, stride=8), :] = part
     save = pltpu.make_async_copy(modes_ref, modes_hbm, sems.at[2])
     save.start()
     for load in loads:
         load.wait()
-    spectrum = []
-    for m in range(8):
-        part, gain = lanes(modes, m), gain_ref[m]
-        spectrum.append(
-            jnp.concatenate(
-                [gain * part[:edge] + past_ref[0, m], gain * part[edge:] + past_ref[1, m]], axis=0
-            )
+    backward = (block(-1, 0), block(-1, 1))
+    for group in range(8 // PAIR):
+        value = jnp.concatenate(
+            [
+                jnp.concatenate(
+                    [gain_ref[m] * held_ref[plane, m] + past_ref[plane, m] for plane in range(2)], axis=0
+                )
+                for m in lines(group)
+            ],
+            axis=1,
         )
-    third = dot3(backward, split(jnp.concatenate(spectrum, axis=1)), NN)
-    turned = []
-    for m in range(8):
-        part = lanes(third, m)
-        real, imag = part[:edge], part[edge:]
-        turned.append(
-            jnp.concatenate(
-                [2.0 * (real * cosine - imag * sine), 2.0 * (imag * cosine + real * sine)], axis=1
-            )
-        )
-    last = dot3(backward, split(jnp.concatenate(turned, axis=0)), NT)
-    for plane in range(2):
-        for m in range(8):
-            out_ref[pl.ds(plane * 8 + m, edge, stride=16), :] = lanes(last, m)[
-                plane * edge : (plane + 1) * edge
-            ]
+        value = dot3(backward, split(value), NN)
+        value = dot3(backward, split(rotate(value, -1, twist_ref[2], twist_ref[3])), NT)
+        for place, m in enumerate(lines(group)):
+            for plane, part in enumerate(lanes(value, place)):
+                out_ref[pl.ds(plane * 8 + m, edge, stride=16), :] = part
     save.wait()
 
 
@@ -311,6 +310,7 @@
         out_specs=(HBM, VMEM),
         scratch_shapes=[
             pltpu.VMEM(gain.shape, F32),
+            pltpu.VMEM(past.shape, F32),
             pltpu.VMEM(past.shape, F32),
             pltpu.VMEM(modes, F32),
             pltpu.SemaphoreType.DMA((3,)),
@@ -457,14 +457,15 @@
     depth_len = cells * depth_size
     place = lax.axis_index("depth")
     me = place.reshape(1)
-    lines, source = [], fault_slip
-    for column, width in FORWARD:
-        blocks = [
-            lax.dynamic_slice(source, ((place ^ k) * edge, column), (edge, width))
-            for k in range(depth_size)
-        ]
-        source, *blocks = lax.optimization_barrier((source, *blocks))
-        lines.append(exchange(blocks, depth_size))
+    block = lambda source, k, part: lax.dynamic_slice(
+        source, ((place ^ k) * edge, part[0]), (edge, part[1])
+    )
+    far = [block(fault_slip, k, FORWARD[0]) for k in (2, 3)]
+    source, *far = lax.optimization_barrier((fault_slip, *far))
+    near = [block(source, k, FORWARD[0]) for k in (0, 1)]
+    lines = [exchange(near + far, depth_size)]
+    for part in FORWARD[1:]:
+        lines.append(exchange([block(source, k, part) for k in range(depth_size)], depth_size))
     tables = depth_tables(depth_len, devices)
     gain, past = past_sum(kernel, history)
     waves = None

time: 96.8 us -> 95.3 us (0.985)
  Pallas kernels: 25.6 us -> 24.5 us
    pallas_call x1, Pallas kernels: 4.1 us -> 2.98 us  [strike_both(): pl.pallas_call(strike_kernel, out_shape=(pltpu.HBM(modes, F32), jax.Shape...]
where the time goes in v4:
time: 95.3 us; the launch traced here: 94.9 us
  starting transfers between devices  26.5 us (28%)
  Pallas kernels  24.5 us (26%)
  blocking collectives  23.3 us (24%)
  waiting for transfers between devices  15.5 us (16%)
  local copies, waits for them, and re-layouts  4.09 us (4%)
  between operations  1.01 us (1%)
    all_to_all x1, blocking collectives, body(): lax.all_to_all(waves.reshape(devices, 16, edge), ALL, 0, 0)  23.3 us
    ppermute x12, starting transfers between devices, exchange(): lax.ppermute(part, 'depth', [(place, place ^ k) for place in range(size)])  17.4 us
    all_to_all x1, waiting for transfers between devices, body(): pencil = lax.all_to_all(waves.reshape(devices, 16, edge), ALL, 0, 0)  10.9 us
    all_to_all x1, starting transfers between devices, body(): pencil = lax.all_to_all(waves.reshape(devices, 16, edge), ALL, 0, 0)  9.06 us
    pallas_call x1, Pallas kernels, past_sum(): pl.pallas_call(past_kernel, grid=(length // block,), out_shape=(pltpu.HBM...  8.27 us
    pallas_call x4, Pallas kernels, friction_finish(): pl.pallas_call(functools.partial(friction_kernel, slots, column), in_spec...  5.56 us
    ppermute x12, waiting for transfers between devices, exchange(): lax.ppermute(part, 'depth', [(place, place ^ k) for place in range(size)])  4.65 us
    pallas_call x2, Pallas kernels, depth_forward(): pl.pallas_call(functools.partial(depth_forward_kernel, first, column), ou...  3.18 us
  transfers between devices with their start and end apart: 13, of which 5 were waited for; matrix products, arithmetic and copies ran while one was open for 1% of the time, Pallas kernels for 18%

profile of v4, /device:TPU:1, one launch (start us, length us, event | category | flops | bytes accessed | tf_op | source)
XLA Modules:
  0.0 94.9 jit_solution(487667985255438543)
XLA Ops:
  0.6 1.0 %constant_dynamic-slice_fusion.6 = (f32[128,256]{1,0:T(8,128)S(1)}, f32[128,256]{1,0:T(8,128)S(1)}) fusion(f32[512,512]{1,0:T(8,128)} %slip_ref.7, s32[]{:T(128)S(6)} %select_n.17, s32[]{:T(128)S(6)} %select_n.16), kind=kLoop, calls=%fused_computation.6 | loop fusion | bytes 524296 | tf_op jit(solution)/shard_map/dynamic_slice | solution.py:460
  1.6 4.5 %collective-permute-start.4 = (f32[128,256]{1,0:T(8,128)S(1)}, f32[128,256]{1,0:T(8,128)S(1)}, u32[]{:S(2)}, u32[]{:S(2)}) collective-permute-start(f32[128,256]{1,0:T(8,128)S(1)} %get-tuple-element.37), channel_id=1, source_target_pairs={{0,2},{1,3},{2,0},{3,1},{4,6},{5,7},{6,4},{7,5},{8,10},{9,11},{10,... | collective-permute-start | bytes 393224 | tf_op jit(solution)/shard_map/ppermute | solution.py:447
  6.1 0.7 collective-permute-start.5
  6.8 1.3 %constant_dynamic-slice_fusion.4 = (f32[128,256]{1,0:T(8,128)S(1)}, f32[128,256]{1,0:T(8,128)S(1)}, f32[128,256]{1,0:T(8,128)S(1)}, f32[128,256]{1,0:T(8,128)S(1...) fusion(f32[512,512]{1,0:T(8,128)} %slip_ref.7, s32[]{:T(128)S(6)} %select_n.19, s32[]{:T(128)S(6)} %select_n.18, ...), kind=kLoop, calls=%fused_computation.4 | loop fusion | bytes 1572880 | tf_op jit(solution)/shard_map/dynamic_slice | solution.py:460
  8.1 0.4 collective-permute-start.3
  8.4 3.2 %collective-permute-start.2 = (f32[128,256]{1,0:T(8,128)S(1)}, f32[128,256]{1,0:T(8,128)S(1)}, u32[]{:S(2)}, u32[]{:S(2)}) collective-permute-start(f32[128,256]{1,0:T(8,128)S(1)} %get-tuple-element.61), channel_id=1, source_target_pairs={{0,3},{1,2},{2,1},{3,0},{4,7},{5,6},{6,5},{7,4},{8,11},{9,10},{10,... | collective-permute-start | bytes 393224 | tf_op jit(solution)/shard_map/ppermute | solution.py:447
  11.7 0.0 collective-permute-start.1
  11.7 0.0 collective-permute-done.4.two_ref
  11.7 0.4 collective-permute-start
  12.1 0.0 copy-start.8
  12.1 1.0 %copy-done.8 = f32[2,128,512]{2,1,0:T(8,128)S(1)} copy-done((f32[2,128,512]{2,1,0:T(8,128)S(1)}, f32[2,128,512]{2,1,0:T(8,128)}, u32[]{:S(2)}) %copy-start.8) | copy-done | bytes 524312
  13.2 0.0 copy-start.9
  13.2 0.8 copy-done.9
  13.9 1.0 %depth_tables.1 = (bf16[4,512,512]{2,1,0:T(8,128)(2,1)S(1)}, bf16[4,512,512]{2,1,0:T(8,128)(2,1)S(1)}) custom-call(f32[2,128,512]{2,1,0:T(8,128)S(1)} %copy-done.8, f32[2,8,512]{2,1,0:T(8,128)S(1)} %copy-done.9), custom_call_target="tpu_custom_call" | custom-call | flops 10000000 | bytes 5000000 | tf_op jit(solution)/shard_map/depth_tables/pallas_call | solution.py:89
  14.9 0.0 copy-start
  15.0 0.0 collective-permute-done.5.three_ref
  15.0 0.0 collective-permute-done.3.one_ref
  15.0 1.0 %depth_forward.2.refs_0_ = f32[16,128,128]{2,1,0:T(8,128)S(1)} custom-call(s32[1]{0:T(128)} %bitcast.me_ref, f32[128,256]{1,0:T(8,128)S(1)} %get-tuple-element.60.own_ref, f32[128,256]{1,0:T(8,128)S(1)} %collective-permute-done.3.one_ref, f32[128,256]{1,0:T(8,128)S(1)} %collective-permute-done.4.two_ref, f32[128,256]{1,0:T(8,128)S(1)} %collective-permute-done.5.three_ref, ...), custom_call_target="tpu_custom_call" | custom-call | flops 1200000000 | bytes 4000000 | tf_op jit(solution)/shard_map/depth_forward/pallas_call | solution.py:144
  16.0 0.3 collective-permute-done.2.three_ref
  16.3 3.0 %collective-permute-done.1.two_ref = f32[128,256]{1,0:T(8,128)S(1)} collective-permute-done((f32[128,256]{1,0:T(8,128)S(1)}, f32[128,256]{1,0:T(8,128)S(1)}, u32[]{:S(2)}, u32[]{:S(2)}) %collective-permute-start.1) | collective-permute-done | bytes 131104 | tf_op jit(solution)/shard_map/ppermute | solution.py:447
  19.3 0.0 collective-permute-done.one_ref
  19.3 2.2 %depth_forward.3 = f32[2048,128]{1,0:T(8,128)} custom-call(s32[1]{0:T(128)} %bitcast.me_ref, f32[128,256]{1,0:T(8,128)S(1)} %get-tuple-element.64.own_ref, f32[128,256]{1,0:T(8,128)S(1)} %collective-permute-done.one_ref, f32[128,256]{1,0:T(8,128)S(1)} %collective-permute-done.1.two_ref, f32[128,256]{1,0:T(8,128)S(1)} %collective-permute-done.2.three_ref, ...), custom_call_target="tpu_custom_call" | custom-call | flops 1200000000 | bytes 4000000 | tf_op jit(solution)/shard_map/depth_forward/pallas_call | solution.py:144
  21.5 0.0 copy-done
  21.5 9.1 %all-to-all-start = ((f32[128,16,128]{2,1,0:T(8,128)}), f32[128,16,128]{2,1,0:T(8,128)S(1)}, u32[]{:S(2)}, u32[]{:S(2)}) async-start(f32[128,16,128]{2,1,0:T(8,128)} %bitcast.1), calls=%async_computation | async-start | bytes 2097152 | tf_op jit(solution)/shard_map/all_to_all | solution.py:474
  30.6 0.0 copy-start.10
  30.6 0.0 copy-start.11
  30.6 8.3 %past_sum.1 = (f32[8,128,128]{2,1,0:T(8,128)}, f32[2,8,128,128]{3,2,1,0:T(8,128)}) custom-call(f32[9,8,16384]{2,1,0:T(8,128)} %kernel_ref.1, f32[8,2,8,16384]{3,2,1,0:T(8,128)} %history_ref.1), custom_call_target="tpu_custom_call" | custom-call | flops 4200000 | bytes 14700000 | tf_op jit(solution)/shard_map/past_sum/pallas_call | solution.py:338
  38.9 10.9 %all-to-all-done = f32[128,16,128]{2,1,0:T(8,128)S(1)} async-done(((f32[128,16,128]{2,1,0:T(8,128)}), f32[128,16,128]{2,1,0:T(8,128)S(1)}, u32[]{:S(2)}, u32[]{:S(2)}) %all-to-all-start) | async-done | bytes 1048608 | tf_op jit(solution)/shard_map/all_to_all | solution.py:474
  49.7 0.0 copy-start.1
  49.7 0.0 copy-done.10
  49.7 0.0 copy-done.11
  49.7 3.0 %strike_both.1 = (f32[2,1024,128]{2,1,0:T(8,128)}, f32[2048,128]{1,0:T(8,128)S(1)}) custom-call(f32[2048,128]{1,0:T(8,128)S(1)} %bitcast.12, f32[8,128,128]{2,1,0:T(8,128)} %get-tuple-element.39.gain_hbm, f32[2,8,128,128]{3,2,1,0:T(8,128)} %get-tuple-element.40.past_hbm, bf16[4,128,128]{2,1,0:T(8,128)(2,1)S(1)} %copy-done.11, f32[4,128,128]{2,1,0:T(8,128)S(1)} %copy-done.10), custom_call_target="tpu_custom_call" | custom-call | flops 1600000000 | bytes 6000000 | tf_op jit(solution)/shard_map/strike_both/pallas_call | solution.py:303
  52.7 23.3 %all_to_all.10 = f32[128,16,128]{2,1,0:T(8,128)S(1)} all-to-all(f32[128,16,128]{2,1,0:T(8,128)S(1)} %bitcast.13), channel_id=1, replica_groups=mesh['strike'=32,'depth'=4] {'strike','depth'}, dimensions={0} | all-to-all | bytes 2097152 | tf_op jit(solution)/shard_map/all_to_all | solution.py:480
  76.0 0.0 copy-done.1
  76.0 0.0 copy-start.2
  76.0 0.0 copy-start.3
  76.0 0.0 copy-start.5
  76.0 0.0 copy-start.6
  76.0 0.0 copy-start.7
  76.0 1.1 %depth_inverse.3 = (f32[128,256]{1,0:T(8,128)S(1)}, f32[128,256]{1,0:T(8,128)S(1)}, f32[128,256]{1,0:T(8,128)S(1)}, f32[128,256]{1,0:T(8,128)S(1)}) custom-call(s32[1]{0:T(128)} %bitcast.me_ref, f32[2048,128]{1,0:T(8,128)S(1)} %bitcast.10, bf16[4,512,512]{2,1,0:T(8,128)(2,1)S(1)} %get-tuple-element.35.high_ref, bf16[4,512,512]{2,1,0:T(8,128)(2,1)S(1)} %copy-done.1), custom_call_target="tpu_custom_call" | custom-call | flops 1200000000 | bytes 4000000 | tf_op jit(solution)/shard_map/depth_inverse/pallas_call | solution.py:208
  77.2 1.3 %collective-permute-start.9 = (f32[128,256]{1,0:T(8,128)S(1)}, f32[128,256]{1,0:T(8,128)S(1)}, u32[]{:S(2)}, u32[]{:S(2)}) collective-permute-start(f32[128,256]{1,0:T(8,128)S(1)} %get-tuple-element.47), channel_id=1, source_target_pairs={{0,1},{1,0},{2,3},{3,2},{4,5},{5,4},{6,7},{7,6},{8,9},{9,8},{10,11... | collective-permute-start | bytes 393224 | tf_op jit(solution)/shard_map/ppermute | solution.py:447
  78.5 0.6 collective-permute-start.10
  79.1 2.6 %collective-permute-start.11 = (f32[128,256]{1,0:T(8,128)S(1)}, f32[128,256]{1,0:T(8,128)S(1)}, u32[]{:S(2)}, u32[]{:S(2)}) collective-permute-start(f32[128,256]{1,0:T(8,128)S(1)} %get-tuple-element.49), channel_id=1, source_target_pairs={{0,3},{1,2},{2,1},{3,0},{4,7},{5,6},{6,5},{7,4},{8,11},{9,10},{10,... | collective-permute-start | bytes 393224 | tf_op jit(solution)/shard_map/ppermute | solution.py:447
  81.7 1.1 %depth_inverse.2 = (f32[128,256]{1,0:T(8,128)S(1)}, f32[128,256]{1,0:T(8,128)S(1)}, f32[128,256]{1,0:T(8,128)S(1)}, f32[128,256]{1,0:T(8,128)S(1)}) custom-call(s32[1]{0:T(128)} %bitcast.me_ref, f32[2048,128]{1,0:T(8,128)S(1)} %bitcast.11, bf16[4,512,512]{2,1,0:T(8,128)(2,1)S(1)} %get-tuple-element.35.high_ref, bf16[4,512,512]{2,1,0:T(8,128)(2,1)S(1)} %copy-done.1), custom_call_target="tpu_custom_call" | custom-call | flops 1200000000 | bytes 4000000 | tf_op jit(solution)/shard_map/depth_inverse/pallas_call | solution.py:208
  82.9 0.2 collective-permute-start.8
  83.1 0.7 collective-permute-start.7
  83.8 0.0 collective-permute-done.9.refs_1_
  83.8 2.8 %collective-permute-start.6 = (f32[128,256]{1,0:T(8,128)S(1)}, f32[128,256]{1,0:T(8,128)S(1)}, u32[]{:S(2)}, u32[]{:S(2)}) collective-permute-start(f32[128,256]{1,0:T(8,128)S(1)} %get-tuple-element.42), channel_id=1, source_target_pairs={{0,3},{1,2},{2,1},{3,0},{4,7},{5,6},{6,5},{7,4},{8,11},{9,10},{10,... | collective-permute-start | bytes 393224 | tf_op jit(solution)/shard_map/ppermute | solution.py:447
  86.6 0.0 copy-done.2
  86.6 0.0 copy-done.3
  86.6 0.0 copy-done.5
  86.6 0.0 copy-done.6
  86.6 0.0 copy-done.7
  86.6 1.2 %friction_start.1 = (f32[512,512]{1,0:T(8,128)S(1)}, f32[512,512]{1,0:T(8,128)S(1)}, f32[512,512]{1,0:T(8,128)S(1)}) custom-call(f32[512,512]{1,0:T(8,128)S(1)} %copy-done.5, f32[512,512]{1,0:T(8,128)S(1)} %copy-done.6, f32[512,512]{1,0:T(8,128)S(1)} %copy-done.7, f32[512,512]{1,0:T(8,128)S(1)} %copy-done.2, f32[512,512]{1,0:T(8,128)S(1)} %copy-done.3), custom_call_target="tpu_custom_call" | custom-call | flops 20000000 | bytes 8000000 | tf_op jit(solution)/shard_map/friction_start/pallas_call | solution.py:386
  87.8 0.0 collective-permute-done.10.refs_2_
  87.8 0.7 collective-permute-done.11.refs_3_
  88.5 0.0 copy-done.4
  88.5 2.0 %friction_finish.4 = (f32[512,512]{1,0:T(8,128)}, f32[512,512]{1,0:T(8,128)}) custom-call(s32[1]{0:T(128)} %bitcast.me_ref, f32[512,512]{1,0:T(8,128)S(1)} %get-tuple-element.31.scale_ref, f32[512,512]{1,0:T(8,128)S(1)} %get-tuple-element.32.rest_ref, f32[512,512]{1,0:T(8,128)S(1)} %get-tuple-element.33.gain_ref, f32[512,512]{1,0:T(8,128)S(1)} %copy-done.2, ...), custom_call_target="tpu_custom_call" | custom-call | flops 20000000 | bytes 5000000 | tf_op jit(solution)/shard_map/friction_finish/pallas_call | solution.py:429
  90.6 0.0 collective-permute-done.8.refs_1_
  90.6 1.4 %friction_finish.5 = (f32[512,512]{1,0:T(8,128)}, f32[512,512]{1,0:T(8,128)}) custom-call(s32[1]{0:T(128)} %bitcast.me_ref, f32[512,512]{1,0:T(8,128)S(1)} %get-tuple-element.31.scale_ref, f32[512,512]{1,0:T(8,128)S(1)} %get-tuple-element.32.rest_ref, f32[512,512]{1,0:T(8,128)S(1)} %get-tuple-element.33.gain_ref, ...), custom_call_target="tpu_custom_call", output_to_operand_aliasing={{0}: (9, {}), {1}: (10, {})} | custom-call | flops 20000000 | bytes 5000000 | tf_op jit(solution)/shard_map/friction_finish/pallas_call | solution.py:429
  92.0 0.0 collective-permute-done.7.refs_0_
  92.0 1.1 %friction_finish.6 = (f32[512,512]{1,0:T(8,128)}, f32[512,512]{1,0:T(8,128)}) custom-call(s32[1]{0:T(128)} %bitcast.me_ref, f32[512,512]{1,0:T(8,128)S(1)} %get-tuple-element.31.scale_ref, f32[512,512]{1,0:T(8,128)S(1)} %get-tuple-element.32.rest_ref, f32[512,512]{1,0:T(8,128)S(1)} %get-tuple-element.33.gain_ref, ...), custom_call_target="tpu_custom_call", output_to_operand_aliasing={{0}: (8, {}), {1}: (9, {})} | custom-call | flops 20000000 | bytes 5000000 | tf_op jit(solution)/shard_map/friction_finish/pallas_call | solution.py:429
  93.1 0.6 collective-permute-done.6.refs_0_
  93.6 1.1 %friction_finish.7 = (f32[512,512]{1,0:T(8,128)}, f32[512,512]{1,0:T(8,128)}) custom-call(s32[1]{0:T(128)} %bitcast.me_ref, f32[512,512]{1,0:T(8,128)S(1)} %get-tuple-element.31.scale_ref, f32[512,512]{1,0:T(8,128)S(1)} %get-tuple-element.32.rest_ref, f32[512,512]{1,0:T(8,128)S(1)} %get-tuple-element.33.gain_ref, ...), custom_call_target="tpu_custom_call", output_to_operand_aliasing={{0}: (8, {}), {1}: (9, {})} | custom-call | flops 20000000 | bytes 5000000 | tf_op jit(solution)/shard_map/friction_finish/pallas_call | solution.py:429
  (1 shorter events, 0.0 us)
Async XLA Ops:
  1.6 10.1 %collective-permute-start.4 = (f32[128,256]{1,0:T(8,128)S(1)}, f32[128,256]{1,0:T(8,128)S(1)}, u32[]{:S(2)}, u32[]{:S(2)}) collective-permute-start(f32[128,256]{1,0:T(8,128)S(1)} %get-tuple-element.37), channel_id=1, source_target_pairs={{0,2},{1,3},{2,0},{3,1},{4,6},{5,7},{6,4},{7,5},{8,10},{9,11},{10,... | collective-permute-start | bytes 393224 | tf_op jit(solution)/shard_map/ppermute | solution.py:447
  6.1 8.8 %collective-permute-start.5 = (f32[128,256]{1,0:T(8,128)S(1)}, f32[128,256]{1,0:T(8,128)S(1)}, u32[]{:S(2)}, u32[]{:S(2)}) collective-permute-start(f32[128,256]{1,0:T(8,128)S(1)} %get-tuple-element.38), channel_id=1, source_target_pairs={{0,3},{1,2},{2,1},{3,0},{4,7},{5,6},{6,5},{7,4},{8,11},{9,10},{10,... | collective-permute-start | bytes 393224 | tf_op jit(solution)/shard_map/ppermute | solution.py:447
  8.1 6.9 %collective-permute-start.3 = (f32[128,256]{1,0:T(8,128)S(1)}, f32[128,256]{1,0:T(8,128)S(1)}, u32[]{:S(2)}, u32[]{:S(2)}) collective-permute-start(f32[128,256]{1,0:T(8,128)S(1)} %get-tuple-element.59), channel_id=1, source_target_pairs={{0,1},{1,0},{2,3},{3,2},{4,5},{5,4},{6,7},{7,6},{8,9},{9,8},{10,11... | collective-permute-start | bytes 393224 | tf_op jit(solution)/shard_map/ppermute | solution.py:447
  8.4 7.8 %collective-permute-start.2 = (f32[128,256]{1,0:T(8,128)S(1)}, f32[128,256]{1,0:T(8,128)S(1)}, u32[]{:S(2)}, u32[]{:S(2)}) collective-permute-start(f32[128,256]{1,0:T(8,128)S(1)} %get-tuple-element.61), channel_id=1, source_target_pairs={{0,3},{1,2},{2,1},{3,0},{4,7},{5,6},{6,5},{7,4},{8,11},{9,10},{10,... | collective-permute-start | bytes 393224 | tf_op jit(solution)/shard_map/ppermute | solution.py:447
  11.7 7.6 %collective-permute-start.1 = (f32[128,256]{1,0:T(8,128)S(1)}, f32[128,256]{1,0:T(8,128)S(1)}, u32[]{:S(2)}, u32[]{:S(2)}) collective-permute-start(f32[128,256]{1,0:T(8,128)S(1)} %get-tuple-element.62), channel_id=1, source_target_pairs={{0,2},{1,3},{2,0},{3,1},{4,6},{5,7},{6,4},{7,5},{8,10},{9,11},{10,... | collective-permute-start | bytes 393224 | tf_op jit(solution)/shard_map/ppermute | solution.py:447
  11.7 7.6 %collective-permute-start = (f32[128,256]{1,0:T(8,128)S(1)}, f32[128,256]{1,0:T(8,128)S(1)}, u32[]{:S(2)}, u32[]{:S(2)}) collective-permute-start(f32[128,256]{1,0:T(8,128)S(1)} %get-tuple-element.63), channel_id=1, source_target_pairs={{0,1},{1,0},{2,3},{3,2},{4,5},{5,4},{6,7},{7,6},{8,9},{9,8},{10,11... | collective-permute-start | bytes 393224 | tf_op jit(solution)/shard_map/ppermute | solution.py:447
  12.1 1.0 %copy-start.8 = (f32[2,128,512]{2,1,0:T(8,128)S(1)}, f32[2,128,512]{2,1,0:T(8,128)}, u32[]{:S(2)}) copy-start(f32[2,128,512]{2,1,0:T(8,128)} %constant.26.clone.coarse_ref) | copy-start | bytes 1572868
  13.2 0.8 copy-start.9
  14.9 6.6 %copy-start = (bf16[4,512,512]{2,1,0:T(8,128)(2,1)}, bf16[4,512,512]{2,1,0:T(8,128)(2,1)S(1)}, u32[]{:S(2)}) copy-start(bf16[4,512,512]{2,1,0:T(8,128)(2,1)S(1)} %get-tuple-element.36.low_ref) | copy-start | bytes 6291460
  21.5 28.2 %all-to-all-start = ((f32[128,16,128]{2,1,0:T(8,128)}), f32[128,16,128]{2,1,0:T(8,128)S(1)}, u32[]{:S(2)}, u32[]{:S(2)}) async-start(f32[128,16,128]{2,1,0:T(8,128)} %bitcast.1), calls=%async_computation | async-start | bytes 2097152 | tf_op jit(solution)/shard_map/all_to_all | solution.py:474
  30.6 19.2 %copy-start.10 = (f32[4,128,128]{2,1,0:T(8,128)S(1)}, f32[4,128,128]{2,1,0:T(8,128)}, u32[]{:S(2)}) copy-start(f32[4,128,128]{2,1,0:T(8,128)} %constant.29.clone.twist_ref) | copy-start | bytes 786436
  30.6 19.2 %copy-start.11 = (bf16[4,128,128]{2,1,0:T(8,128)(2,1)S(1)}, bf16[4,128,128]{2,1,0:T(8,128)(2,1)}, u32[]{:S(2)}) copy-start(bf16[4,128,128]{2,1,0:T(8,128)(2,1)} %constant.28.clone.wave_ref) | copy-start | bytes 393220
  49.7 26.3 %copy-start.1 = (bf16[4,512,512]{2,1,0:T(8,128)(2,1)S(1)}, bf16[4,512,512]{2,1,0:T(8,128)(2,1)}, u32[]{:S(2)}) copy-start(bf16[4,512,512]{2,1,0:T(8,128)(2,1)} %copy-done) | copy-start | bytes 6291460
  76.0 10.6 %copy-start.2 = (f32[512,512]{1,0:T(8,128)S(1)}, f32[512,512]{1,0:T(8,128)}, u32[]{:S(2)}) copy-start(f32[512,512]{1,0:T(8,128)} %strength_ref.9) | copy-start | bytes 3145732
  76.0 10.6 %copy-start.3 = (f32[512,512]{1,0:T(8,128)S(1)}, f32[512,512]{1,0:T(8,128)}, u32[]{:S(2)}) copy-start(f32[512,512]{1,0:T(8,128)} %stress_ref.9) | copy-start | bytes 3145732
  76.0 10.6 %copy-start.5 = (f32[512,512]{1,0:T(8,128)S(1)}, f32[512,512]{1,0:T(8,128)}, u32[]{:S(2)}) copy-start(f32[512,512]{1,0:T(8,128)} %rate_ref.1) | copy-start | bytes 3145732
  76.0 10.6 %copy-start.6 = (f32[512,512]{1,0:T(8,128)S(1)}, f32[512,512]{1,0:T(8,128)}, u32[]{:S(2)}) copy-start(f32[512,512]{1,0:T(8,128)} %state_ref.1) | copy-start | bytes 3145732
  76.0 10.6 %copy-start.7 = (f32[512,512]{1,0:T(8,128)S(1)}, f32[512,512]{1,0:T(8,128)}, u32[]{:S(2)}) copy-start(f32[512,512]{1,0:T(8,128)} %weak_ref.1) | copy-start | bytes 3145732
  77.2 6.6 %collective-permute-start.9 = (f32[128,256]{1,0:T(8,128)S(1)}, f32[128,256]{1,0:T(8,128)S(1)}, u32[]{:S(2)}, u32[]{:S(2)}) collective-permute-start(f32[128,256]{1,0:T(8,128)S(1)} %get-tuple-element.47), channel_id=1, source_target_pairs={{0,1},{1,0},{2,3},{3,2},{4,5},{5,4},{6,7},{7,6},{8,9},{9,8},{10,11... | collective-permute-start | bytes 393224 | tf_op jit(solution)/shard_map/ppermute | solution.py:447
  78.5 9.3 %collective-permute-start.10 = (f32[128,256]{1,0:T(8,128)S(1)}, f32[128,256]{1,0:T(8,128)S(1)}, u32[]{:S(2)}, u32[]{:S(2)}) collective-permute-start(f32[128,256]{1,0:T(8,128)S(1)} %get-tuple-element.48), channel_id=1, source_target_pairs={{0,2},{1,3},{2,0},{3,1},{4,6},{5,7},{6,4},{7,5},{8,10},{9,11},{10,... | collective-permute-start | bytes 393224 | tf_op jit(solution)/shard_map/ppermute | solution.py:447
  79.1 9.4 %copy-start.4 = (f32[512,512]{1,0:T(8,128)S(1)}, f32[512,512]{1,0:T(8,128)}, u32[]{:S(2)}) copy-start(f32[512,512]{1,0:T(8,128)} %slip_ref.7) | copy-start | bytes 3145732
  79.1 9.4 %collective-permute-start.11 = (f32[128,256]{1,0:T(8,128)S(1)}, f32[128,256]{1,0:T(8,128)S(1)}, u32[]{:S(2)}, u32[]{:S(2)}) collective-permute-start(f32[128,256]{1,0:T(8,128)S(1)} %get-tuple-element.49), channel_id=1, source_target_pairs={{0,3},{1,2},{2,1},{3,0},{4,7},{5,6},{6,5},{7,4},{8,11},{9,10},{10,... | collective-permute-start | bytes 393224 | tf_op jit(solution)/shard_map/ppermute | solution.py:447
  82.9 7.7 %collective-permute-start.8 = (f32[128,256]{1,0:T(8,128)S(1)}, f32[128,256]{1,0:T(8,128)S(1)}, u32[]{:S(2)}, u32[]{:S(2)}) collective-permute-start(f32[128,256]{1,0:T(8,128)S(1)} %get-tuple-element.45), channel_id=1, source_target_pairs={{0,1},{1,0},{2,3},{3,2},{4,5},{5,4},{6,7},{7,6},{8,9},{9,8},{10,11... | collective-permute-start | bytes 393224 | tf_op jit(solution)/shard_map/ppermute | solution.py:447
  83.1 8.9 %collective-permute-start.7 = (f32[128,256]{1,0:T(8,128)S(1)}, f32[128,256]{1,0:T(8,128)S(1)}, u32[]{:S(2)}, u32[]{:S(2)}) collective-permute-start(f32[128,256]{1,0:T(8,128)S(1)} %get-tuple-element.43), channel_id=1, source_target_pairs={{0,2},{1,3},{2,0},{3,1},{4,6},{5,7},{6,4},{7,5},{8,10},{9,11},{10,... | collective-permute-start | bytes 393224 | tf_op jit(solution)/shard_map/ppermute | solution.py:447
  83.8 9.9 %collective-permute-start.6 = (f32[128,256]{1,0:T(8,128)S(1)}, f32[128,256]{1,0:T(8,128)S(1)}, u32[]{:S(2)}, u32[]{:S(2)}) collective-permute-start(f32[128,256]{1,0:T(8,128)S(1)} %get-tuple-element.42), channel_id=1, source_target_pairs={{0,3},{1,2},{2,1},{3,0},{4,7},{5,6},{6,5},{7,4},{8,11},{9,10},{10,... | collective-permute-start | bytes 393224 | tf_op jit(solution)/shard_map/ppermute | solution.py:447

commit v5 on v4

--- a/solution.py
+++ b/solution.py
@@ -15,7 +15,7 @@
 RELAXATION = 0.5
 ADVANCE = 0.5
 LAGS = 8
-FORWARD = ((0, 256), (256, 256))
+FORWARD = ((0, 384), (384, 128))
 INVERSE = ((0, 256), (256, 256))
 SLOTS = (((0, 1, 2, 3),), ((0, 1), (2,), (3,)))
 PAIR = 2
@@ -162,37 +162,33 @@
     sigma = (1 - (me & 2)).astype(F32)
 
     def get(cls, plane):
-        return jnp.concatenate(
+        value = jnp.concatenate(
             [y_ref[pl.ds(plane * 8 + half * 4 + cls, blocks, stride=16), :] for half in range(2)],
             axis=0,
         )
-
-    def turn(cls, value):
-        return dot3(split(value), (high_ref[cls, :, cols], low_ref[cls, :, cols]), TN)
+        if cls == 0:
+            first = lax.broadcasted_iota(jnp.int32, value.shape, 0) == 0
+            value = jnp.where(first, 0.5 * value, value)
+        return split(value.T)
+
+    def turn(cls, *lines):
+        left = [
+            jnp.concatenate([jnp.concatenate(line, axis=1) for line in part], axis=0)
+            for part in zip(*[[(a, b) for a, b in zip(*line)] for line in lines])
+        ]
+        return dot3(left, (high_ref[cls, :, cols], low_ref[cls, :, cols]), NN)
+
+    def minus(parts):
+        return [-part for part in parts]
 
     real, imag = get(0, 0), get(0, 1)
-    first = lax.broadcasted_iota(jnp.int32, real.shape, 0) == 0
-    real = jnp.where(first, 0.5 * real, real)
-    imag = jnp.where(first, 0.5 * imag, imag)
-    zero = turn(0, jnp.concatenate([real, -imag], axis=0))
-    two = tau * turn(2, jnp.concatenate([get(2, 0), -get(2, 1)], axis=0))
+    zero = turn(0, (real, minus(imag)))
+    real, imag = get(2, 0), get(2, 1)
+    two = tau * turn(2, (real, minus(imag)))
     real, imag = get(1, 0), get(1, 1)
-    odd = turn(
-        1,
-        jnp.concatenate(
-            [jnp.concatenate([real, -imag], axis=0), jnp.concatenate([-imag, -real], axis=0)], axis=1
-        ),
-    )
+    odd = turn(1, (real, minus(imag)), (minus(imag), minus(real)))
     real, imag = get(3, 0), get(3, 1)
-    odd = sigma * (
-        odd
-        + turn(
-            3,
-            jnp.concatenate(
-                [jnp.concatenate([real, -imag], axis=0), jnp.concatenate([imag, real], axis=0)], axis=1
-            ),
-        )
-    )
+    odd = sigma * (odd + turn(3, (real, minus(imag)), (imag, real)))
     low, high = odd[:rows], odd[rows:]
     base, turned = zero + two, jnp.where(swap, high, low)
     own_ref[...] = base + turned

time: 95.3 us -> 95.1 us (level)
  waiting for transfers between devices: 15.5 us -> 13 us
  starting transfers between devices: 26.5 us -> 27.8 us
    ppermute x12, waiting for transfers between devices: 4.65 us -> 2.17 us  [exchange(): lax.ppermute(part, 'depth', [(place, place ^ k) for place in range(size)])]
    all_to_all x1, starting transfers between devices: 9.06 us -> 10.1 us  [body(): pencil = lax.all_to_all(waves.reshape(devices, 16, edge), ALL, 0, 0)]
    dynamic_slice x2 -> x3, local copies, waits for them, and re-layouts: 2.25 us -> 3.06 us  [body(): lax.dynamic_slice(source, ((place ^ k) * edge, part[0]), (edge, part[1]))]
  transfers between devices with their start and end apart: 13 -> 13, of which waited for: 5 -> 5; matrix products, arithmetic and copies ran while one was open for 1% -> 2% of each run, Pallas kernels for 18% -> 19%
where the time goes in v5:
time: 95.1 us; the launch traced here: 94.5 us
  starting transfers between devices  27.8 us (29%)
  Pallas kernels  24.5 us (26%)
  blocking collectives  23.3 us (25%)
  waiting for transfers between devices  13 us (14%)
  local copies, waits for them, and re-layouts  4.9 us (5%)
  between operations  1.01 us (1%)
    all_to_all x1, blocking collectives, body(): lax.all_to_all(waves.reshape(devices, 16, edge), ALL, 0, 0)  23.3 us
    ppermute x12, starting transfers between devices, exchange(): lax.ppermute(part, 'depth', [(place, place ^ k) for place in range(size)])  17.7 us
    all_to_all x1, waiting for transfers between devices, body(): pencil = lax.all_to_all(waves.reshape(devices, 16, edge), ALL, 0, 0)  10.9 us
    all_to_all x1, starting transfers between devices, body(): pencil = lax.all_to_all(waves.reshape(devices, 16, edge), ALL, 0, 0)  10.1 us
    pallas_call x1, Pallas kernels, past_sum(): pl.pallas_call(past_kernel, grid=(length // block,), out_shape=(pltpu.HBM...  8.27 us
    pallas_call x4, Pallas kernels, friction_finish(): pl.pallas_call(functools.partial(friction_kernel, slots, column), in_spec...  5.56 us
    pallas_call x2, Pallas kernels, depth_forward(): pl.pallas_call(functools.partial(depth_forward_kernel, first, column), ou...  3.37 us
    dynamic_slice x3, local copies, waits for them, and re-layouts, body(): lax.dynamic_slice(source, ((place ^ k) * edge, part[0]), (edge, part[1]))  3.06 us
  transfers between devices with their start and end apart: 13, of which 5 were waited for; matrix products, arithmetic and copies ran while one was open for 2% of the time, Pallas kernels for 19%

profile of v5, /device:TPU:1, one launch (start us, length us, event | category | flops | bytes accessed | tf_op | source)
XLA Modules:
  0.0 94.5 jit_solution(12963889006124333292)
XLA Ops:
  0.6 1.1 %constant_dynamic-slice_fusion.6 = (f32[128,384]{1,0:T(8,128)S(1)}, f32[128,384]{1,0:T(8,128)S(1)}) fusion(f32[512,512]{1,0:T(8,128)} %slip_ref.7, s32[]{:T(128)S(6)} %select_n.17, s32[]{:T(128)S(6)} %select_n.16), kind=kLoop, calls=%fused_computation.6 | loop fusion | bytes 786440 | tf_op jit(solution)/shard_map/dynamic_slice | solution.py:456
  1.7 4.5 %collective-permute-start.4 = (f32[128,384]{1,0:T(8,128)S(1)}, f32[128,384]{1,0:T(8,128)S(1)}, u32[]{:S(2)}, u32[]{:S(2)}) collective-permute-start(f32[128,384]{1,0:T(8,128)S(1)} %get-tuple-element.37), channel_id=1, source_target_pairs={{0,2},{1,3},{2,0},{3,1},{4,6},{5,7},{6,4},{7,5},{8,10},{9,11},{10,... | collective-permute-start | bytes 589832 | tf_op jit(solution)/shard_map/ppermute | solution.py:443
  6.2 0.7 collective-permute-start.5
  6.9 1.0 %constant_dynamic-slice_fusion.4 = (f32[128,384]{1,0:T(8,128)S(1)}, f32[128,384]{1,0:T(8,128)S(1)}) fusion(f32[512,512]{1,0:T(8,128)} %slip_ref.7, s32[]{:T(128)S(6)} %select_n.19, s32[]{:T(128)S(6)} %select_n.18), kind=kLoop, calls=%fused_computation.4 | loop fusion | bytes 786440 | tf_op jit(solution)/shard_map/dynamic_slice | solution.py:456
  7.9 0.4 collective-permute-start.3
  8.3 1.0 %constant_dynamic-slice_fusion = (f32[128,128]{1,0:T(8,128)S(1)}, f32[128,128]{1,0:T(8,128)S(1)}, f32[128,128]{1,0:T(8,128)S(1)}, f32[128,128]{1,0:T(8,128)S(1)}) fusion(f32[512,512]{1,0:T(8,128)} %slip_ref.7, s32[]{:T(128)S(6)} %select_n.17, s32[]{:T(128)S(6)} %select_n.16, s32[]{:T(128)S(6)} %select_n.19, s32[]{:T(128)S(6)} %select_n.18), kind=kLoop, calls=%fused_computation | loop fusion | bytes 524304 | tf_op jit(solution)/shard_map/dynamic_slice | solution.py:456
  9.3 3.3 %collective-permute-start.2 = (f32[128,128]{1,0:T(8,128)S(1)}, f32[128,128]{1,0:T(8,128)S(1)}, u32[]{:S(2)}, u32[]{:S(2)}) collective-permute-start(f32[128,128]{1,0:T(8,128)S(1)} %get-tuple-element.61), channel_id=1, source_target_pairs={{0,3},{1,2},{2,1},{3,0},{4,7},{5,6},{6,5},{7,4},{8,11},{9,10},{10,... | collective-permute-start | bytes 196616 | tf_op jit(solution)/shard_map/ppermute | solution.py:443
  12.6 0.0 collective-permute-start.1
  12.6 0.0 copy-start.8
  12.6 1.0 %copy-done.8 = f32[2,128,512]{2,1,0:T(8,128)S(1)} copy-done((f32[2,128,512]{2,1,0:T(8,128)S(1)}, f32[2,128,512]{2,1,0:T(8,128)}, u32[]{:S(2)}) %copy-start.8) | copy-done | bytes 524312
  13.6 0.0 copy-start.9
  13.6 0.8 copy-done.9
  14.4 1.0 %depth_tables.1 = (bf16[4,512,512]{2,1,0:T(8,128)(2,1)S(1)}, bf16[4,512,512]{2,1,0:T(8,128)(2,1)S(1)}) custom-call(f32[2,128,512]{2,1,0:T(8,128)S(1)} %copy-done.8, f32[2,8,512]{2,1,0:T(8,128)S(1)} %copy-done.9), custom_call_target="tpu_custom_call" | custom-call | flops 10000000 | bytes 5000000 | tf_op jit(solution)/shard_map/depth_tables/pallas_call | solution.py:89
  15.4 0.0 copy-start
  15.4 0.0 collective-permute-done.4.two_ref
  15.4 0.6 collective-permute-start
  16.0 0.2 collective-permute-done.5.three_ref
  16.2 0.0 collective-permute-done.3.one_ref
  16.2 1.5 %depth_forward.2.refs_0_ = f32[16,128,128]{2,1,0:T(8,128)S(1)} custom-call(s32[1]{0:T(128)} %bitcast.me_ref, f32[128,384]{1,0:T(8,128)S(1)} %get-tuple-element.60.own_ref, f32[128,384]{1,0:T(8,128)S(1)} %collective-permute-done.3.one_ref, f32[128,384]{1,0:T(8,128)S(1)} %collective-permute-done.4.two_ref, f32[128,384]{1,0:T(8,128)S(1)} %collective-permute-done.5.three_ref, ...), custom_call_target="tpu_custom_call" | custom-call | flops 1200000000 | bytes 4000000 | tf_op jit(solution)/shard_map/depth_forward/pallas_call | solution.py:144
  17.8 0.0 collective-permute-done.2.three_ref
  17.8 0.6 collective-permute-done.1.two_ref
  18.3 0.0 collective-permute-done.one_ref
  18.4 1.8 %depth_forward.3 = f32[2048,128]{1,0:T(8,128)} custom-call(s32[1]{0:T(128)} %bitcast.me_ref, f32[128,128]{1,0:T(8,128)S(1)} %get-tuple-element.64.own_ref, f32[128,128]{1,0:T(8,128)S(1)} %collective-permute-done.one_ref, f32[128,128]{1,0:T(8,128)S(1)} %collective-permute-done.1.two_ref, f32[128,128]{1,0:T(8,128)S(1)} %collective-permute-done.2.three_ref, ...), custom_call_target="tpu_custom_call" | custom-call | flops 1200000000 | bytes 4000000 | tf_op jit(solution)/shard_map/depth_forward/pallas_call | solution.py:144
  20.2 0.0 copy-done
  20.2 10.1 %all-to-all-start = ((f32[128,16,128]{2,1,0:T(8,128)}), f32[128,16,128]{2,1,0:T(8,128)S(1)}, u32[]{:S(2)}, u32[]{:S(2)}) async-start(f32[128,16,128]{2,1,0:T(8,128)} %bitcast.1), calls=%async_computation | async-start | bytes 2097152 | tf_op jit(solution)/shard_map/all_to_all | solution.py:470
  30.3 0.0 copy-start.10
  30.3 0.0 copy-start.11
  30.3 8.3 %past_sum.1 = (f32[8,128,128]{2,1,0:T(8,128)}, f32[2,8,128,128]{3,2,1,0:T(8,128)}) custom-call(f32[9,8,16384]{2,1,0:T(8,128)} %kernel_ref.1, f32[8,2,8,16384]{3,2,1,0:T(8,128)} %history_ref.1), custom_call_target="tpu_custom_call" | custom-call | flops 4200000 | bytes 14700000 | tf_op jit(solution)/shard_map/past_sum/pallas_call | solution.py:334
  38.6 10.9 %all-to-all-done = f32[128,16,128]{2,1,0:T(8,128)S(1)} async-done(((f32[128,16,128]{2,1,0:T(8,128)}), f32[128,16,128]{2,1,0:T(8,128)S(1)}, u32[]{:S(2)}, u32[]{:S(2)}) %all-to-all-start) | async-done | bytes 1048608 | tf_op jit(solution)/shard_map/all_to_all | solution.py:470
  49.5 0.0 copy-start.1
  49.5 0.0 copy-done.10
  49.5 0.0 copy-done.11
  49.5 3.0 %strike_both.1 = (f32[2,1024,128]{2,1,0:T(8,128)}, f32[2048,128]{1,0:T(8,128)S(1)}) custom-call(f32[2048,128]{1,0:T(8,128)S(1)} %bitcast.12, f32[8,128,128]{2,1,0:T(8,128)} %get-tuple-element.39.gain_hbm, f32[2,8,128,128]{3,2,1,0:T(8,128)} %get-tuple-element.40.past_hbm, bf16[4,128,128]{2,1,0:T(8,128)(2,1)S(1)} %copy-done.11, f32[4,128,128]{2,1,0:T(8,128)S(1)} %copy-done.10), custom_call_target="tpu_custom_call" | custom-call | flops 1600000000 | bytes 6000000 | tf_op jit(solution)/shard_map/strike_both/pallas_call | solution.py:299
  52.5 23.3 %all_to_all.10 = f32[128,16,128]{2,1,0:T(8,128)S(1)} all-to-all(f32[128,16,128]{2,1,0:T(8,128)S(1)} %bitcast.13), channel_id=1, replica_groups=mesh['strike'=32,'depth'=4] {'strike','depth'}, dimensions={0} | all-to-all | bytes 2097152 | tf_op jit(solution)/shard_map/all_to_all | solution.py:476
  75.7 0.0 copy-done.1
  75.7 0.0 copy-start.2
  75.7 0.0 copy-start.3
  75.7 0.0 copy-start.6
  75.8 0.0 copy-start.7
  75.8 1.1 %depth_inverse.3 = (f32[128,256]{1,0:T(8,128)S(1)}, f32[128,256]{1,0:T(8,128)S(1)}, f32[128,256]{1,0:T(8,128)S(1)}, f32[128,256]{1,0:T(8,128)S(1)}) custom-call(s32[1]{0:T(128)} %bitcast.me_ref, f32[2048,128]{1,0:T(8,128)S(1)} %bitcast.10, bf16[4,512,512]{2,1,0:T(8,128)(2,1)S(1)} %get-tuple-element.35.high_ref, bf16[4,512,512]{2,1,0:T(8,128)(2,1)S(1)} %copy-done.1), custom_call_target="tpu_custom_call" | custom-call | flops 1200000000 | bytes 4000000 | tf_op jit(solution)/shard_map/depth_inverse/pallas_call | solution.py:204
  76.9 1.3 %collective-permute-start.9 = (f32[128,256]{1,0:T(8,128)S(1)}, f32[128,256]{1,0:T(8,128)S(1)}, u32[]{:S(2)}, u32[]{:S(2)}) collective-permute-start(f32[128,256]{1,0:T(8,128)S(1)} %get-tuple-element.47), channel_id=1, source_target_pairs={{0,1},{1,0},{2,3},{3,2},{4,5},{5,4},{6,7},{7,6},{8,9},{9,8},{10,11... | collective-permute-start | bytes 393224 | tf_op jit(solution)/shard_map/ppermute | solution.py:443
  78.1 0.6 collective-permute-start.10
  78.8 2.6 %collective-permute-start.11 = (f32[128,256]{1,0:T(8,128)S(1)}, f32[128,256]{1,0:T(8,128)S(1)}, u32[]{:S(2)}, u32[]{:S(2)}) collective-permute-start(f32[128,256]{1,0:T(8,128)S(1)} %get-tuple-element.49), channel_id=1, source_target_pairs={{0,3},{1,2},{2,1},{3,0},{4,7},{5,6},{6,5},{7,4},{8,11},{9,10},{10,... | collective-permute-start | bytes 393224 | tf_op jit(solution)/shard_map/ppermute | solution.py:443
  81.4 1.1 %depth_inverse.2 = (f32[128,256]{1,0:T(8,128)S(1)}, f32[128,256]{1,0:T(8,128)S(1)}, f32[128,256]{1,0:T(8,128)S(1)}, f32[128,256]{1,0:T(8,128)S(1)}) custom-call(s32[1]{0:T(128)} %bitcast.me_ref, f32[2048,128]{1,0:T(8,128)S(1)} %bitcast.11, bf16[4,512,512]{2,1,0:T(8,128)(2,1)S(1)} %get-tuple-element.35.high_ref, bf16[4,512,512]{2,1,0:T(8,128)(2,1)S(1)} %copy-done.1), custom_call_target="tpu_custom_call" | custom-call | flops 1200000000 | bytes 4000000 | tf_op jit(solution)/shard_map/depth_inverse/pallas_call | solution.py:204
  82.5 0.2 collective-permute-start.8
  82.7 0.6 collective-permute-start.7
  83.3 0.0 collective-permute-done.9.refs_1_
  83.3 2.9 %collective-permute-start.6 = (f32[128,256]{1,0:T(8,128)S(1)}, f32[128,256]{1,0:T(8,128)S(1)}, u32[]{:S(2)}, u32[]{:S(2)}) collective-permute-start(f32[128,256]{1,0:T(8,128)S(1)} %get-tuple-element.42), channel_id=1, source_target_pairs={{0,3},{1,2},{2,1},{3,0},{4,7},{5,6},{6,5},{7,4},{8,11},{9,10},{10,... | collective-permute-start | bytes 393224 | tf_op jit(solution)/shard_map/ppermute | solution.py:443
  86.2 0.0 copy-done.2
  86.2 0.0 copy-done.3
  86.2 0.0 copy-done.5
  86.2 0.0 copy-done.6
  86.2 0.0 copy-done.7
  86.2 1.2 %friction_start.1 = (f32[512,512]{1,0:T(8,128)S(1)}, f32[512,512]{1,0:T(8,128)S(1)}, f32[512,512]{1,0:T(8,128)S(1)}) custom-call(f32[512,512]{1,0:T(8,128)S(1)} %copy-done.5, f32[512,512]{1,0:T(8,128)S(1)} %copy-done.6, f32[512,512]{1,0:T(8,128)S(1)} %copy-done.7, f32[512,512]{1,0:T(8,128)S(1)} %copy-done.2, f32[512,512]{1,0:T(8,128)S(1)} %copy-done.3), custom_call_target="tpu_custom_call" | custom-call | flops 20000000 | bytes 8000000 | tf_op jit(solution)/shard_map/friction_start/pallas_call | solution.py:382
  87.4 0.0 collective-permute-done.10.refs_2_
  87.4 0.8 collective-permute-done.11.refs_3_
  88.2 0.0 copy-done.4
  88.2 2.0 %friction_finish.4 = (f32[512,512]{1,0:T(8,128)}, f32[512,512]{1,0:T(8,128)}) custom-call(s32[1]{0:T(128)} %bitcast.me_ref, f32[512,512]{1,0:T(8,128)S(1)} %get-tuple-element.31.scale_ref, f32[512,512]{1,0:T(8,128)S(1)} %get-tuple-element.32.rest_ref, f32[512,512]{1,0:T(8,128)S(1)} %get-tuple-element.33.gain_ref, f32[512,512]{1,0:T(8,128)S(1)} %copy-done.2, ...), custom_call_target="tpu_custom_call" | custom-call | flops 20000000 | bytes 5000000 | tf_op jit(solution)/shard_map/friction_finish/pallas_call | solution.py:425
  90.2 0.0 collective-permute-done.8.refs_1_
  90.2 1.4 %friction_finish.5 = (f32[512,512]{1,0:T(8,128)}, f32[512,512]{1,0:T(8,128)}) custom-call(s32[1]{0:T(128)} %bitcast.me_ref, f32[512,512]{1,0:T(8,128)S(1)} %get-tuple-element.31.scale_ref, f32[512,512]{1,0:T(8,128)S(1)} %get-tuple-element.32.rest_ref, f32[512,512]{1,0:T(8,128)S(1)} %get-tuple-element.33.gain_ref, ...), custom_call_target="tpu_custom_call", output_to_operand_aliasing={{0}: (9, {}), {1}: (10, {})} | custom-call | flops 20000000 | bytes 5000000 | tf_op jit(solution)/shard_map/friction_finish/pallas_call | solution.py:425
  91.6 0.0 collective-permute-done.7.refs_0_
  91.6 1.1 %friction_finish.6 = (f32[512,512]{1,0:T(8,128)}, f32[512,512]{1,0:T(8,128)}) custom-call(s32[1]{0:T(128)} %bitcast.me_ref, f32[512,512]{1,0:T(8,128)S(1)} %get-tuple-element.31.scale_ref, f32[512,512]{1,0:T(8,128)S(1)} %get-tuple-element.32.rest_ref, f32[512,512]{1,0:T(8,128)S(1)} %get-tuple-element.33.gain_ref, ...), custom_call_target="tpu_custom_call", output_to_operand_aliasing={{0}: (8, {}), {1}: (9, {})} | custom-call | flops 20000000 | bytes 5000000 | tf_op jit(solution)/shard_map/friction_finish/pallas_call | solution.py:425
  92.7 0.6 collective-permute-done.6.refs_0_
  93.3 1.1 %friction_finish.7 = (f32[512,512]{1,0:T(8,128)}, f32[512,512]{1,0:T(8,128)}) custom-call(s32[1]{0:T(128)} %bitcast.me_ref, f32[512,512]{1,0:T(8,128)S(1)} %get-tuple-element.31.scale_ref, f32[512,512]{1,0:T(8,128)S(1)} %get-tuple-element.32.rest_ref, f32[512,512]{1,0:T(8,128)S(1)} %get-tuple-element.33.gain_ref, ...), custom_call_target="tpu_custom_call", output_to_operand_aliasing={{0}: (8, {}), {1}: (9, {})} | custom-call | flops 20000000 | bytes 5000000 | tf_op jit(solution)/shard_map/friction_finish/pallas_call | solution.py:425
  (2 shorter events, 0.0 us)
Async XLA Ops:
  1.7 13.7 %collective-permute-start.4 = (f32[128,384]{1,0:T(8,128)S(1)}, f32[128,384]{1,0:T(8,128)S(1)}, u32[]{:S(2)}, u32[]{:S(2)}) collective-permute-start(f32[128,384]{1,0:T(8,128)S(1)} %get-tuple-element.37), channel_id=1, source_target_pairs={{0,2},{1,3},{2,0},{3,1},{4,6},{5,7},{6,4},{7,5},{8,10},{9,11},{10,... | collective-permute-start | bytes 589832 | tf_op jit(solution)/shard_map/ppermute | solution.py:443
  6.2 10.0 %collective-permute-start.5 = (f32[128,384]{1,0:T(8,128)S(1)}, f32[128,384]{1,0:T(8,128)S(1)}, u32[]{:S(2)}, u32[]{:S(2)}) collective-permute-start(f32[128,384]{1,0:T(8,128)S(1)} %get-tuple-element.38), channel_id=1, source_target_pairs={{0,3},{1,2},{2,1},{3,0},{4,7},{5,6},{6,5},{7,4},{8,11},{9,10},{10,... | collective-permute-start | bytes 589832 | tf_op jit(solution)/shard_map/ppermute | solution.py:443
  7.9 8.3 %collective-permute-start.3 = (f32[128,384]{1,0:T(8,128)S(1)}, f32[128,384]{1,0:T(8,128)S(1)}, u32[]{:S(2)}, u32[]{:S(2)}) collective-permute-start(f32[128,384]{1,0:T(8,128)S(1)} %get-tuple-element.59), channel_id=1, source_target_pairs={{0,1},{1,0},{2,3},{3,2},{4,5},{5,4},{6,7},{7,6},{8,9},{9,8},{10,11... | collective-permute-start | bytes 589832 | tf_op jit(solution)/shard_map/ppermute | solution.py:443
  9.3 8.5 %collective-permute-start.2 = (f32[128,128]{1,0:T(8,128)S(1)}, f32[128,128]{1,0:T(8,128)S(1)}, u32[]{:S(2)}, u32[]{:S(2)}) collective-permute-start(f32[128,128]{1,0:T(8,128)S(1)} %get-tuple-element.61), channel_id=1, source_target_pairs={{0,3},{1,2},{2,1},{3,0},{4,7},{5,6},{6,5},{7,4},{8,11},{9,10},{10,... | collective-permute-start | bytes 196616 | tf_op jit(solution)/shard_map/ppermute | solution.py:443
  12.6 5.8 %collective-permute-start.1 = (f32[128,128]{1,0:T(8,128)S(1)}, f32[128,128]{1,0:T(8,128)S(1)}, u32[]{:S(2)}, u32[]{:S(2)}) collective-permute-start(f32[128,128]{1,0:T(8,128)S(1)} %get-tuple-element.62), channel_id=1, source_target_pairs={{0,2},{1,3},{2,0},{3,1},{4,6},{5,7},{6,4},{7,5},{8,10},{9,11},{10,... | collective-permute-start | bytes 196616 | tf_op jit(solution)/shard_map/ppermute | solution.py:443
  12.6 1.0 %copy-start.8 = (f32[2,128,512]{2,1,0:T(8,128)S(1)}, f32[2,128,512]{2,1,0:T(8,128)}, u32[]{:S(2)}) copy-start(f32[2,128,512]{2,1,0:T(8,128)} %constant.26.clone.coarse_ref) | copy-start | bytes 1572868
  13.6 0.8 copy-start.9
  15.4 4.8 %copy-start = (bf16[4,512,512]{2,1,0:T(8,128)(2,1)}, bf16[4,512,512]{2,1,0:T(8,128)(2,1)S(1)}, u32[]{:S(2)}) copy-start(bf16[4,512,512]{2,1,0:T(8,128)(2,1)S(1)} %get-tuple-element.36.low_ref) | copy-start | bytes 6291460
  15.4 2.9 %collective-permute-start = (f32[128,128]{1,0:T(8,128)S(1)}, f32[128,128]{1,0:T(8,128)S(1)}, u32[]{:S(2)}, u32[]{:S(2)}) collective-permute-start(f32[128,128]{1,0:T(8,128)S(1)} %get-tuple-element.63), channel_id=1, source_target_pairs={{0,1},{1,0},{2,3},{3,2},{4,5},{5,4},{6,7},{7,6},{8,9},{9,8},{10,11... | collective-permute-start | bytes 196616 | tf_op jit(solution)/shard_map/ppermute | solution.py:443
  20.2 29.3 %all-to-all-start = ((f32[128,16,128]{2,1,0:T(8,128)}), f32[128,16,128]{2,1,0:T(8,128)S(1)}, u32[]{:S(2)}, u32[]{:S(2)}) async-start(f32[128,16,128]{2,1,0:T(8,128)} %bitcast.1), calls=%async_computation | async-start | bytes 2097152 | tf_op jit(solution)/shard_map/all_to_all | solution.py:470
  30.3 19.2 %copy-start.10 = (f32[4,128,128]{2,1,0:T(8,128)S(1)}, f32[4,128,128]{2,1,0:T(8,128)}, u32[]{:S(2)}) copy-start(f32[4,128,128]{2,1,0:T(8,128)} %constant.29.clone.twist_ref) | copy-start | bytes 786436
  30.3 19.2 %copy-start.11 = (bf16[4,128,128]{2,1,0:T(8,128)(2,1)S(1)}, bf16[4,128,128]{2,1,0:T(8,128)(2,1)}, u32[]{:S(2)}) copy-start(bf16[4,128,128]{2,1,0:T(8,128)(2,1)} %constant.28.clone.wave_ref) | copy-start | bytes 393220
  49.5 26.3 %copy-start.1 = (bf16[4,512,512]{2,1,0:T(8,128)(2,1)S(1)}, bf16[4,512,512]{2,1,0:T(8,128)(2,1)}, u32[]{:S(2)}) copy-start(bf16[4,512,512]{2,1,0:T(8,128)(2,1)} %copy-done) | copy-start | bytes 6291460
  75.7 10.5 %copy-start.2 = (f32[512,512]{1,0:T(8,128)S(1)}, f32[512,512]{1,0:T(8,128)}, u32[]{:S(2)}) copy-start(f32[512,512]{1,0:T(8,128)} %strength_ref.9) | copy-start | bytes 3145732
  75.7 10.5 %copy-start.3 = (f32[512,512]{1,0:T(8,128)S(1)}, f32[512,512]{1,0:T(8,128)}, u32[]{:S(2)}) copy-start(f32[512,512]{1,0:T(8,128)} %stress_ref.9) | copy-start | bytes 3145732
  75.7 10.5 %copy-start.5 = (f32[512,512]{1,0:T(8,128)S(1)}, f32[512,512]{1,0:T(8,128)}, u32[]{:S(2)}) copy-start(f32[512,512]{1,0:T(8,128)} %rate_ref.1) | copy-start | bytes 3145732
  75.7 10.5 %copy-start.6 = (f32[512,512]{1,0:T(8,128)S(1)}, f32[512,512]{1,0:T(8,128)}, u32[]{:S(2)}) copy-start(f32[512,512]{1,0:T(8,128)} %state_ref.1) | copy-start | bytes 3145732
  75.8 10.5 %copy-start.7 = (f32[512,512]{1,0:T(8,128)S(1)}, f32[512,512]{1,0:T(8,128)}, u32[]{:S(2)}) copy-start(f32[512,512]{1,0:T(8,128)} %weak_ref.1) | copy-start | bytes 3145732
  76.9 6.4 %collective-permute-start.9 = (f32[128,256]{1,0:T(8,128)S(1)}, f32[128,256]{1,0:T(8,128)S(1)}, u32[]{:S(2)}, u32[]{:S(2)}) collective-permute-start(f32[128,256]{1,0:T(8,128)S(1)} %get-tuple-element.47), channel_id=1, source_target_pairs={{0,1},{1,0},{2,3},{3,2},{4,5},{5,4},{6,7},{7,6},{8,9},{9,8},{10,11... | collective-permute-start | bytes 393224 | tf_op jit(solution)/shard_map/ppermute | solution.py:443
  78.1 9.2 %collective-permute-start.10 = (f32[128,256]{1,0:T(8,128)S(1)}, f32[128,256]{1,0:T(8,128)S(1)}, u32[]{:S(2)}, u32[]{:S(2)}) collective-permute-start(f32[128,256]{1,0:T(8,128)S(1)} %get-tuple-element.48), channel_id=1, source_target_pairs={{0,2},{1,3},{2,0},{3,1},{4,6},{5,7},{6,4},{7,5},{8,10},{9,11},{10,... | collective-permute-start | bytes 393224 | tf_op jit(solution)/shard_map/ppermute | solution.py:443
  78.7 9.4 %copy-start.4 = (f32[512,512]{1,0:T(8,128)S(1)}, f32[512,512]{1,0:T(8,128)}, u32[]{:S(2)}) copy-start(f32[512,512]{1,0:T(8,128)} %slip_ref.7) | copy-start | bytes 3145732
  78.8 9.4 %collective-permute-start.11 = (f32[128,256]{1,0:T(8,128)S(1)}, f32[128,256]{1,0:T(8,128)S(1)}, u32[]{:S(2)}, u32[]{:S(2)}) collective-permute-start(f32[128,256]{1,0:T(8,128)S(1)} %get-tuple-element.49), channel_id=1, source_target_pairs={{0,3},{1,2},{2,1},{3,0},{4,7},{5,6},{6,5},{7,4},{8,11},{9,10},{10,... | collective-permute-start | bytes 393224 | tf_op jit(solution)/shard_map/ppermute | solution.py:443
  82.5 7.8 %collective-permute-start.8 = (f32[128,256]{1,0:T(8,128)S(1)}, f32[128,256]{1,0:T(8,128)S(1)}, u32[]{:S(2)}, u32[]{:S(2)}) collective-permute-start(f32[128,256]{1,0:T(8,128)S(1)} %get-tuple-element.45), channel_id=1, source_target_pairs={{0,1},{1,0},{2,3},{3,2},{4,5},{5,4},{6,7},{7,6},{8,9},{9,8},{10,11... | collective-permute-start | bytes 393224 | tf_op jit(solution)/shard_map/ppermute | solution.py:443
  82.7 8.9 %collective-permute-start.7 = (f32[128,256]{1,0:T(8,128)S(1)}, f32[128,256]{1,0:T(8,128)S(1)}, u32[]{:S(2)}, u32[]{:S(2)}) collective-permute-start(f32[128,256]{1,0:T(8,128)S(1)} %get-tuple-element.43), channel_id=1, source_target_pairs={{0,2},{1,3},{2,0},{3,1},{4,6},{5,7},{6,4},{7,5},{8,10},{9,11},{10,... | collective-permute-start | bytes 393224 | tf_op jit(solution)/shard_map/ppermute | solution.py:443
  83.3 10.0 %collective-permute-start.6 = (f32[128,256]{1,0:T(8,128)S(1)}, f32[128,256]{1,0:T(8,128)S(1)}, u32[]{:S(2)}, u32[]{:S(2)}) collective-permute-start(f32[128,256]{1,0:T(8,128)S(1)} %get-tuple-element.42), channel_id=1, source_target_pairs={{0,3},{1,2},{2,1},{3,0},{4,7},{5,6},{6,5},{7,4},{8,11},{9,10},{10,... | collective-permute-start | bytes 393224 | tf_op jit(solution)/shard_map/ppermute | solution.py:443

commit v6 on v5

--- a/solution.py
+++ b/solution.py
@@ -260,35 +260,47 @@
                 rows.append([real * cosine - imag * sine, imag * cosine + real * sine])
         return jnp.concatenate([jnp.concatenate(row, axis=1) for row in rows], axis=0)
 
+    groups = 8 // PAIR
     forward = (block(1, 0), block(1, 1))
-    for group in range(8 // PAIR):
-        value = jnp.concatenate([gather(m) for m in lines(group)], axis=1)
-        value = dot3(forward, split(value), NN)
-        value = dot3(forward, split(rotate(value, 1, twist_ref[0], twist_ref[1])), NT)
-        for place, m in enumerate(lines(group)):
-            for plane, part in enumerate(lanes(value, place)):
-                held_ref[plane, m] = part
-                modes_ref[plane, pl.ds(m, edge, stride=8), :] = part
+    kept = None
+    for group in range(groups + 1):
+        before, kept = kept, None
+        if group < groups:
+            value = jnp.concatenate([gather(m) for m in lines(group)], axis=1)
+            kept = dot3(forward, split(value), NN)
+        if group > 0:
+            value = dot3(forward, split(rotate(before, 1, twist_ref[0], twist_ref[1])), NT)
+            for place, m in enumerate(lines(group - 1)):
+                for plane, part in enumerate(lanes(value, place)):
+                    held_ref[plane, m] = part
+                    modes_ref[plane, pl.ds(m, edge, stride=8), :] = part
     save = pltpu.make_async_copy(modes_ref, modes_hbm, sems.at[2])
     save.start()
     for load in loads:
         load.wait()
     backward = (block(-1, 0), block(-1, 1))
-    for group in range(8 // PAIR):
-        value = jnp.concatenate(
-            [
-                jnp.concatenate(
-                    [gain_ref[m] * held_ref[plane, m] + past_ref[plane, m] for plane in range(2)], axis=0
-                )
-                for m in lines(group)
-            ],
-            axis=1,
-        )
-        value = dot3(backward, split(value), NN)
-        value = dot3(backward, split(rotate(value, -1, twist_ref[2], twist_ref[3])), NT)
-        for place, m in enumerate(lines(group)):
-            for plane, part in enumerate(lanes(value, place)):
-                out_ref[pl.ds(plane * 8 + m, edge, stride=16), :] = part
+    for group in range(groups + 1):
+        before, kept = kept, None
+        if group < groups:
+            value = jnp.concatenate(
+                [
+                    jnp.concatenate(
+                        [
+                            gain_ref[m] * held_ref[plane, m] + past_ref[plane, m]
+                            for plane in range(2)
+                        ],
+                        axis=0,
+                    )
+                    for m in lines(group)
+                ],
+                axis=1,
+            )
+            kept = dot3(backward, split(value), NN)
+        if group > 0:
+            value = dot3(backward, split(rotate(before, -1, twist_ref[2], twist_ref[3])), NT)
+            for place, m in enumerate(lines(group - 1)):
+                for plane, part in enumerate(lanes(value, place)):
+                    out_ref[pl.ds(plane * 8 + m, edge, stride=16), :] = part
     save.wait()
 
 

time: 95.1 us -> 95 us (level)
  no operation moved by 1% of the time
where the time goes in v6:
time: 95 us; the launch traced here: 94.5 us
  starting transfers between devices  27.8 us (29%)
  Pallas kernels  24.5 us (26%)
  blocking collectives  23.3 us (25%)
  waiting for transfers between devices  13 us (14%)
  local copies, waits for them, and re-layouts  4.9 us (5%)
  between operations  1.01 us (1%)
    all_to_all x1, blocking collectives, body(): lax.all_to_all(waves.reshape(devices, 16, edge), ALL, 0, 0)  23.3 us
    ppermute x12, starting transfers between devices, exchange(): lax.ppermute(part, 'depth', [(place, place ^ k) for place in range(size)])  17.7 us
    all_to_all x1, waiting for transfers between devices, body(): pencil = lax.all_to_all(waves.reshape(devices, 16, edge), ALL, 0, 0)  10.9 us
    all_to_all x1, starting transfers between devices, body(): pencil = lax.all_to_all(waves.reshape(devices, 16, edge), ALL, 0, 0)  10.1 us
    pallas_call x1, Pallas kernels, past_sum(): pl.pallas_call(past_kernel, grid=(length // block,), out_shape=(pltpu.HBM...  8.27 us
    pallas_call x4, Pallas kernels, friction_finish(): pl.pallas_call(functools.partial(friction_kernel, slots, column), in_spec...  5.56 us
    pallas_call x2, Pallas kernels, depth_forward(): pl.pallas_call(functools.partial(depth_forward_kernel, first, column), ou...  3.37 us
    dynamic_slice x3, local copies, waits for them, and re-layouts, body(): lax.dynamic_slice(source, ((place ^ k) * edge, part[0]), (edge, part[1]))  3.06 us
  transfers between devices with their start and end apart: 13, of which 5 were waited for; matrix products, arithmetic and copies ran while one was open for 2% of the time, Pallas kernels for 19%

profile of v6, /device:TPU:1, one launch (start us, length us, event | category | flops | bytes accessed | tf_op | source)
XLA Modules:
  0.0 94.5 jit_solution(16060314697757453164)
XLA Ops:
  0.6 1.1 %constant_dynamic-slice_fusion.6 = (f32[128,384]{1,0:T(8,128)S(1)}, f32[128,384]{1,0:T(8,128)S(1)}) fusion(f32[512,512]{1,0:T(8,128)} %slip_ref.7, s32[]{:T(128)S(6)} %select_n.17, s32[]{:T(128)S(6)} %select_n.16), kind=kLoop, calls=%fused_computation.6 | loop fusion | bytes 786440 | tf_op jit(solution)/shard_map/dynamic_slice | solution.py:468
  1.7 4.5 %collective-permute-start.4 = (f32[128,384]{1,0:T(8,128)S(1)}, f32[128,384]{1,0:T(8,128)S(1)}, u32[]{:S(2)}, u32[]{:S(2)}) collective-permute-start(f32[128,384]{1,0:T(8,128)S(1)} %get-tuple-element.37), channel_id=1, source_target_pairs={{0,2},{1,3},{2,0},{3,1},{4,6},{5,7},{6,4},{7,5},{8,10},{9,11},{10,... | collective-permute-start | bytes 589832 | tf_op jit(solution)/shard_map/ppermute | solution.py:455
  6.2 0.7 collective-permute-start.5
  6.9 1.0 %constant_dynamic-slice_fusion.4 = (f32[128,384]{1,0:T(8,128)S(1)}, f32[128,384]{1,0:T(8,128)S(1)}) fusion(f32[512,512]{1,0:T(8,128)} %slip_ref.7, s32[]{:T(128)S(6)} %select_n.19, s32[]{:T(128)S(6)} %select_n.18), kind=kLoop, calls=%fused_computation.4 | loop fusion | bytes 786440 | tf_op jit(solution)/shard_map/dynamic_slice | solution.py:468
  7.9 0.4 collective-permute-start.3
  8.3 1.0 %constant_dynamic-slice_fusion = (f32[128,128]{1,0:T(8,128)S(1)}, f32[128,128]{1,0:T(8,128)S(1)}, f32[128,128]{1,0:T(8,128)S(1)}, f32[128,128]{1,0:T(8,128)S(1)}) fusion(f32[512,512]{1,0:T(8,128)} %slip_ref.7, s32[]{:T(128)S(6)} %select_n.17, s32[]{:T(128)S(6)} %select_n.16, s32[]{:T(128)S(6)} %select_n.19, s32[]{:T(128)S(6)} %select_n.18), kind=kLoop, calls=%fused_computation | loop fusion | bytes 524304 | tf_op jit(solution)/shard_map/dynamic_slice | solution.py:468
  9.3 3.3 %collective-permute-start.2 = (f32[128,128]{1,0:T(8,128)S(1)}, f32[128,128]{1,0:T(8,128)S(1)}, u32[]{:S(2)}, u32[]{:S(2)}) collective-permute-start(f32[128,128]{1,0:T(8,128)S(1)} %get-tuple-element.61), channel_id=1, source_target_pairs={{0,3},{1,2},{2,1},{3,0},{4,7},{5,6},{6,5},{7,4},{8,11},{9,10},{10,... | collective-permute-start | bytes 196616 | tf_op jit(solution)/shard_map/ppermute | solution.py:455
  12.6 0.0 collective-permute-start.1
  12.6 0.0 copy-start.8
  12.6 1.0 %copy-done.8 = f32[2,128,512]{2,1,0:T(8,128)S(1)} copy-done((f32[2,128,512]{2,1,0:T(8,128)S(1)}, f32[2,128,512]{2,1,0:T(8,128)}, u32[]{:S(2)}) %copy-start.8) | copy-done | bytes 524312
  13.6 0.0 copy-start.9
  13.6 0.8 copy-done.9
  14.4 1.0 %depth_tables.1 = (bf16[4,512,512]{2,1,0:T(8,128)(2,1)S(1)}, bf16[4,512,512]{2,1,0:T(8,128)(2,1)S(1)}) custom-call(f32[2,128,512]{2,1,0:T(8,128)S(1)} %copy-done.8, f32[2,8,512]{2,1,0:T(8,128)S(1)} %copy-done.9), custom_call_target="tpu_custom_call" | custom-call | flops 10000000 | bytes 5000000 | tf_op jit(solution)/shard_map/depth_tables/pallas_call | solution.py:89
  15.4 0.0 copy-start
  15.4 0.0 collective-permute-done.4.two_ref
  15.4 0.6 collective-permute-start
  16.0 0.2 collective-permute-done.5.three_ref
  16.2 0.0 collective-permute-done.3.one_ref
  16.2 1.5 %depth_forward.2.refs_0_ = f32[16,128,128]{2,1,0:T(8,128)S(1)} custom-call(s32[1]{0:T(128)} %bitcast.me_ref, f32[128,384]{1,0:T(8,128)S(1)} %get-tuple-element.60.own_ref, f32[128,384]{1,0:T(8,128)S(1)} %collective-permute-done.3.one_ref, f32[128,384]{1,0:T(8,128)S(1)} %collective-permute-done.4.two_ref, f32[128,384]{1,0:T(8,128)S(1)} %collective-permute-done.5.three_ref, ...), custom_call_target="tpu_custom_call" | custom-call | flops 1200000000 | bytes 4000000 | tf_op jit(solution)/shard_map/depth_forward/pallas_call | solution.py:144
  17.8 0.0 collective-permute-done.2.three_ref
  17.8 0.6 collective-permute-done.1.two_ref
  18.3 0.0 collective-permute-done.one_ref
  18.4 1.8 %depth_forward.3 = f32[2048,128]{1,0:T(8,128)} custom-call(s32[1]{0:T(128)} %bitcast.me_ref, f32[128,128]{1,0:T(8,128)S(1)} %get-tuple-element.64.own_ref, f32[128,128]{1,0:T(8,128)S(1)} %collective-permute-done.one_ref, f32[128,128]{1,0:T(8,128)S(1)} %collective-permute-done.1.two_ref, f32[128,128]{1,0:T(8,128)S(1)} %collective-permute-done.2.three_ref, ...), custom_call_target="tpu_custom_call" | custom-call | flops 1200000000 | bytes 4000000 | tf_op jit(solution)/shard_map/depth_forward/pallas_call | solution.py:144
  20.2 0.0 copy-done
  20.2 10.1 %all-to-all-start = ((f32[128,16,128]{2,1,0:T(8,128)}), f32[128,16,128]{2,1,0:T(8,128)S(1)}, u32[]{:S(2)}, u32[]{:S(2)}) async-start(f32[128,16,128]{2,1,0:T(8,128)} %bitcast.1), calls=%async_computation | async-start | bytes 2097152 | tf_op jit(solution)/shard_map/all_to_all | solution.py:482
  30.3 0.0 copy-start.10
  30.3 0.0 copy-start.11
  30.3 8.3 %past_sum.1 = (f32[8,128,128]{2,1,0:T(8,128)}, f32[2,8,128,128]{3,2,1,0:T(8,128)}) custom-call(f32[9,8,16384]{2,1,0:T(8,128)} %kernel_ref.1, f32[8,2,8,16384]{3,2,1,0:T(8,128)} %history_ref.1), custom_call_target="tpu_custom_call" | custom-call | flops 4200000 | bytes 14700000 | tf_op jit(solution)/shard_map/past_sum/pallas_call | solution.py:346
  38.6 10.9 %all-to-all-done = f32[128,16,128]{2,1,0:T(8,128)S(1)} async-done(((f32[128,16,128]{2,1,0:T(8,128)}), f32[128,16,128]{2,1,0:T(8,128)S(1)}, u32[]{:S(2)}, u32[]{:S(2)}) %all-to-all-start) | async-done | bytes 1048608 | tf_op jit(solution)/shard_map/all_to_all | solution.py:482
  49.5 0.0 copy-start.1
  49.5 0.0 copy-done.10
  49.5 0.0 copy-done.11
  49.5 2.9 %strike_both.1 = (f32[2,1024,128]{2,1,0:T(8,128)}, f32[2048,128]{1,0:T(8,128)S(1)}) custom-call(f32[2048,128]{1,0:T(8,128)S(1)} %bitcast.12, f32[8,128,128]{2,1,0:T(8,128)} %get-tuple-element.39.gain_hbm, f32[2,8,128,128]{3,2,1,0:T(8,128)} %get-tuple-element.40.past_hbm, bf16[4,128,128]{2,1,0:T(8,128)(2,1)S(1)} %copy-done.11, f32[4,128,128]{2,1,0:T(8,128)S(1)} %copy-done.10), custom_call_target="tpu_custom_call" | custom-call | flops 1600000000 | bytes 6000000 | tf_op jit(solution)/shard_map/strike_both/pallas_call | solution.py:311
  52.4 23.3 %all_to_all.10 = f32[128,16,128]{2,1,0:T(8,128)S(1)} all-to-all(f32[128,16,128]{2,1,0:T(8,128)S(1)} %bitcast.13), channel_id=1, replica_groups=mesh['strike'=32,'depth'=4] {'strike','depth'}, dimensions={0} | all-to-all | bytes 2097152 | tf_op jit(solution)/shard_map/all_to_all | solution.py:488
  75.7 0.0 copy-done.1
  75.7 0.0 copy-start.2
  75.7 0.0 copy-start.3
  75.7 0.0 copy-start.6
  75.7 0.0 copy-start.7
  75.7 1.1 %depth_inverse.3 = (f32[128,256]{1,0:T(8,128)S(1)}, f32[128,256]{1,0:T(8,128)S(1)}, f32[128,256]{1,0:T(8,128)S(1)}, f32[128,256]{1,0:T(8,128)S(1)}) custom-call(s32[1]{0:T(128)} %bitcast.me_ref, f32[2048,128]{1,0:T(8,128)S(1)} %bitcast.10, bf16[4,512,512]{2,1,0:T(8,128)(2,1)S(1)} %get-tuple-element.35.high_ref, bf16[4,512,512]{2,1,0:T(8,128)(2,1)S(1)} %copy-done.1), custom_call_target="tpu_custom_call" | custom-call | flops 1200000000 | bytes 4000000 | tf_op jit(solution)/shard_map/depth_inverse/pallas_call | solution.py:204
  76.8 1.3 %collective-permute-start.9 = (f32[128,256]{1,0:T(8,128)S(1)}, f32[128,256]{1,0:T(8,128)S(1)}, u32[]{:S(2)}, u32[]{:S(2)}) collective-permute-start(f32[128,256]{1,0:T(8,128)S(1)} %get-tuple-element.47), channel_id=1, source_target_pairs={{0,1},{1,0},{2,3},{3,2},{4,5},{5,4},{6,7},{7,6},{8,9},{9,8},{10,11... | collective-permute-start | bytes 393224 | tf_op jit(solution)/shard_map/ppermute | solution.py:455
  78.1 0.6 collective-permute-start.10
  78.7 2.6 %collective-permute-start.11 = (f32[128,256]{1,0:T(8,128)S(1)}, f32[128,256]{1,0:T(8,128)S(1)}, u32[]{:S(2)}, u32[]{:S(2)}) collective-permute-start(f32[128,256]{1,0:T(8,128)S(1)} %get-tuple-element.49), channel_id=1, source_target_pairs={{0,3},{1,2},{2,1},{3,0},{4,7},{5,6},{6,5},{7,4},{8,11},{9,10},{10,... | collective-permute-start | bytes 393224 | tf_op jit(solution)/shard_map/ppermute | solution.py:455
  81.3 1.1 %depth_inverse.2 = (f32[128,256]{1,0:T(8,128)S(1)}, f32[128,256]{1,0:T(8,128)S(1)}, f32[128,256]{1,0:T(8,128)S(1)}, f32[128,256]{1,0:T(8,128)S(1)}) custom-call(s32[1]{0:T(128)} %bitcast.me_ref, f32[2048,128]{1,0:T(8,128)S(1)} %bitcast.11, bf16[4,512,512]{2,1,0:T(8,128)(2,1)S(1)} %get-tuple-element.35.high_ref, bf16[4,512,512]{2,1,0:T(8,128)(2,1)S(1)} %copy-done.1), custom_call_target="tpu_custom_call" | custom-call | flops 1200000000 | bytes 4000000 | tf_op jit(solution)/shard_map/depth_inverse/pallas_call | solution.py:204
  82.4 0.2 collective-permute-start.8
  82.6 0.7 collective-permute-start.7
  83.3 0.0 collective-permute-done.9.refs_1_
  83.3 2.8 %collective-permute-start.6 = (f32[128,256]{1,0:T(8,128)S(1)}, f32[128,256]{1,0:T(8,128)S(1)}, u32[]{:S(2)}, u32[]{:S(2)}) collective-permute-start(f32[128,256]{1,0:T(8,128)S(1)} %get-tuple-element.42), channel_id=1, source_target_pairs={{0,3},{1,2},{2,1},{3,0},{4,7},{5,6},{6,5},{7,4},{8,11},{9,10},{10,... | collective-permute-start | bytes 393224 | tf_op jit(solution)/shard_map/ppermute | solution.py:455
  86.1 0.0 copy-done.2
  86.1 0.0 copy-done.3
  86.1 0.0 copy-done.5
  86.1 0.0 copy-done.6
  86.1 0.0 copy-done.7
  86.1 1.2 %friction_start.1 = (f32[512,512]{1,0:T(8,128)S(1)}, f32[512,512]{1,0:T(8,128)S(1)}, f32[512,512]{1,0:T(8,128)S(1)}) custom-call(f32[512,512]{1,0:T(8,128)S(1)} %copy-done.5, f32[512,512]{1,0:T(8,128)S(1)} %copy-done.6, f32[512,512]{1,0:T(8,128)S(1)} %copy-done.7, f32[512,512]{1,0:T(8,128)S(1)} %copy-done.2, f32[512,512]{1,0:T(8,128)S(1)} %copy-done.3), custom_call_target="tpu_custom_call" | custom-call | flops 20000000 | bytes 8000000 | tf_op jit(solution)/shard_map/friction_start/pallas_call | solution.py:394
  87.3 0.0 collective-permute-done.10.refs_2_
  87.3 0.8 collective-permute-done.11.refs_3_
  88.1 0.0 copy-done.4
  88.1 2.0 %friction_finish.4 = (f32[512,512]{1,0:T(8,128)}, f32[512,512]{1,0:T(8,128)}) custom-call(s32[1]{0:T(128)} %bitcast.me_ref, f32[512,512]{1,0:T(8,128)S(1)} %get-tuple-element.31.scale_ref, f32[512,512]{1,0:T(8,128)S(1)} %get-tuple-element.32.rest_ref, f32[512,512]{1,0:T(8,128)S(1)} %get-tuple-element.33.gain_ref, f32[512,512]{1,0:T(8,128)S(1)} %copy-done.2, ...), custom_call_target="tpu_custom_call" | custom-call | flops 20000000 | bytes 5000000 | tf_op jit(solution)/shard_map/friction_finish/pallas_call | solution.py:437
  90.2 0.0 collective-permute-done.8.refs_1_
  90.2 1.4 %friction_finish.5 = (f32[512,512]{1,0:T(8,128)}, f32[512,512]{1,0:T(8,128)}) custom-call(s32[1]{0:T(128)} %bitcast.me_ref, f32[512,512]{1,0:T(8,128)S(1)} %get-tuple-element.31.scale_ref, f32[512,512]{1,0:T(8,128)S(1)} %get-tuple-element.32.rest_ref, f32[512,512]{1,0:T(8,128)S(1)} %get-tuple-element.33.gain_ref, ...), custom_call_target="tpu_custom_call", output_to_operand_aliasing={{0}: (9, {}), {1}: (10, {})} | custom-call | flops 20000000 | bytes 5000000 | tf_op jit(solution)/shard_map/friction_finish/pallas_call | solution.py:437
  91.6 0.0 collective-permute-done.7.refs_0_
  91.6 1.1 %friction_finish.6 = (f32[512,512]{1,0:T(8,128)}, f32[512,512]{1,0:T(8,128)}) custom-call(s32[1]{0:T(128)} %bitcast.me_ref, f32[512,512]{1,0:T(8,128)S(1)} %get-tuple-element.31.scale_ref, f32[512,512]{1,0:T(8,128)S(1)} %get-tuple-element.32.rest_ref, f32[512,512]{1,0:T(8,128)S(1)} %get-tuple-element.33.gain_ref, ...), custom_call_target="tpu_custom_call", output_to_operand_aliasing={{0}: (8, {}), {1}: (9, {})} | custom-call | flops 20000000 | bytes 5000000 | tf_op jit(solution)/shard_map/friction_finish/pallas_call | solution.py:437
  92.7 0.6 collective-permute-done.6.refs_0_
  93.2 1.1 %friction_finish.7 = (f32[512,512]{1,0:T(8,128)}, f32[512,512]{1,0:T(8,128)}) custom-call(s32[1]{0:T(128)} %bitcast.me_ref, f32[512,512]{1,0:T(8,128)S(1)} %get-tuple-element.31.scale_ref, f32[512,512]{1,0:T(8,128)S(1)} %get-tuple-element.32.rest_ref, f32[512,512]{1,0:T(8,128)S(1)} %get-tuple-element.33.gain_ref, ...), custom_call_target="tpu_custom_call", output_to_operand_aliasing={{0}: (8, {}), {1}: (9, {})} | custom-call | flops 20000000 | bytes 5000000 | tf_op jit(solution)/shard_map/friction_finish/pallas_call | solution.py:437
  (2 shorter events, 0.0 us)
Async XLA Ops:
  1.7 13.7 %collective-permute-start.4 = (f32[128,384]{1,0:T(8,128)S(1)}, f32[128,384]{1,0:T(8,128)S(1)}, u32[]{:S(2)}, u32[]{:S(2)}) collective-permute-start(f32[128,384]{1,0:T(8,128)S(1)} %get-tuple-element.37), channel_id=1, source_target_pairs={{0,2},{1,3},{2,0},{3,1},{4,6},{5,7},{6,4},{7,5},{8,10},{9,11},{10,... | collective-permute-start | bytes 589832 | tf_op jit(solution)/shard_map/ppermute | solution.py:455
  6.2 10.0 %collective-permute-start.5 = (f32[128,384]{1,0:T(8,128)S(1)}, f32[128,384]{1,0:T(8,128)S(1)}, u32[]{:S(2)}, u32[]{:S(2)}) collective-permute-start(f32[128,384]{1,0:T(8,128)S(1)} %get-tuple-element.38), channel_id=1, source_target_pairs={{0,3},{1,2},{2,1},{3,0},{4,7},{5,6},{6,5},{7,4},{8,11},{9,10},{10,... | collective-permute-start | bytes 589832 | tf_op jit(solution)/shard_map/ppermute | solution.py:455
  7.9 8.3 %collective-permute-start.3 = (f32[128,384]{1,0:T(8,128)S(1)}, f32[128,384]{1,0:T(8,128)S(1)}, u32[]{:S(2)}, u32[]{:S(2)}) collective-permute-start(f32[128,384]{1,0:T(8,128)S(1)} %get-tuple-element.59), channel_id=1, source_target_pairs={{0,1},{1,0},{2,3},{3,2},{4,5},{5,4},{6,7},{7,6},{8,9},{9,8},{10,11... | collective-permute-start | bytes 589832 | tf_op jit(solution)/shard_map/ppermute | solution.py:455
  9.3 8.5 %collective-permute-start.2 = (f32[128,128]{1,0:T(8,128)S(1)}, f32[128,128]{1,0:T(8,128)S(1)}, u32[]{:S(2)}, u32[]{:S(2)}) collective-permute-start(f32[128,128]{1,0:T(8,128)S(1)} %get-tuple-element.61), channel_id=1, source_target_pairs={{0,3},{1,2},{2,1},{3,0},{4,7},{5,6},{6,5},{7,4},{8,11},{9,10},{10,... | collective-permute-start | bytes 196616 | tf_op jit(solution)/shard_map/ppermute | solution.py:455
  12.6 5.8 %collective-permute-start.1 = (f32[128,128]{1,0:T(8,128)S(1)}, f32[128,128]{1,0:T(8,128)S(1)}, u32[]{:S(2)}, u32[]{:S(2)}) collective-permute-start(f32[128,128]{1,0:T(8,128)S(1)} %get-tuple-element.62), channel_id=1, source_target_pairs={{0,2},{1,3},{2,0},{3,1},{4,6},{5,7},{6,4},{7,5},{8,10},{9,11},{10,... | collective-permute-start | bytes 196616 | tf_op jit(solution)/shard_map/ppermute | solution.py:455
  12.6 1.0 %copy-start.8 = (f32[2,128,512]{2,1,0:T(8,128)S(1)}, f32[2,128,512]{2,1,0:T(8,128)}, u32[]{:S(2)}) copy-start(f32[2,128,512]{2,1,0:T(8,128)} %constant.26.clone.coarse_ref) | copy-start | bytes 1572868
  13.6 0.8 copy-start.9
  15.4 4.8 %copy-start = (bf16[4,512,512]{2,1,0:T(8,128)(2,1)}, bf16[4,512,512]{2,1,0:T(8,128)(2,1)S(1)}, u32[]{:S(2)}) copy-start(bf16[4,512,512]{2,1,0:T(8,128)(2,1)S(1)} %get-tuple-element.36.low_ref) | copy-start | bytes 6291460
  15.4 2.9 %collective-permute-start = (f32[128,128]{1,0:T(8,128)S(1)}, f32[128,128]{1,0:T(8,128)S(1)}, u32[]{:S(2)}, u32[]{:S(2)}) collective-permute-start(f32[128,128]{1,0:T(8,128)S(1)} %get-tuple-element.63), channel_id=1, source_target_pairs={{0,1},{1,0},{2,3},{3,2},{4,5},{5,4},{6,7},{7,6},{8,9},{9,8},{10,11... | collective-permute-start | bytes 196616 | tf_op jit(solution)/shard_map/ppermute | solution.py:455
  20.2 29.3 %all-to-all-start = ((f32[128,16,128]{2,1,0:T(8,128)}), f32[128,16,128]{2,1,0:T(8,128)S(1)}, u32[]{:S(2)}, u32[]{:S(2)}) async-start(f32[128,16,128]{2,1,0:T(8,128)} %bitcast.1), calls=%async_computation | async-start | bytes 2097152 | tf_op jit(solution)/shard_map/all_to_all | solution.py:482
  30.3 19.2 %copy-start.10 = (f32[4,128,128]{2,1,0:T(8,128)S(1)}, f32[4,128,128]{2,1,0:T(8,128)}, u32[]{:S(2)}) copy-start(f32[4,128,128]{2,1,0:T(8,128)} %constant.29.clone.twist_ref) | copy-start | bytes 786436
  30.3 19.2 %copy-start.11 = (bf16[4,128,128]{2,1,0:T(8,128)(2,1)S(1)}, bf16[4,128,128]{2,1,0:T(8,128)(2,1)}, u32[]{:S(2)}) copy-start(bf16[4,128,128]{2,1,0:T(8,128)(2,1)} %constant.28.clone.wave_ref) | copy-start | bytes 393220
  49.5 26.2 %copy-start.1 = (bf16[4,512,512]{2,1,0:T(8,128)(2,1)S(1)}, bf16[4,512,512]{2,1,0:T(8,128)(2,1)}, u32[]{:S(2)}) copy-start(bf16[4,512,512]{2,1,0:T(8,128)(2,1)} %copy-done) | copy-start | bytes 6291460
  75.7 10.5 %copy-start.2 = (f32[512,512]{1,0:T(8,128)S(1)}, f32[512,512]{1,0:T(8,128)}, u32[]{:S(2)}) copy-start(f32[512,512]{1,0:T(8,128)} %strength_ref.9) | copy-start | bytes 3145732
  75.7 10.5 %copy-start.3 = (f32[512,512]{1,0:T(8,128)S(1)}, f32[512,512]{1,0:T(8,128)}, u32[]{:S(2)}) copy-start(f32[512,512]{1,0:T(8,128)} %stress_ref.9) | copy-start | bytes 3145732
  75.7 10.5 %copy-start.5 = (f32[512,512]{1,0:T(8,128)S(1)}, f32[512,512]{1,0:T(8,128)}, u32[]{:S(2)}) copy-start(f32[512,512]{1,0:T(8,128)} %rate_ref.1) | copy-start | bytes 3145732
  75.7 10.5 %copy-start.6 = (f32[512,512]{1,0:T(8,128)S(1)}, f32[512,512]{1,0:T(8,128)}, u32[]{:S(2)}) copy-start(f32[512,512]{1,0:T(8,128)} %state_ref.1) | copy-start | bytes 3145732
  75.7 10.5 %copy-start.7 = (f32[512,512]{1,0:T(8,128)S(1)}, f32[512,512]{1,0:T(8,128)}, u32[]{:S(2)}) copy-start(f32[512,512]{1,0:T(8,128)} %weak_ref.1) | copy-start | bytes 3145732
  76.8 6.5 %collective-permute-start.9 = (f32[128,256]{1,0:T(8,128)S(1)}, f32[128,256]{1,0:T(8,128)S(1)}, u32[]{:S(2)}, u32[]{:S(2)}) collective-permute-start(f32[128,256]{1,0:T(8,128)S(1)} %get-tuple-element.47), channel_id=1, source_target_pairs={{0,1},{1,0},{2,3},{3,2},{4,5},{5,4},{6,7},{7,6},{8,9},{9,8},{10,11... | collective-permute-start | bytes 393224 | tf_op jit(solution)/shard_map/ppermute | solution.py:455
  78.1 9.2 %collective-permute-start.10 = (f32[128,256]{1,0:T(8,128)S(1)}, f32[128,256]{1,0:T(8,128)S(1)}, u32[]{:S(2)}, u32[]{:S(2)}) collective-permute-start(f32[128,256]{1,0:T(8,128)S(1)} %get-tuple-element.48), channel_id=1, source_target_pairs={{0,2},{1,3},{2,0},{3,1},{4,6},{5,7},{6,4},{7,5},{8,10},{9,11},{10,... | collective-permute-start | bytes 393224 | tf_op jit(solution)/shard_map/ppermute | solution.py:455
  78.7 9.4 %copy-start.4 = (f32[512,512]{1,0:T(8,128)S(1)}, f32[512,512]{1,0:T(8,128)}, u32[]{:S(2)}) copy-start(f32[512,512]{1,0:T(8,128)} %slip_ref.7) | copy-start | bytes 3145732
  78.7 9.4 %collective-permute-start.11 = (f32[128,256]{1,0:T(8,128)S(1)}, f32[128,256]{1,0:T(8,128)S(1)}, u32[]{:S(2)}, u32[]{:S(2)}) collective-permute-start(f32[128,256]{1,0:T(8,128)S(1)} %get-tuple-element.49), channel_id=1, source_target_pairs={{0,3},{1,2},{2,1},{3,0},{4,7},{5,6},{6,5},{7,4},{8,11},{9,10},{10,... | collective-permute-start | bytes 393224 | tf_op jit(solution)/shard_map/ppermute | solution.py:455
  82.4 7.8 %collective-permute-start.8 = (f32[128,256]{1,0:T(8,128)S(1)}, f32[128,256]{1,0:T(8,128)S(1)}, u32[]{:S(2)}, u32[]{:S(2)}) collective-permute-start(f32[128,256]{1,0:T(8,128)S(1)} %get-tuple-element.45), channel_id=1, source_target_pairs={{0,1},{1,0},{2,3},{3,2},{4,5},{5,4},{6,7},{7,6},{8,9},{9,8},{10,11... | collective-permute-start | bytes 393224 | tf_op jit(solution)/shard_map/ppermute | solution.py:455
  82.6 8.9 %collective-permute-start.7 = (f32[128,256]{1,0:T(8,128)S(1)}, f32[128,256]{1,0:T(8,128)S(1)}, u32[]{:S(2)}, u32[]{:S(2)}) collective-permute-start(f32[128,256]{1,0:T(8,128)S(1)} %get-tuple-element.43), channel_id=1, source_target_pairs={{0,2},{1,3},{2,0},{3,1},{4,6},{5,7},{6,4},{7,5},{8,10},{9,11},{10,... | collective-permute-start | bytes 393224 | tf_op jit(solution)/shard_map/ppermute | solution.py:455
  83.3 9.9 %collective-permute-start.6 = (f32[128,256]{1,0:T(8,128)S(1)}, f32[128,256]{1,0:T(8,128)S(1)}, u32[]{:S(2)}, u32[]{:S(2)}) collective-permute-start(f32[128,256]{1,0:T(8,128)S(1)} %get-tuple-element.42), channel_id=1, source_target_pairs={{0,3},{1,2},{2,1},{3,0},{4,7},{5,6},{6,5},{7,4},{8,11},{9,10},{10,... | collective-permute-start | bytes 393224 | tf_op jit(solution)/shard_map/ppermute | solution.py:455

commit v7 on v6

--- a/solution.py
+++ b/solution.py
@@ -57,6 +57,11 @@
     )
 
 
+def place_of(mode, plane):
+    half, cls = divmod(mode, 4)
+    return (cls % 2) * 8 + plane * 4 + half * 2 + cls // 2
+
+
 def depth_seeds(depth_len, blocks):
     cells = depth_len // 4
     cell = np.arange(cells)
@@ -119,8 +124,17 @@
                 if first:
                     refs[0][slot] = part
                 else:
-                    start = plane * 8 + half * 4 + cls
-                    refs[1][pl.ds(start, blocks, stride=16), :] = part + refs[0][slot]
+                    start = place_of(half * 4 + cls, plane)
+                    refs[2][pl.ds(start, blocks, stride=16), :] = part + refs[0][slot]
+
+    def send(side):
+        if first:
+            return []
+        source = refs[2].reshape(blocks, 16, rows)
+        tiles = pl.ds(side * 8, 8)
+        save = pltpu.make_async_copy(source.at[:, tiles, :], refs[1].at[:, tiles, :], refs[3].at[side])
+        save.start()
+        return [save]
 
     def turn(cls, parts):
         return dot3((high_ref[cls, :, cols], low_ref[cls, :, cols]), parts, NT)
@@ -129,23 +143,28 @@
     for cls, value in ((0, even + odd), (2, tau * (even - odd))):
         res = turn(cls, split(value))
         put(cls, res[:top], -res[top:])
+    saves = send(0)
     parts = split(both)
     res = turn(1, parts)
     put(1, res[:top, :rows] - res[top:, rows:], -(res[top:, :rows] + res[:top, rows:]))
     res = turn(3, parts)
     put(3, res[:top, :rows] + res[top:, rows:], res[:top, rows:] - res[top:, :rows])
+    for save in saves + send(1):
+        save.wait()
 
 
 def depth_forward(column, me, parts, tables, held=None):
     blocks = tables[0].shape[1] // 4
     rows = parts[0].shape[0]
     first = held is None
-    shape = (16, blocks, rows) if first else (blocks * 16, rows)
+    shape = (16, blocks, rows) if first else (blocks, 16, rows)
+    held_rows = [pltpu.VMEM((blocks * 16, rows), F32), pltpu.SemaphoreType.DMA((2,))]
     return pl.pallas_call(
         functools.partial(depth_forward_kernel, first, column),
-        out_shape=jax.ShapeDtypeStruct(shape, F32),
+        out_shape=jax.ShapeDtypeStruct(shape, F32) if first else pltpu.HBM(shape, F32),
         in_specs=[SMEM] + [VMEM] * (6 if first else 7),
-        out_specs=VMEM,
+        out_specs=VMEM if first else HBM,
+        scratch_shapes=[] if first else held_rows,
         compiler_params=pltpu.CompilerParams(vmem_limit_bytes=GRANT),
         name="depth_forward",
         cost_estimate=pl.CostEstimate(flops=1_200_000_000, bytes_accessed=4_000_000, transcendentals=0),
@@ -240,7 +259,7 @@
 
     def gather(m):
         return jnp.concatenate(
-            [x_ref[pl.ds(plane * 8 + m, edge, stride=16), :] for plane in range(2)], axis=0
+            [x_ref[pl.ds(place_of(m, plane), edge, stride=16), :] for plane in range(2)], axis=0
         )
 
     def block(sign, part):
@@ -479,7 +498,7 @@
     waves = None
     for (column, _), parts in zip(FORWARD, lines):
         waves = depth_forward(column, me, parts, tables, waves)
-    pencil = lax.all_to_all(waves.reshape(devices, 16, edge), ALL, 0, 0)
+    pencil = lax.all_to_all(waves, ALL, 0, 0)
     scale = 1.0 / math.sqrt(depth_len * edge * devices)
     modes, waves = strike_both(
         pencil.reshape(devices * 16, edge), gain, past, strike_tables(edge, scale)

time: 95 us -> 94.8 us (level)
  no operation moved by 1% of the time
where the time goes in v7:
time: 94.8 us; the launch traced here: 94.3 us
  starting transfers between devices  27.8 us (29%)
  Pallas kernels  24.1 us (25%)
  blocking collectives  23.3 us (25%)
  waiting for transfers between devices  13.1 us (14%)
  local copies, waits for them, and re-layouts  4.9 us (5%)
  between operations  1.02 us (1%)
    all_to_all x1, blocking collectives, body(): lax.all_to_all(waves.reshape(devices, 16, edge), ALL, 0, 0)  23.3 us
    ppermute x12, starting transfers between devices, exchange(): lax.ppermute(part, 'depth', [(place, place ^ k) for place in range(size)])  17.7 us
    all_to_all x1, waiting for transfers between devices, body(): pencil = lax.all_to_all(waves, ALL, 0, 0)  10.9 us
    all_to_all x1, starting transfers between devices, body(): pencil = lax.all_to_all(waves, ALL, 0, 0)  10.1 us
    pallas_call x1, Pallas kernels, past_sum(): pl.pallas_call(past_kernel, grid=(length // block,), out_shape=(pltpu.HBM...  8.27 us
    pallas_call x4, Pallas kernels, friction_finish(): pl.pallas_call(functools.partial(friction_kernel, slots, column), in_spec...  5.56 us
    pallas_call x2, Pallas kernels, depth_forward(): pl.pallas_call(functools.partial(depth_forward_kernel, first, column), ou...  3.17 us
    dynamic_slice x3, local copies, waits for them, and re-layouts, body(): lax.dynamic_slice(source, ((place ^ k) * edge, part[0]), (edge, part[1]))  3.06 us
  transfers between devices with their start and end apart: 13, of which 5 were waited for; matrix products, arithmetic and copies ran while one was open for 2% of the time, Pallas kernels for 19%

profile of v7, /device:TPU:1, one launch (start us, length us, event | category | flops | bytes accessed | tf_op | source)
XLA Modules:
  0.0 94.3 jit_solution(5879144854492413940)
XLA Ops:
  0.6 1.1 %constant_dynamic-slice_fusion.6 = (f32[128,384]{1,0:T(8,128)S(1)}, f32[128,384]{1,0:T(8,128)S(1)}) fusion(f32[512,512]{1,0:T(8,128)} %slip_ref.7, s32[]{:T(128)S(6)} %select_n.17, s32[]{:T(128)S(6)} %select_n.16), kind=kLoop, calls=%fused_computation.6 | loop fusion | bytes 786440 | tf_op jit(solution)/shard_map/dynamic_slice | solution.py:487
  1.7 4.5 %collective-permute-start.4 = (f32[128,384]{1,0:T(8,128)S(1)}, f32[128,384]{1,0:T(8,128)S(1)}, u32[]{:S(2)}, u32[]{:S(2)}) collective-permute-start(f32[128,384]{1,0:T(8,128)S(1)} %get-tuple-element.37), channel_id=1, source_target_pairs={{0,2},{1,3},{2,0},{3,1},{4,6},{5,7},{6,4},{7,5},{8,10},{9,11},{10,... | collective-permute-start | bytes 589832 | tf_op jit(solution)/shard_map/ppermute | solution.py:474
  6.2 0.7 collective-permute-start.5
  6.9 1.0 %constant_dynamic-slice_fusion.4 = (f32[128,384]{1,0:T(8,128)S(1)}, f32[128,384]{1,0:T(8,128)S(1)}) fusion(f32[512,512]{1,0:T(8,128)} %slip_ref.7, s32[]{:T(128)S(6)} %select_n.19, s32[]{:T(128)S(6)} %select_n.18), kind=kLoop, calls=%fused_computation.4 | loop fusion | bytes 786440 | tf_op jit(solution)/shard_map/dynamic_slice | solution.py:487
  7.9 0.4 collective-permute-start.3
  8.3 1.0 %constant_dynamic-slice_fusion = (f32[128,128]{1,0:T(8,128)S(1)}, f32[128,128]{1,0:T(8,128)S(1)}, f32[128,128]{1,0:T(8,128)S(1)}, f32[128,128]{1,0:T(8,128)S(1)}) fusion(f32[512,512]{1,0:T(8,128)} %slip_ref.7, s32[]{:T(128)S(6)} %select_n.17, s32[]{:T(128)S(6)} %select_n.16, s32[]{:T(128)S(6)} %select_n.19, s32[]{:T(128)S(6)} %select_n.18), kind=kLoop, calls=%fused_computation | loop fusion | bytes 524304 | tf_op jit(solution)/shard_map/dynamic_slice | solution.py:487
  9.3 3.3 %collective-permute-start.2 = (f32[128,128]{1,0:T(8,128)S(1)}, f32[128,128]{1,0:T(8,128)S(1)}, u32[]{:S(2)}, u32[]{:S(2)}) collective-permute-start(f32[128,128]{1,0:T(8,128)S(1)} %get-tuple-element.61), channel_id=1, source_target_pairs={{0,3},{1,2},{2,1},{3,0},{4,7},{5,6},{6,5},{7,4},{8,11},{9,10},{10,... | collective-permute-start | bytes 196616 | tf_op jit(solution)/shard_map/ppermute | solution.py:474
  12.6 0.0 collective-permute-start.1
  12.6 0.0 copy-start.8
  12.6 1.0 %copy-done.8 = f32[2,128,512]{2,1,0:T(8,128)S(1)} copy-done((f32[2,128,512]{2,1,0:T(8,128)S(1)}, f32[2,128,512]{2,1,0:T(8,128)}, u32[]{:S(2)}) %copy-start.8) | copy-done | bytes 524312
  13.6 0.0 copy-start.9
  13.6 0.8 copy-done.9
  14.4 1.0 %depth_tables.1 = (bf16[4,512,512]{2,1,0:T(8,128)(2,1)S(1)}, bf16[4,512,512]{2,1,0:T(8,128)(2,1)S(1)}) custom-call(f32[2,128,512]{2,1,0:T(8,128)S(1)} %copy-done.8, f32[2,8,512]{2,1,0:T(8,128)S(1)} %copy-done.9), custom_call_target="tpu_custom_call" | custom-call | flops 10000000 | bytes 5000000 | tf_op jit(solution)/shard_map/depth_tables/pallas_call | solution.py:94
  15.4 0.0 copy-start
  15.4 0.0 collective-permute-done.4.two_ref
  15.4 0.6 collective-permute-start
  16.0 0.2 collective-permute-done.5.three_ref
  16.2 0.0 collective-permute-done.3.one_ref
  16.2 1.5 %depth_forward.2.refs_0_ = f32[16,128,128]{2,1,0:T(8,128)S(1)} custom-call(s32[1]{0:T(128)} %bitcast.me_ref, f32[128,384]{1,0:T(8,128)S(1)} %get-tuple-element.60.own_ref, f32[128,384]{1,0:T(8,128)S(1)} %collective-permute-done.3.one_ref, f32[128,384]{1,0:T(8,128)S(1)} %collective-permute-done.4.two_ref, f32[128,384]{1,0:T(8,128)S(1)} %collective-permute-done.5.three_ref, ...), custom_call_target="tpu_custom_call" | custom-call | flops 1200000000 | bytes 4000000 | tf_op jit(solution)/shard_map/depth_forward/pallas_call | solution.py:162
  17.7 0.0 collective-permute-done.2.three_ref
  17.7 0.6 collective-permute-done.1.two_ref
  18.3 0.0 collective-permute-done.one_ref
  18.4 0.0 copy-done
  18.4 1.7 %depth_forward.3 = f32[128,16,128]{2,1,0:T(8,128)} custom-call(s32[1]{0:T(128)} %bitcast.me_ref, f32[128,128]{1,0:T(8,128)S(1)} %get-tuple-element.64.own_ref, f32[128,128]{1,0:T(8,128)S(1)} %collective-permute-done.one_ref, f32[128,128]{1,0:T(8,128)S(1)} %collective-permute-done.1.two_ref, f32[128,128]{1,0:T(8,128)S(1)} %collective-permute-done.2.three_ref, ...), custom_call_target="tpu_custom_call" | custom-call | flops 1200000000 | bytes 4000000 | tf_op jit(solution)/shard_map/depth_forward/pallas_call | solution.py:162
  20.0 10.1 %all-to-all-start = ((f32[128,16,128]{2,1,0:T(8,128)}), f32[128,16,128]{2,1,0:T(8,128)S(1)}, u32[]{:S(2)}, u32[]{:S(2)}) async-start(f32[128,16,128]{2,1,0:T(8,128)} %depth_forward.3), calls=%async_computation | async-start | bytes 2097152 | tf_op jit(solution)/shard_map/all_to_all | solution.py:501
  30.1 0.0 copy-start.10
  30.2 0.0 copy-start.11
  30.2 8.3 %past_sum.1 = (f32[8,128,128]{2,1,0:T(8,128)}, f32[2,8,128,128]{3,2,1,0:T(8,128)}) custom-call(f32[9,8,16384]{2,1,0:T(8,128)} %kernel_ref.1, f32[8,2,8,16384]{3,2,1,0:T(8,128)} %history_ref.1), custom_call_target="tpu_custom_call" | custom-call | flops 4200000 | bytes 14700000 | tf_op jit(solution)/shard_map/past_sum/pallas_call | solution.py:365
  38.4 10.9 %all-to-all-done = f32[128,16,128]{2,1,0:T(8,128)S(1)} async-done(((f32[128,16,128]{2,1,0:T(8,128)}), f32[128,16,128]{2,1,0:T(8,128)S(1)}, u32[]{:S(2)}, u32[]{:S(2)}) %all-to-all-start) | async-done | bytes 1048608 | tf_op jit(solution)/shard_map/all_to_all | solution.py:501
  49.3 0.0 copy-start.1
  49.3 0.0 copy-done.10
  49.3 0.0 copy-done.11
  49.3 2.9 %strike_both.1 = (f32[2,1024,128]{2,1,0:T(8,128)}, f32[2048,128]{1,0:T(8,128)S(1)}) custom-call(f32[2048,128]{1,0:T(8,128)S(1)} %bitcast.11, f32[8,128,128]{2,1,0:T(8,128)} %get-tuple-element.39.gain_hbm, f32[2,8,128,128]{3,2,1,0:T(8,128)} %get-tuple-element.40.past_hbm, bf16[4,128,128]{2,1,0:T(8,128)(2,1)S(1)} %copy-done.11, f32[4,128,128]{2,1,0:T(8,128)S(1)} %copy-done.10), custom_call_target="tpu_custom_call" | custom-call | flops 1600000000 | bytes 6000000 | tf_op jit(solution)/shard_map/strike_both/pallas_call | solution.py:330
  52.2 23.3 %all_to_all.10 = f32[128,16,128]{2,1,0:T(8,128)S(1)} all-to-all(f32[128,16,128]{2,1,0:T(8,128)S(1)} %bitcast.12), channel_id=1, replica_groups=mesh['strike'=32,'depth'=4] {'strike','depth'}, dimensions={0} | all-to-all | bytes 2097152 | tf_op jit(solution)/shard_map/all_to_all | solution.py:507
  75.5 0.0 copy-done.1
  75.5 0.0 copy-start.2
  75.5 0.0 copy-start.5
  75.5 0.0 copy-start.6
  75.5 0.0 copy-start.7
  75.5 1.0 %depth_inverse.3 = (f32[128,256]{1,0:T(8,128)S(1)}, f32[128,256]{1,0:T(8,128)S(1)}, f32[128,256]{1,0:T(8,128)S(1)}, f32[128,256]{1,0:T(8,128)S(1)}) custom-call(s32[1]{0:T(128)} %bitcast.me_ref, f32[2048,128]{1,0:T(8,128)S(1)} %bitcast.9, bf16[4,512,512]{2,1,0:T(8,128)(2,1)S(1)} %get-tuple-element.35.high_ref, bf16[4,512,512]{2,1,0:T(8,128)(2,1)S(1)} %copy-done.1), custom_call_target="tpu_custom_call" | custom-call | flops 1200000000 | bytes 4000000 | tf_op jit(solution)/shard_map/depth_inverse/pallas_call | solution.py:223
  76.6 1.3 %collective-permute-start.9 = (f32[128,256]{1,0:T(8,128)S(1)}, f32[128,256]{1,0:T(8,128)S(1)}, u32[]{:S(2)}, u32[]{:S(2)}) collective-permute-start(f32[128,256]{1,0:T(8,128)S(1)} %get-tuple-element.47), channel_id=1, source_target_pairs={{0,1},{1,0},{2,3},{3,2},{4,5},{5,4},{6,7},{7,6},{8,9},{9,8},{10,11... | collective-permute-start | bytes 393224 | tf_op jit(solution)/shard_map/ppermute | solution.py:474
  77.9 0.6 collective-permute-start.10
  78.5 2.6 %collective-permute-start.11 = (f32[128,256]{1,0:T(8,128)S(1)}, f32[128,256]{1,0:T(8,128)S(1)}, u32[]{:S(2)}, u32[]{:S(2)}) collective-permute-start(f32[128,256]{1,0:T(8,128)S(1)} %get-tuple-element.49), channel_id=1, source_target_pairs={{0,3},{1,2},{2,1},{3,0},{4,7},{5,6},{6,5},{7,4},{8,11},{9,10},{10,... | collective-permute-start | bytes 393224 | tf_op jit(solution)/shard_map/ppermute | solution.py:474
  81.1 1.0 %depth_inverse.2 = (f32[128,256]{1,0:T(8,128)S(1)}, f32[128,256]{1,0:T(8,128)S(1)}, f32[128,256]{1,0:T(8,128)S(1)}, f32[128,256]{1,0:T(8,128)S(1)}) custom-call(s32[1]{0:T(128)} %bitcast.me_ref, f32[2048,128]{1,0:T(8,128)S(1)} %bitcast.10, bf16[4,512,512]{2,1,0:T(8,128)(2,1)S(1)} %get-tuple-element.35.high_ref, bf16[4,512,512]{2,1,0:T(8,128)(2,1)S(1)} %copy-done.1), custom_call_target="tpu_custom_call" | custom-call | flops 1200000000 | bytes 4000000 | tf_op jit(solution)/shard_map/depth_inverse/pallas_call | solution.py:223
  82.1 0.2 collective-permute-start.8
  82.4 0.7 collective-permute-start.7
  83.1 0.0 collective-permute-done.9.refs_1_
  83.1 2.8 %collective-permute-start.6 = (f32[128,256]{1,0:T(8,128)S(1)}, f32[128,256]{1,0:T(8,128)S(1)}, u32[]{:S(2)}, u32[]{:S(2)}) collective-permute-start(f32[128,256]{1,0:T(8,128)S(1)} %get-tuple-element.42), channel_id=1, source_target_pairs={{0,3},{1,2},{2,1},{3,0},{4,7},{5,6},{6,5},{7,4},{8,11},{9,10},{10,... | collective-permute-start | bytes 393224 | tf_op jit(solution)/shard_map/ppermute | solution.py:474
  85.9 0.0 copy-done.2
  85.9 0.0 copy-done.3
  85.9 0.0 copy-done.5
  85.9 0.0 copy-done.6
  85.9 0.0 copy-done.7
  85.9 1.2 %friction_start.1 = (f32[512,512]{1,0:T(8,128)S(1)}, f32[512,512]{1,0:T(8,128)S(1)}, f32[512,512]{1,0:T(8,128)S(1)}) custom-call(f32[512,512]{1,0:T(8,128)S(1)} %copy-done.5, f32[512,512]{1,0:T(8,128)S(1)} %copy-done.6, f32[512,512]{1,0:T(8,128)S(1)} %copy-done.7, f32[512,512]{1,0:T(8,128)S(1)} %copy-done.2, f32[512,512]{1,0:T(8,128)S(1)} %copy-done.3), custom_call_target="tpu_custom_call" | custom-call | flops 20000000 | bytes 8000000 | tf_op jit(solution)/shard_map/friction_start/pallas_call | solution.py:413
  87.1 0.0 collective-permute-done.10.refs_2_
  87.1 0.8 collective-permute-done.11.refs_3_
  87.9 0.0 copy-done.4
  87.9 2.0 %friction_finish.4 = (f32[512,512]{1,0:T(8,128)}, f32[512,512]{1,0:T(8,128)}) custom-call(s32[1]{0:T(128)} %bitcast.me_ref, f32[512,512]{1,0:T(8,128)S(1)} %get-tuple-element.31.scale_ref, f32[512,512]{1,0:T(8,128)S(1)} %get-tuple-element.32.rest_ref, f32[512,512]{1,0:T(8,128)S(1)} %get-tuple-element.33.gain_ref, f32[512,512]{1,0:T(8,128)S(1)} %copy-done.2, ...), custom_call_target="tpu_custom_call" | custom-call | flops 20000000 | bytes 5000000 | tf_op jit(solution)/shard_map/friction_finish/pallas_call | solution.py:456
  89.9 0.0 collective-permute-done.8.refs_1_
  89.9 1.4 %friction_finish.5 = (f32[512,512]{1,0:T(8,128)}, f32[512,512]{1,0:T(8,128)}) custom-call(s32[1]{0:T(128)} %bitcast.me_ref, f32[512,512]{1,0:T(8,128)S(1)} %get-tuple-element.31.scale_ref, f32[512,512]{1,0:T(8,128)S(1)} %get-tuple-element.32.rest_ref, f32[512,512]{1,0:T(8,128)S(1)} %get-tuple-element.33.gain_ref, ...), custom_call_target="tpu_custom_call", output_to_operand_aliasing={{0}: (9, {}), {1}: (10, {})} | custom-call | flops 20000000 | bytes 5000000 | tf_op jit(solution)/shard_map/friction_finish/pallas_call | solution.py:456
  91.3 0.0 collective-permute-done.7.refs_0_
  91.4 1.1 %friction_finish.6 = (f32[512,512]{1,0:T(8,128)}, f32[512,512]{1,0:T(8,128)}) custom-call(s32[1]{0:T(128)} %bitcast.me_ref, f32[512,512]{1,0:T(8,128)S(1)} %get-tuple-element.31.scale_ref, f32[512,512]{1,0:T(8,128)S(1)} %get-tuple-element.32.rest_ref, f32[512,512]{1,0:T(8,128)S(1)} %get-tuple-element.33.gain_ref, ...), custom_call_target="tpu_custom_call", output_to_operand_aliasing={{0}: (8, {}), {1}: (9, {})} | custom-call | flops 20000000 | bytes 5000000 | tf_op jit(solution)/shard_map/friction_finish/pallas_call | solution.py:456
  92.4 0.6 collective-permute-done.6.refs_0_
  93.0 1.1 %friction_finish.7 = (f32[512,512]{1,0:T(8,128)}, f32[512,512]{1,0:T(8,128)}) custom-call(s32[1]{0:T(128)} %bitcast.me_ref, f32[512,512]{1,0:T(8,128)S(1)} %get-tuple-element.31.scale_ref, f32[512,512]{1,0:T(8,128)S(1)} %get-tuple-element.32.rest_ref, f32[512,512]{1,0:T(8,128)S(1)} %get-tuple-element.33.gain_ref, ...), custom_call_target="tpu_custom_call", output_to_operand_aliasing={{0}: (8, {}), {1}: (9, {})} | custom-call | flops 20000000 | bytes 5000000 | tf_op jit(solution)/shard_map/friction_finish/pallas_call | solution.py:456
  (2 shorter events, 0.0 us)
Async XLA Ops:
  1.7 13.7 %collective-permute-start.4 = (f32[128,384]{1,0:T(8,128)S(1)}, f32[128,384]{1,0:T(8,128)S(1)}, u32[]{:S(2)}, u32[]{:S(2)}) collective-permute-start(f32[128,384]{1,0:T(8,128)S(1)} %get-tuple-element.37), channel_id=1, source_target_pairs={{0,2},{1,3},{2,0},{3,1},{4,6},{5,7},{6,4},{7,5},{8,10},{9,11},{10,... | collective-permute-start | bytes 589832 | tf_op jit(solution)/shard_map/ppermute | solution.py:474
  6.2 10.0 %collective-permute-start.5 = (f32[128,384]{1,0:T(8,128)S(1)}, f32[128,384]{1,0:T(8,128)S(1)}, u32[]{:S(2)}, u32[]{:S(2)}) collective-permute-start(f32[128,384]{1,0:T(8,128)S(1)} %get-tuple-element.38), channel_id=1, source_target_pairs={{0,3},{1,2},{2,1},{3,0},{4,7},{5,6},{6,5},{7,4},{8,11},{9,10},{10,... | collective-permute-start | bytes 589832 | tf_op jit(solution)/shard_map/ppermute | solution.py:474
  7.9 8.3 %collective-permute-start.3 = (f32[128,384]{1,0:T(8,128)S(1)}, f32[128,384]{1,0:T(8,128)S(1)}, u32[]{:S(2)}, u32[]{:S(2)}) collective-permute-start(f32[128,384]{1,0:T(8,128)S(1)} %get-tuple-element.59), channel_id=1, source_target_pairs={{0,1},{1,0},{2,3},{3,2},{4,5},{5,4},{6,7},{7,6},{8,9},{9,8},{10,11... | collective-permute-start | bytes 589832 | tf_op jit(solution)/shard_map/ppermute | solution.py:474
  9.3 8.5 %collective-permute-start.2 = (f32[128,128]{1,0:T(8,128)S(1)}, f32[128,128]{1,0:T(8,128)S(1)}, u32[]{:S(2)}, u32[]{:S(2)}) collective-permute-start(f32[128,128]{1,0:T(8,128)S(1)} %get-tuple-element.61), channel_id=1, source_target_pairs={{0,3},{1,2},{2,1},{3,0},{4,7},{5,6},{6,5},{7,4},{8,11},{9,10},{10,... | collective-permute-start | bytes 196616 | tf_op jit(solution)/shard_map/ppermute | solution.py:474
  12.6 5.8 %collective-permute-start.1 = (f32[128,128]{1,0:T(8,128)S(1)}, f32[128,128]{1,0:T(8,128)S(1)}, u32[]{:S(2)}, u32[]{:S(2)}) collective-permute-start(f32[128,128]{1,0:T(8,128)S(1)} %get-tuple-element.62), channel_id=1, source_target_pairs={{0,2},{1,3},{2,0},{3,1},{4,6},{5,7},{6,4},{7,5},{8,10},{9,11},{10,... | collective-permute-start | bytes 196616 | tf_op jit(solution)/shard_map/ppermute | solution.py:474
  12.6 1.0 %copy-start.8 = (f32[2,128,512]{2,1,0:T(8,128)S(1)}, f32[2,128,512]{2,1,0:T(8,128)}, u32[]{:S(2)}) copy-start(f32[2,128,512]{2,1,0:T(8,128)} %constant.26.clone.coarse_ref) | copy-start | bytes 1572868
  13.6 0.8 copy-start.9
  15.4 3.0 %copy-start = (bf16[4,512,512]{2,1,0:T(8,128)(2,1)}, bf16[4,512,512]{2,1,0:T(8,128)(2,1)S(1)}, u32[]{:S(2)}) copy-start(bf16[4,512,512]{2,1,0:T(8,128)(2,1)S(1)} %get-tuple-element.36.low_ref) | copy-start | bytes 6291460
  15.4 2.9 %collective-permute-start = (f32[128,128]{1,0:T(8,128)S(1)}, f32[128,128]{1,0:T(8,128)S(1)}, u32[]{:S(2)}, u32[]{:S(2)}) collective-permute-start(f32[128,128]{1,0:T(8,128)S(1)} %get-tuple-element.63), channel_id=1, source_target_pairs={{0,1},{1,0},{2,3},{3,2},{4,5},{5,4},{6,7},{7,6},{8,9},{9,8},{10,11... | collective-permute-start | bytes 196616 | tf_op jit(solution)/shard_map/ppermute | solution.py:474
  20.0 29.3 %all-to-all-start = ((f32[128,16,128]{2,1,0:T(8,128)}), f32[128,16,128]{2,1,0:T(8,128)S(1)}, u32[]{:S(2)}, u32[]{:S(2)}) async-start(f32[128,16,128]{2,1,0:T(8,128)} %depth_forward.3), calls=%async_computation | async-start | bytes 2097152 | tf_op jit(solution)/shard_map/all_to_all | solution.py:501
  30.1 19.2 %copy-start.10 = (f32[4,128,128]{2,1,0:T(8,128)S(1)}, f32[4,128,128]{2,1,0:T(8,128)}, u32[]{:S(2)}) copy-start(f32[4,128,128]{2,1,0:T(8,128)} %constant.29.clone.twist_ref) | copy-start | bytes 786436
  30.2 19.2 %copy-start.11 = (bf16[4,128,128]{2,1,0:T(8,128)(2,1)S(1)}, bf16[4,128,128]{2,1,0:T(8,128)(2,1)}, u32[]{:S(2)}) copy-start(bf16[4,128,128]{2,1,0:T(8,128)(2,1)} %constant.28.clone.wave_ref) | copy-start | bytes 393220
  49.3 26.2 %copy-start.1 = (bf16[4,512,512]{2,1,0:T(8,128)(2,1)S(1)}, bf16[4,512,512]{2,1,0:T(8,128)(2,1)}, u32[]{:S(2)}) copy-start(bf16[4,512,512]{2,1,0:T(8,128)(2,1)} %copy-done) | copy-start | bytes 6291460
  75.5 10.4 %copy-start.2 = (f32[512,512]{1,0:T(8,128)S(1)}, f32[512,512]{1,0:T(8,128)}, u32[]{:S(2)}) copy-start(f32[512,512]{1,0:T(8,128)} %strength_ref.9) | copy-start | bytes 3145732
  75.5 10.4 %copy-start.3 = (f32[512,512]{1,0:T(8,128)S(1)}, f32[512,512]{1,0:T(8,128)}, u32[]{:S(2)}) copy-start(f32[512,512]{1,0:T(8,128)} %stress_ref.9) | copy-start | bytes 3145732
  75.5 10.4 %copy-start.5 = (f32[512,512]{1,0:T(8,128)S(1)}, f32[512,512]{1,0:T(8,128)}, u32[]{:S(2)}) copy-start(f32[512,512]{1,0:T(8,128)} %rate_ref.1) | copy-start | bytes 3145732
  75.5 10.4 %copy-start.6 = (f32[512,512]{1,0:T(8,128)S(1)}, f32[512,512]{1,0:T(8,128)}, u32[]{:S(2)}) copy-start(f32[512,512]{1,0:T(8,128)} %state_ref.1) | copy-start | bytes 3145732
  75.5 10.4 %copy-start.7 = (f32[512,512]{1,0:T(8,128)S(1)}, f32[512,512]{1,0:T(8,128)}, u32[]{:S(2)}) copy-start(f32[512,512]{1,0:T(8,128)} %weak_ref.1) | copy-start | bytes 3145732
  76.6 6.5 %collective-permute-start.9 = (f32[128,256]{1,0:T(8,128)S(1)}, f32[128,256]{1,0:T(8,128)S(1)}, u32[]{:S(2)}, u32[]{:S(2)}) collective-permute-start(f32[128,256]{1,0:T(8,128)S(1)} %get-tuple-element.47), channel_id=1, source_target_pairs={{0,1},{1,0},{2,3},{3,2},{4,5},{5,4},{6,7},{7,6},{8,9},{9,8},{10,11... | collective-permute-start | bytes 393224 | tf_op jit(solution)/shard_map/ppermute | solution.py:474
  77.9 9.2 %collective-permute-start.10 = (f32[128,256]{1,0:T(8,128)S(1)}, f32[128,256]{1,0:T(8,128)S(1)}, u32[]{:S(2)}, u32[]{:S(2)}) collective-permute-start(f32[128,256]{1,0:T(8,128)S(1)} %get-tuple-element.48), channel_id=1, source_target_pairs={{0,2},{1,3},{2,0},{3,1},{4,6},{5,7},{6,4},{7,5},{8,10},{9,11},{10,... | collective-permute-start | bytes 393224 | tf_op jit(solution)/shard_map/ppermute | solution.py:474
  78.5 9.4 %copy-start.4 = (f32[512,512]{1,0:T(8,128)S(1)}, f32[512,512]{1,0:T(8,128)}, u32[]{:S(2)}) copy-start(f32[512,512]{1,0:T(8,128)} %slip_ref.7) | copy-start | bytes 3145732
  78.5 9.4 %collective-permute-start.11 = (f32[128,256]{1,0:T(8,128)S(1)}, f32[128,256]{1,0:T(8,128)S(1)}, u32[]{:S(2)}, u32[]{:S(2)}) collective-permute-start(f32[128,256]{1,0:T(8,128)S(1)} %get-tuple-element.49), channel_id=1, source_target_pairs={{0,3},{1,2},{2,1},{3,0},{4,7},{5,6},{6,5},{7,4},{8,11},{9,10},{10,... | collective-permute-start | bytes 393224 | tf_op jit(solution)/shard_map/ppermute | solution.py:474
  82.1 7.8 %collective-permute-start.8 = (f32[128,256]{1,0:T(8,128)S(1)}, f32[128,256]{1,0:T(8,128)S(1)}, u32[]{:S(2)}, u32[]{:S(2)}) collective-permute-start(f32[128,256]{1,0:T(8,128)S(1)} %get-tuple-element.45), channel_id=1, source_target_pairs={{0,1},{1,0},{2,3},{3,2},{4,5},{5,4},{6,7},{7,6},{8,9},{9,8},{10,11... | collective-permute-start | bytes 393224 | tf_op jit(solution)/shard_map/ppermute | solution.py:474
  82.4 9.0 %collective-permute-start.7 = (f32[128,256]{1,0:T(8,128)S(1)}, f32[128,256]{1,0:T(8,128)S(1)}, u32[]{:S(2)}, u32[]{:S(2)}) collective-permute-start(f32[128,256]{1,0:T(8,128)S(1)} %get-tuple-element.43), channel_id=1, source_target_pairs={{0,2},{1,3},{2,0},{3,1},{4,6},{5,7},{6,4},{7,5},{8,10},{9,11},{10,... | collective-permute-start | bytes 393224 | tf_op jit(solution)/shard_map/ppermute | solution.py:474
  83.1 10.0 %collective-permute-start.6 = (f32[128,256]{1,0:T(8,128)S(1)}, f32[128,256]{1,0:T(8,128)S(1)}, u32[]{:S(2)}, u32[]{:S(2)}) collective-permute-start(f32[128,256]{1,0:T(8,128)S(1)} %get-tuple-element.42), channel_id=1, source_target_pairs={{0,3},{1,2},{2,1},{3,0},{4,7},{5,6},{6,5},{7,4},{8,11},{9,10},{10,... | collective-permute-start | bytes 393224 | tf_op jit(solution)/shard_map/ppermute | solution.py:474

commit v8 on v7

--- a/solution.py
+++ b/solution.py
@@ -190,24 +190,31 @@
             value = jnp.where(first, 0.5 * value, value)
         return split(value.T)
 
-    def turn(cls, *lines):
-        left = [
+    def stack(*lines):
+        return [
             jnp.concatenate([jnp.concatenate(line, axis=1) for line in part], axis=0)
             for part in zip(*[[(a, b) for a, b in zip(*line)] for line in lines])
         ]
-        return dot3(left, (high_ref[cls, :, cols], low_ref[cls, :, cols]), NN)
+
+    def turn(classes, lefts):
+        left = [jnp.concatenate(part, axis=1) for part in zip(*lefts)]
+        table = [
+            jnp.concatenate([ref[cls, :, cols] for cls in classes], axis=0)
+            for ref in (high_ref, low_ref)
+        ]
+        return dot3(left, table, NN)
 
     def minus(parts):
         return [-part for part in parts]
 
     real, imag = get(0, 0), get(0, 1)
-    zero = turn(0, (real, minus(imag)))
+    zero = turn((0,), [stack((real, minus(imag)))])
     real, imag = get(2, 0), get(2, 1)
-    two = tau * turn(2, (real, minus(imag)))
+    two = tau * turn((2,), [stack((real, minus(imag)))])
     real, imag = get(1, 0), get(1, 1)
-    odd = turn(1, (real, minus(imag)), (minus(imag), minus(real)))
+    odd = stack((real, minus(imag)), (minus(imag), minus(real)))
     real, imag = get(3, 0), get(3, 1)
-    odd = sigma * (odd + turn(3, (real, minus(imag)), (imag, real)))
+    odd = sigma * turn((1, 3), [odd, stack((real, minus(imag)), (imag, real))])
     low, high = odd[:rows], odd[rows:]
     base, turned = zero + two, jnp.where(swap, high, low)
     own_ref[...] = base + turned

time: 94.8 us -> 94.8 us (level)
  no operation moved by 1% of the time
where the time goes in v8:
time: 94.8 us; the launch traced here: 94.3 us
  starting transfers between devices  27.8 us (29%)
  Pallas kernels  24.1 us (25%)
  blocking collectives  23.3 us (25%)
  waiting for transfers between devices  13.1 us (14%)
  local copies, waits for them, and re-layouts  4.9 us (5%)
  between operations  1.02 us (1%)
    all_to_all x1, blocking collectives, body(): lax.all_to_all(waves.reshape(devices, 16, edge), ALL, 0, 0)  23.3 us
    ppermute x12, starting transfers between devices, exchange(): lax.ppermute(part, 'depth', [(place, place ^ k) for place in range(size)])  17.7 us
    all_to_all x1, waiting for transfers between devices, body(): pencil = lax.all_to_all(waves, ALL, 0, 0)  10.9 us
    all_to_all x1, starting transfers between devices, body(): pencil = lax.all_to_all(waves, ALL, 0, 0)  10.1 us
    pallas_call x1, Pallas kernels, past_sum(): pl.pallas_call(past_kernel, grid=(length // block,), out_shape=(pltpu.HBM...  8.27 us
    pallas_call x4, Pallas kernels, friction_finish(): pl.pallas_call(functools.partial(friction_kernel, slots, column), in_spec...  5.56 us
    pallas_call x2, Pallas kernels, depth_forward(): pl.pallas_call(functools.partial(depth_forward_kernel, first, column), ou...  3.17 us
    dynamic_slice x3, local copies, waits for them, and re-layouts, body(): lax.dynamic_slice(source, ((place ^ k) * edge, part[0]), (edge, part[1]))  3.06 us
  transfers between devices with their start and end apart: 13, of which 5 were waited for; matrix products, arithmetic and copies ran while one was open for 2% of the time, Pallas kernels for 19%

profile of v8, /device:TPU:1, one launch (start us, length us, event | category | flops | bytes accessed | tf_op | source)
XLA Modules:
  0.0 94.3 jit_solution(4946731873301558434)
XLA Ops:
  0.6 1.1 %constant_dynamic-slice_fusion.6 = (f32[128,384]{1,0:T(8,128)S(1)}, f32[128,384]{1,0:T(8,128)S(1)}) fusion(f32[512,512]{1,0:T(8,128)} %slip_ref.7, s32[]{:T(128)S(6)} %select_n.17, s32[]{:T(128)S(6)} %select_n.16), kind=kLoop, calls=%fused_computation.6 | loop fusion | bytes 786440 | tf_op jit(solution)/shard_map/dynamic_slice | solution.py:494
  1.7 4.5 %collective-permute-start.4 = (f32[128,384]{1,0:T(8,128)S(1)}, f32[128,384]{1,0:T(8,128)S(1)}, u32[]{:S(2)}, u32[]{:S(2)}) collective-permute-start(f32[128,384]{1,0:T(8,128)S(1)} %get-tuple-element.37), channel_id=1, source_target_pairs={{0,2},{1,3},{2,0},{3,1},{4,6},{5,7},{6,4},{7,5},{8,10},{9,11},{10,... | collective-permute-start | bytes 589832 | tf_op jit(solution)/shard_map/ppermute | solution.py:481
  6.2 0.7 collective-permute-start.5
  6.9 1.0 %constant_dynamic-slice_fusion.4 = (f32[128,384]{1,0:T(8,128)S(1)}, f32[128,384]{1,0:T(8,128)S(1)}) fusion(f32[512,512]{1,0:T(8,128)} %slip_ref.7, s32[]{:T(128)S(6)} %select_n.19, s32[]{:T(128)S(6)} %select_n.18), kind=kLoop, calls=%fused_computation.4 | loop fusion | bytes 786440 | tf_op jit(solution)/shard_map/dynamic_slice | solution.py:494
  7.9 0.4 collective-permute-start.3
  8.3 1.0 %constant_dynamic-slice_fusion = (f32[128,128]{1,0:T(8,128)S(1)}, f32[128,128]{1,0:T(8,128)S(1)}, f32[128,128]{1,0:T(8,128)S(1)}, f32[128,128]{1,0:T(8,128)S(1)}) fusion(f32[512,512]{1,0:T(8,128)} %slip_ref.7, s32[]{:T(128)S(6)} %select_n.17, s32[]{:T(128)S(6)} %select_n.16, s32[]{:T(128)S(6)} %select_n.19, s32[]{:T(128)S(6)} %select_n.18), kind=kLoop, calls=%fused_computation | loop fusion | bytes 524304 | tf_op jit(solution)/shard_map/dynamic_slice | solution.py:494
  9.3 3.3 %collective-permute-start.2 = (f32[128,128]{1,0:T(8,128)S(1)}, f32[128,128]{1,0:T(8,128)S(1)}, u32[]{:S(2)}, u32[]{:S(2)}) collective-permute-start(f32[128,128]{1,0:T(8,128)S(1)} %get-tuple-element.61), channel_id=1, source_target_pairs={{0,3},{1,2},{2,1},{3,0},{4,7},{5,6},{6,5},{7,4},{8,11},{9,10},{10,... | collective-permute-start | bytes 196616 | tf_op jit(solution)/shard_map/ppermute | solution.py:481
  12.6 0.0 collective-permute-start.1
  12.6 0.0 copy-start.8
  12.6 1.0 %copy-done.8 = f32[2,128,512]{2,1,0:T(8,128)S(1)} copy-done((f32[2,128,512]{2,1,0:T(8,128)S(1)}, f32[2,128,512]{2,1,0:T(8,128)}, u32[]{:S(2)}) %copy-start.8) | copy-done | bytes 524312
  13.6 0.0 copy-start.9
  13.6 0.8 copy-done.9
  14.4 1.0 %depth_tables.1 = (bf16[4,512,512]{2,1,0:T(8,128)(2,1)S(1)}, bf16[4,512,512]{2,1,0:T(8,128)(2,1)S(1)}) custom-call(f32[2,128,512]{2,1,0:T(8,128)S(1)} %copy-done.8, f32[2,8,512]{2,1,0:T(8,128)S(1)} %copy-done.9), custom_call_target="tpu_custom_call" | custom-call | flops 10000000 | bytes 5000000 | tf_op jit(solution)/shard_map/depth_tables/pallas_call | solution.py:94
  15.4 0.0 copy-start
  15.4 0.0 collective-permute-done.4.two_ref
  15.4 0.6 collective-permute-start
  16.0 0.2 collective-permute-done.5.three_ref
  16.2 0.0 collective-permute-done.3.one_ref
  16.2 1.5 %depth_forward.2.refs_0_ = f32[16,128,128]{2,1,0:T(8,128)S(1)} custom-call(s32[1]{0:T(128)} %bitcast.me_ref, f32[128,384]{1,0:T(8,128)S(1)} %get-tuple-element.60.own_ref, f32[128,384]{1,0:T(8,128)S(1)} %collective-permute-done.3.one_ref, f32[128,384]{1,0:T(8,128)S(1)} %collective-permute-done.4.two_ref, f32[128,384]{1,0:T(8,128)S(1)} %collective-permute-done.5.three_ref, ...), custom_call_target="tpu_custom_call" | custom-call | flops 1200000000 | bytes 4000000 | tf_op jit(solution)/shard_map/depth_forward/pallas_call | solution.py:162
  17.7 0.0 collective-permute-done.2.three_ref
  17.7 0.6 collective-permute-done.1.two_ref
  18.3 0.0 collective-permute-done.one_ref
  18.4 0.0 copy-done
  18.4 1.7 %depth_forward.3 = f32[128,16,128]{2,1,0:T(8,128)} custom-call(s32[1]{0:T(128)} %bitcast.me_ref, f32[128,128]{1,0:T(8,128)S(1)} %get-tuple-element.64.own_ref, f32[128,128]{1,0:T(8,128)S(1)} %collective-permute-done.one_ref, f32[128,128]{1,0:T(8,128)S(1)} %collective-permute-done.1.two_ref, f32[128,128]{1,0:T(8,128)S(1)} %collective-permute-done.2.three_ref, ...), custom_call_target="tpu_custom_call" | custom-call | flops 1200000000 | bytes 4000000 | tf_op jit(solution)/shard_map/depth_forward/pallas_call | solution.py:162
  20.0 10.1 %all-to-all-start = ((f32[128,16,128]{2,1,0:T(8,128)}), f32[128,16,128]{2,1,0:T(8,128)S(1)}, u32[]{:S(2)}, u32[]{:S(2)}) async-start(f32[128,16,128]{2,1,0:T(8,128)} %depth_forward.3), calls=%async_computation | async-start | bytes 2097152 | tf_op jit(solution)/shard_map/all_to_all | solution.py:508
  30.1 0.0 copy-start.10
  30.2 0.0 copy-start.11
  30.2 8.3 %past_sum.1 = (f32[8,128,128]{2,1,0:T(8,128)}, f32[2,8,128,128]{3,2,1,0:T(8,128)}) custom-call(f32[9,8,16384]{2,1,0:T(8,128)} %kernel_ref.1, f32[8,2,8,16384]{3,2,1,0:T(8,128)} %history_ref.1), custom_call_target="tpu_custom_call" | custom-call | flops 4200000 | bytes 14700000 | tf_op jit(solution)/shard_map/past_sum/pallas_call | solution.py:372
  38.4 10.9 %all-to-all-done = f32[128,16,128]{2,1,0:T(8,128)S(1)} async-done(((f32[128,16,128]{2,1,0:T(8,128)}), f32[128,16,128]{2,1,0:T(8,128)S(1)}, u32[]{:S(2)}, u32[]{:S(2)}) %all-to-all-start) | async-done | bytes 1048608 | tf_op jit(solution)/shard_map/all_to_all | solution.py:508
  49.3 0.0 copy-start.1
  49.3 0.0 copy-done.10
  49.3 0.0 copy-done.11
  49.3 2.9 %strike_both.1 = (f32[2,1024,128]{2,1,0:T(8,128)}, f32[2048,128]{1,0:T(8,128)S(1)}) custom-call(f32[2048,128]{1,0:T(8,128)S(1)} %bitcast.11, f32[8,128,128]{2,1,0:T(8,128)} %get-tuple-element.39.gain_hbm, f32[2,8,128,128]{3,2,1,0:T(8,128)} %get-tuple-element.40.past_hbm, bf16[4,128,128]{2,1,0:T(8,128)(2,1)S(1)} %copy-done.11, f32[4,128,128]{2,1,0:T(8,128)S(1)} %copy-done.10), custom_call_target="tpu_custom_call" | custom-call | flops 1600000000 | bytes 6000000 | tf_op jit(solution)/shard_map/strike_both/pallas_call | solution.py:337
  52.2 23.3 %all_to_all.10 = f32[128,16,128]{2,1,0:T(8,128)S(1)} all-to-all(f32[128,16,128]{2,1,0:T(8,128)S(1)} %bitcast.12), channel_id=1, replica_groups=mesh['strike'=32,'depth'=4] {'strike','depth'}, dimensions={0} | all-to-all | bytes 2097152 | tf_op jit(solution)/shard_map/all_to_all | solution.py:514
  75.5 0.0 copy-done.1
  75.5 0.0 copy-start.2
  75.5 0.0 copy-start.5
  75.5 0.0 copy-start.6
  75.5 0.0 copy-start.7
  75.5 1.0 %depth_inverse.3 = (f32[128,256]{1,0:T(8,128)S(1)}, f32[128,256]{1,0:T(8,128)S(1)}, f32[128,256]{1,0:T(8,128)S(1)}, f32[128,256]{1,0:T(8,128)S(1)}) custom-call(s32[1]{0:T(128)} %bitcast.me_ref, f32[2048,128]{1,0:T(8,128)S(1)} %bitcast.9, bf16[4,512,512]{2,1,0:T(8,128)(2,1)S(1)} %get-tuple-element.35.high_ref, bf16[4,512,512]{2,1,0:T(8,128)(2,1)S(1)} %copy-done.1), custom_call_target="tpu_custom_call" | custom-call | flops 1200000000 | bytes 4000000 | tf_op jit(solution)/shard_map/depth_inverse/pallas_call | solution.py:230
  76.6 1.3 %collective-permute-start.9 = (f32[128,256]{1,0:T(8,128)S(1)}, f32[128,256]{1,0:T(8,128)S(1)}, u32[]{:S(2)}, u32[]{:S(2)}) collective-permute-start(f32[128,256]{1,0:T(8,128)S(1)} %get-tuple-element.47), channel_id=1, source_target_pairs={{0,1},{1,0},{2,3},{3,2},{4,5},{5,4},{6,7},{7,6},{8,9},{9,8},{10,11... | collective-permute-start | bytes 393224 | tf_op jit(solution)/shard_map/ppermute | solution.py:481
  77.9 0.6 collective-permute-start.10
  78.5 2.6 %collective-permute-start.11 = (f32[128,256]{1,0:T(8,128)S(1)}, f32[128,256]{1,0:T(8,128)S(1)}, u32[]{:S(2)}, u32[]{:S(2)}) collective-permute-start(f32[128,256]{1,0:T(8,128)S(1)} %get-tuple-element.49), channel_id=1, source_target_pairs={{0,3},{1,2},{2,1},{3,0},{4,7},{5,6},{6,5},{7,4},{8,11},{9,10},{10,... | collective-permute-start | bytes 393224 | tf_op jit(solution)/shard_map/ppermute | solution.py:481
  81.1 1.0 %depth_inverse.2 = (f32[128,256]{1,0:T(8,128)S(1)}, f32[128,256]{1,0:T(8,128)S(1)}, f32[128,256]{1,0:T(8,128)S(1)}, f32[128,256]{1,0:T(8,128)S(1)}) custom-call(s32[1]{0:T(128)} %bitcast.me_ref, f32[2048,128]{1,0:T(8,128)S(1)} %bitcast.10, bf16[4,512,512]{2,1,0:T(8,128)(2,1)S(1)} %get-tuple-element.35.high_ref, bf16[4,512,512]{2,1,0:T(8,128)(2,1)S(1)} %copy-done.1), custom_call_target="tpu_custom_call" | custom-call | flops 1200000000 | bytes 4000000 | tf_op jit(solution)/shard_map/depth_inverse/pallas_call | solution.py:230
  82.1 0.2 collective-permute-start.8
  82.4 0.7 collective-permute-start.7
  83.1 0.0 collective-permute-done.9.refs_1_
  83.1 2.8 %collective-permute-start.6 = (f32[128,256]{1,0:T(8,128)S(1)}, f32[128,256]{1,0:T(8,128)S(1)}, u32[]{:S(2)}, u32[]{:S(2)}) collective-permute-start(f32[128,256]{1,0:T(8,128)S(1)} %get-tuple-element.42), channel_id=1, source_target_pairs={{0,3},{1,2},{2,1},{3,0},{4,7},{5,6},{6,5},{7,4},{8,11},{9,10},{10,... | collective-permute-start | bytes 393224 | tf_op jit(solution)/shard_map/ppermute | solution.py:481
  85.9 0.0 copy-done.2
  85.9 0.0 copy-done.3
  85.9 0.0 copy-done.5
  85.9 0.0 copy-done.6
  85.9 0.0 copy-done.7
  85.9 1.2 %friction_start.1 = (f32[512,512]{1,0:T(8,128)S(1)}, f32[512,512]{1,0:T(8,128)S(1)}, f32[512,512]{1,0:T(8,128)S(1)}) custom-call(f32[512,512]{1,0:T(8,128)S(1)} %copy-done.5, f32[512,512]{1,0:T(8,128)S(1)} %copy-done.6, f32[512,512]{1,0:T(8,128)S(1)} %copy-done.7, f32[512,512]{1,0:T(8,128)S(1)} %copy-done.2, f32[512,512]{1,0:T(8,128)S(1)} %copy-done.3), custom_call_target="tpu_custom_call" | custom-call | flops 20000000 | bytes 8000000 | tf_op jit(solution)/shard_map/friction_start/pallas_call | solution.py:420
  87.1 0.0 collective-permute-done.10.refs_2_
  87.1 0.8 collective-permute-done.11.refs_3_
  87.9 0.0 copy-done.4
  87.9 2.0 %friction_finish.4 = (f32[512,512]{1,0:T(8,128)}, f32[512,512]{1,0:T(8,128)}) custom-call(s32[1]{0:T(128)} %bitcast.me_ref, f32[512,512]{1,0:T(8,128)S(1)} %get-tuple-element.31.scale_ref, f32[512,512]{1,0:T(8,128)S(1)} %get-tuple-element.32.rest_ref, f32[512,512]{1,0:T(8,128)S(1)} %get-tuple-element.33.gain_ref, f32[512,512]{1,0:T(8,128)S(1)} %copy-done.2, ...), custom_call_target="tpu_custom_call" | custom-call | flops 20000000 | bytes 5000000 | tf_op jit(solution)/shard_map/friction_finish/pallas_call | solution.py:463
  89.9 0.0 collective-permute-done.8.refs_1_
  89.9 1.4 %friction_finish.5 = (f32[512,512]{1,0:T(8,128)}, f32[512,512]{1,0:T(8,128)}) custom-call(s32[1]{0:T(128)} %bitcast.me_ref, f32[512,512]{1,0:T(8,128)S(1)} %get-tuple-element.31.scale_ref, f32[512,512]{1,0:T(8,128)S(1)} %get-tuple-element.32.rest_ref, f32[512,512]{1,0:T(8,128)S(1)} %get-tuple-element.33.gain_ref, ...), custom_call_target="tpu_custom_call", output_to_operand_aliasing={{0}: (9, {}), {1}: (10, {})} | custom-call | flops 20000000 | bytes 5000000 | tf_op jit(solution)/shard_map/friction_finish/pallas_call | solution.py:463
  91.3 0.0 collective-permute-done.7.refs_0_
  91.4 1.1 %friction_finish.6 = (f32[512,512]{1,0:T(8,128)}, f32[512,512]{1,0:T(8,128)}) custom-call(s32[1]{0:T(128)} %bitcast.me_ref, f32[512,512]{1,0:T(8,128)S(1)} %get-tuple-element.31.scale_ref, f32[512,512]{1,0:T(8,128)S(1)} %get-tuple-element.32.rest_ref, f32[512,512]{1,0:T(8,128)S(1)} %get-tuple-element.33.gain_ref, ...), custom_call_target="tpu_custom_call", output_to_operand_aliasing={{0}: (8, {}), {1}: (9, {})} | custom-call | flops 20000000 | bytes 5000000 | tf_op jit(solution)/shard_map/friction_finish/pallas_call | solution.py:463
  92.4 0.6 collective-permute-done.6.refs_0_
  93.0 1.1 %friction_finish.7 = (f32[512,512]{1,0:T(8,128)}, f32[512,512]{1,0:T(8,128)}) custom-call(s32[1]{0:T(128)} %bitcast.me_ref, f32[512,512]{1,0:T(8,128)S(1)} %get-tuple-element.31.scale_ref, f32[512,512]{1,0:T(8,128)S(1)} %get-tuple-element.32.rest_ref, f32[512,512]{1,0:T(8,128)S(1)} %get-tuple-element.33.gain_ref, ...), custom_call_target="tpu_custom_call", output_to_operand_aliasing={{0}: (8, {}), {1}: (9, {})} | custom-call | flops 20000000 | bytes 5000000 | tf_op jit(solution)/shard_map/friction_finish/pallas_call | solution.py:463
  (2 shorter events, 0.0 us)
Async XLA Ops:
  1.7 13.7 %collective-permute-start.4 = (f32[128,384]{1,0:T(8,128)S(1)}, f32[128,384]{1,0:T(8,128)S(1)}, u32[]{:S(2)}, u32[]{:S(2)}) collective-permute-start(f32[128,384]{1,0:T(8,128)S(1)} %get-tuple-element.37), channel_id=1, source_target_pairs={{0,2},{1,3},{2,0},{3,1},{4,6},{5,7},{6,4},{7,5},{8,10},{9,11},{10,... | collective-permute-start | bytes 589832 | tf_op jit(solution)/shard_map/ppermute | solution.py:481
  6.2 10.0 %collective-permute-start.5 = (f32[128,384]{1,0:T(8,128)S(1)}, f32[128,384]{1,0:T(8,128)S(1)}, u32[]{:S(2)}, u32[]{:S(2)}) collective-permute-start(f32[128,384]{1,0:T(8,128)S(1)} %get-tuple-element.38), channel_id=1, source_target_pairs={{0,3},{1,2},{2,1},{3,0},{4,7},{5,6},{6,5},{7,4},{8,11},{9,10},{10,... | collective-permute-start | bytes 589832 | tf_op jit(solution)/shard_map/ppermute | solution.py:481
  7.9 8.3 %collective-permute-start.3 = (f32[128,384]{1,0:T(8,128)S(1)}, f32[128,384]{1,0:T(8,128)S(1)}, u32[]{:S(2)}, u32[]{:S(2)}) collective-permute-start(f32[128,384]{1,0:T(8,128)S(1)} %get-tuple-element.59), channel_id=1, source_target_pairs={{0,1},{1,0},{2,3},{3,2},{4,5},{5,4},{6,7},{7,6},{8,9},{9,8},{10,11... | collective-permute-start | bytes 589832 | tf_op jit(solution)/shard_map/ppermute | solution.py:481
  9.3 8.5 %collective-permute-start.2 = (f32[128,128]{1,0:T(8,128)S(1)}, f32[128,128]{1,0:T(8,128)S(1)}, u32[]{:S(2)}, u32[]{:S(2)}) collective-permute-start(f32[128,128]{1,0:T(8,128)S(1)} %get-tuple-element.61), channel_id=1, source_target_pairs={{0,3},{1,2},{2,1},{3,0},{4,7},{5,6},{6,5},{7,4},{8,11},{9,10},{10,... | collective-permute-start | bytes 196616 | tf_op jit(solution)/shard_map/ppermute | solution.py:481
  12.6 5.8 %collective-permute-start.1 = (f32[128,128]{1,0:T(8,128)S(1)}, f32[128,128]{1,0:T(8,128)S(1)}, u32[]{:S(2)}, u32[]{:S(2)}) collective-permute-start(f32[128,128]{1,0:T(8,128)S(1)} %get-tuple-element.62), channel_id=1, source_target_pairs={{0,2},{1,3},{2,0},{3,1},{4,6},{5,7},{6,4},{7,5},{8,10},{9,11},{10,... | collective-permute-start | bytes 196616 | tf_op jit(solution)/shard_map/ppermute | solution.py:481
  12.6 1.0 %copy-start.8 = (f32[2,128,512]{2,1,0:T(8,128)S(1)}, f32[2,128,512]{2,1,0:T(8,128)}, u32[]{:S(2)}) copy-start(f32[2,128,512]{2,1,0:T(8,128)} %constant.26.clone.coarse_ref) | copy-start | bytes 1572868
  13.6 0.8 copy-start.9
  15.4 3.0 %copy-start = (bf16[4,512,512]{2,1,0:T(8,128)(2,1)}, bf16[4,512,512]{2,1,0:T(8,128)(2,1)S(1)}, u32[]{:S(2)}) copy-start(bf16[4,512,512]{2,1,0:T(8,128)(2,1)S(1)} %get-tuple-element.36.low_ref) | copy-start | bytes 6291460
  15.4 2.9 %collective-permute-start = (f32[128,128]{1,0:T(8,128)S(1)}, f32[128,128]{1,0:T(8,128)S(1)}, u32[]{:S(2)}, u32[]{:S(2)}) collective-permute-start(f32[128,128]{1,0:T(8,128)S(1)} %get-tuple-element.63), channel_id=1, source_target_pairs={{0,1},{1,0},{2,3},{3,2},{4,5},{5,4},{6,7},{7,6},{8,9},{9,8},{10,11... | collective-permute-start | bytes 196616 | tf_op jit(solution)/shard_map/ppermute | solution.py:481
  20.0 29.3 %all-to-all-start = ((f32[128,16,128]{2,1,0:T(8,128)}), f32[128,16,128]{2,1,0:T(8,128)S(1)}, u32[]{:S(2)}, u32[]{:S(2)}) async-start(f32[128,16,128]{2,1,0:T(8,128)} %depth_forward.3), calls=%async_computation | async-start | bytes 2097152 | tf_op jit(solution)/shard_map/all_to_all | solution.py:508
  30.1 19.2 %copy-start.10 = (f32[4,128,128]{2,1,0:T(8,128)S(1)}, f32[4,128,128]{2,1,0:T(8,128)}, u32[]{:S(2)}) copy-start(f32[4,128,128]{2,1,0:T(8,128)} %constant.29.clone.twist_ref) | copy-start | bytes 786436
  30.2 19.2 %copy-start.11 = (bf16[4,128,128]{2,1,0:T(8,128)(2,1)S(1)}, bf16[4,128,128]{2,1,0:T(8,128)(2,1)}, u32[]{:S(2)}) copy-start(bf16[4,128,128]{2,1,0:T(8,128)(2,1)} %constant.28.clone.wave_ref) | copy-start | bytes 393220
  49.3 26.2 %copy-start.1 = (bf16[4,512,512]{2,1,0:T(8,128)(2,1)S(1)}, bf16[4,512,512]{2,1,0:T(8,128)(2,1)}, u32[]{:S(2)}) copy-start(bf16[4,512,512]{2,1,0:T(8,128)(2,1)} %copy-done) | copy-start | bytes 6291460
  75.5 10.4 %copy-start.2 = (f32[512,512]{1,0:T(8,128)S(1)}, f32[512,512]{1,0:T(8,128)}, u32[]{:S(2)}) copy-start(f32[512,512]{1,0:T(8,128)} %strength_ref.9) | copy-start | bytes 3145732
  75.5 10.4 %copy-start.3 = (f32[512,512]{1,0:T(8,128)S(1)}, f32[512,512]{1,0:T(8,128)}, u32[]{:S(2)}) copy-start(f32[512,512]{1,0:T(8,128)} %stress_ref.9) | copy-start | bytes 3145732
  75.5 10.4 %copy-start.5 = (f32[512,512]{1,0:T(8,128)S(1)}, f32[512,512]{1,0:T(8,128)}, u32[]{:S(2)}) copy-start(f32[512,512]{1,0:T(8,128)} %rate_ref.1) | copy-start | bytes 3145732
  75.5 10.4 %copy-start.6 = (f32[512,512]{1,0:T(8,128)S(1)}, f32[512,512]{1,0:T(8,128)}, u32[]{:S(2)}) copy-start(f32[512,512]{1,0:T(8,128)} %state_ref.1) | copy-start | bytes 3145732
  75.5 10.4 %copy-start.7 = (f32[512,512]{1,0:T(8,128)S(1)}, f32[512,512]{1,0:T(8,128)}, u32[]{:S(2)}) copy-start(f32[512,512]{1,0:T(8,128)} %weak_ref.1) | copy-start | bytes 3145732
  76.6 6.5 %collective-permute-start.9 = (f32[128,256]{1,0:T(8,128)S(1)}, f32[128,256]{1,0:T(8,128)S(1)}, u32[]{:S(2)}, u32[]{:S(2)}) collective-permute-start(f32[128,256]{1,0:T(8,128)S(1)} %get-tuple-element.47), channel_id=1, source_target_pairs={{0,1},{1,0},{2,3},{3,2},{4,5},{5,4},{6,7},{7,6},{8,9},{9,8},{10,11... | collective-permute-start | bytes 393224 | tf_op jit(solution)/shard_map/ppermute | solution.py:481
  77.9 9.2 %collective-permute-start.10 = (f32[128,256]{1,0:T(8,128)S(1)}, f32[128,256]{1,0:T(8,128)S(1)}, u32[]{:S(2)}, u32[]{:S(2)}) collective-permute-start(f32[128,256]{1,0:T(8,128)S(1)} %get-tuple-element.48), channel_id=1, source_target_pairs={{0,2},{1,3},{2,0},{3,1},{4,6},{5,7},{6,4},{7,5},{8,10},{9,11},{10,... | collective-permute-start | bytes 393224 | tf_op jit(solution)/shard_map/ppermute | solution.py:481
  78.5 9.4 %copy-start.4 = (f32[512,512]{1,0:T(8,128)S(1)}, f32[512,512]{1,0:T(8,128)}, u32[]{:S(2)}) copy-start(f32[512,512]{1,0:T(8,128)} %slip_ref.7) | copy-start | bytes 3145732
  78.5 9.4 %collective-permute-start.11 = (f32[128,256]{1,0:T(8,128)S(1)}, f32[128,256]{1,0:T(8,128)S(1)}, u32[]{:S(2)}, u32[]{:S(2)}) collective-permute-start(f32[128,256]{1,0:T(8,128)S(1)} %get-tuple-element.49), channel_id=1, source_target_pairs={{0,3},{1,2},{2,1},{3,0},{4,7},{5,6},{6,5},{7,4},{8,11},{9,10},{10,... | collective-permute-start | bytes 393224 | tf_op jit(solution)/shard_map/ppermute | solution.py:481
  82.1 7.8 %collective-permute-start.8 = (f32[128,256]{1,0:T(8,128)S(1)}, f32[128,256]{1,0:T(8,128)S(1)}, u32[]{:S(2)}, u32[]{:S(2)}) collective-permute-start(f32[128,256]{1,0:T(8,128)S(1)} %get-tuple-element.45), channel_id=1, source_target_pairs={{0,1},{1,0},{2,3},{3,2},{4,5},{5,4},{6,7},{7,6},{8,9},{9,8},{10,11... | collective-permute-start | bytes 393224 | tf_op jit(solution)/shard_map/ppermute | solution.py:481
  82.4 9.0 %collective-permute-start.7 = (f32[128,256]{1,0:T(8,128)S(1)}, f32[128,256]{1,0:T(8,128)S(1)}, u32[]{:S(2)}, u32[]{:S(2)}) collective-permute-start(f32[128,256]{1,0:T(8,128)S(1)} %get-tuple-element.43), channel_id=1, source_target_pairs={{0,2},{1,3},{2,0},{3,1},{4,6},{5,7},{6,4},{7,5},{8,10},{9,11},{10,... | collective-permute-start | bytes 393224 | tf_op jit(solution)/shard_map/ppermute | solution.py:481
  83.1 9.9 %collective-permute-start.6 = (f32[128,256]{1,0:T(8,128)S(1)}, f32[128,256]{1,0:T(8,128)S(1)}, u32[]{:S(2)}, u32[]{:S(2)}) collective-permute-start(f32[128,256]{1,0:T(8,128)S(1)} %get-tuple-element.42), channel_id=1, source_target_pairs={{0,3},{1,2},{2,1},{3,0},{4,7},{5,6},{6,5},{7,4},{8,11},{9,10},{10,... | collective-permute-start | bytes 393224 | tf_op jit(solution)/shard_map/ppermute | solution.py:481
